TPU v7x, 32 devices: a whole 2x2x4 slice. The times are simulated.
32 devices in a mesh: gx: 4 (over x, core), gy: 4 (over z), gz: 2 (over y).
Axes of the slice: x: 2, y: 2, z: 4, core: 2. Of those that a mesh axis runs over, the one named last changes fastest.
Arguments:
- field: bfloat16 [1, 64, 16, 32, 256], P(None, None, 'gx', 'gy', 'gz'), may hold values from -6 to 6
- kernel_one: bfloat16 [3, 3, 3, 64, 64], replicated, may hold values from -0.15625 to 0.15625
- bias_one: float32 [64], replicated, may hold values from -3 to 3
- kernel_two: bfloat16 [3, 3, 3, 64, 64], replicated, may hold values from -0.15625 to 0.15625
- bias_two: float32 [64], replicated, may hold values from -3 to 3
- kernel_three: bfloat16 [3, 3, 3, 64, 64], replicated, may hold values from -0.15625 to 0.15625
- bias_three: float32 [64], replicated, may hold values from -3 to 3
Outputs:
- latent: bfloat16 [1, 64, 16, 32, 256], P(None, None, 'gx', 'gy', 'gz')
All inputs are finite; a program needn't handle non-finite values.
Results may differ from a plain program's by a relative error of at most 0.0048.
Values may be sent and summed in bfloat16 or wider, within the bound.
No kernel may reach another device: no remote copies, remote signals or barrier semaphores. Data moves between devices by JAX's collectives and lax.ppermute only.
A program may use at most 256 MiB of HBM per device.

v0:
```python
import jax
import jax.numpy as jnp
from jax import lax
from jax.sharding import PartitionSpec as P


def extended(cells, sides, width):
    for axis, dim in sides:
        count = lax.axis_size(axis)
        head = lax.slice_in_dim(cells, 0, width, axis=dim)
        tail = lax.slice_in_dim(cells, cells.shape[dim] - width, cells.shape[dim], axis=dim)
        cells = jnp.concatenate(
            [
                lax.ppermute(tail, axis, [(i, (i + 1) % count) for i in range(count)]),
                cells,
                lax.ppermute(head, axis, [((i + 1) % count, i) for i in range(count)]),
            ],
            axis=dim,
        )
    return cells


def conv_valid(padded, kernel, bias):
    width = padded.shape[2] - 2
    height = padded.shape[3] - 2
    length = padded.shape[4] - 2
    outputs = kernel.shape[3]
    inputs = kernel.shape[4]
    total = None
    for along_x in range(3):
        for along_y in range(3):
            matrix = jnp.transpose(kernel[along_x, along_y], (1, 0, 2)).reshape(outputs, 3 * inputs)
            stacked = jnp.concatenate(
                [
                    padded[
                        :,
                        :,
                        along_x : along_x + width,
                        along_y : along_y + height,
                        along_z : along_z + length,
                    ]
                    for along_z in range(3)
                ],
                axis=1,
            )
            term = jnp.einsum(
                "oc,bcxyz->boxyz", matrix, stacked, preferred_element_type=jnp.float32
            )
            total = term if total is None else total + term
    total = total + bias[None, :, None, None, None]
    return jax.nn.gelu(total, approximate=False).astype(jnp.bfloat16)


def shards(field, kernel_one, bias_one, kernel_two, bias_two, kernel_three, bias_three):
    layers = ((kernel_one, bias_one), (kernel_two, bias_two), (kernel_three, bias_three))
    values = field
    for kernel, bias in layers:
        padded = extended(values, (("gx", 2), ("gy", 3), ("gz", 4)), 1)
        values = conv_valid(padded, kernel, bias)
    return values


def solution(mesh):
    return jax.shard_map(
        shards,
        mesh=mesh,
        in_specs=(P(None, None, "gx", "gy", "gz"), P(), P(), P(), P(), P(), P()),
        out_specs=P(None, None, "gx", "gy", "gz"),
        check_vma=False,
    )
```

profile of v0, /device:TPU:0, one launch (start us, length us, event | category | flops | bytes accessed | tf_op | source)
XLA Modules:
  0.0 121.0 jit_solution(5962446504032791109)
XLA Ops:
  0.0 1.3 %copy.103 = bf16[1,64,4,8,128]{4,1,3,2,0:T(8,128)(2,1)S(1)} copy(bf16[1,64,4,8,128]{4,3,2,1,0:T(8,128)(2,1)} %param.7) | data formatting | bytes 1048576 | tf_op args[0]
  1.9 2.0 %collective-permute-start.1 = (bf16[1,64,1,8,128]{4,1,3,2,0:T(8,128)(2,1)S(1)}, bf16[1,64,1,8,128]{4,1,3,2,0:T(8,128)(2,1)S(1)}, u32[]{:S(2)}, u32[]{:S(2)}) collective-permute-start(bf16[1,64,1,8,128]{4,1,3,2,0:T(8,128)(2,1)S(1)} %get-tuple-element.103), channel_id=1, source_target_pairs={{8,0},{16,8},{24,16},{0,24},{9,1},{17,9},{25,17},{1,25},{10,2},{18... | collective-permute-start | bytes 393224 | tf_op jit(solution)/shard_map/ppermute | solution.py:16
  3.9 2.6 %collective-permute-done = bf16[1,64,1,8,128]{4,1,3,2,0:T(8,128)(2,1)S(1)} collective-permute-done((bf16[1,64,1,8,128]{4,1,3,2,0:T(8,128)(2,1)S(1)}, bf16[1,64,1,8,128]{4,1,3,2,0:T(8,128)(2,1)S(1)}, u32[]{:S(2)}, u32[]{:S(2)}) %collective-permute-start) | collective-permute-done | bytes 131104 | tf_op jit(solution)/shard_map/ppermute | solution.py:14
  6.7 1.0 collective-permute-done.1
  7.7 1.6 %collective-permute-start.2 = (bf16[1,64,6,1,128]{4,1,3,2,0:T(8,128)(2,1)S(1)}, bf16[1,64,6,1,128]{4,1,3,2,0:T(8,128)(2,1)S(1)}, u32[]{:S(2)}, u32[]{:S(2)}) collective-permute-start(bf16[1,64,6,1,128]{4,1,3,2,0:T(8,128)(2,1)S(1)} %get-tuple-element.97), channel_id=1, source_target_pairs={{0,2},{2,4},{4,6},{6,0},{1,3},{3,5},{5,7},{7,1},{8,10},{10,12},{12... | collective-permute-start | bytes 294920 | tf_op jit(solution)/shard_map/ppermute | solution.py:14
  9.4 2.6 %collective-permute-start.3 = (bf16[1,64,6,1,128]{4,1,3,2,0:T(8,128)(2,1)S(1)}, bf16[1,64,6,1,128]{4,1,3,2,0:T(8,128)(2,1)S(1)}, u32[]{:S(2)}, u32[]{:S(2)}) collective-permute-start(bf16[1,64,6,1,128]{4,1,3,2,0:T(8,128)(2,1)S(1)} %get-tuple-element.98), channel_id=1, source_target_pairs={{2,0},{4,2},{6,4},{0,6},{3,1},{5,3},{7,5},{1,7},{10,8},{12,10},{14... | collective-permute-start | bytes 294920 | tf_op jit(solution)/shard_map/ppermute | solution.py:16
  12.0 0.7 copy.113
  14.1 0.7 copy.120
  14.8 0.7 copy.122
  16.2 0.7 copy.127
  18.9 1.6 %collective-permute-start.4 = (bf16[1,64,6,10,1]{1,2,4,3,0:T(8,128)(2,1)S(1)}, bf16[1,64,6,10,1]{1,2,4,3,0:T(8,128)(2,1)S(1)}, u32[]{:S(2)}, u32[]{:S(2)}) collective-permute-start(bf16[1,64,6,10,1]{1,2,4,3,0:T(8,128)(2,1)S(1)} %copy.106), channel_id=1, source_target_pairs={{0,1},{1,0},{2,3},{3,2},{4,5},{5,4},{6,7},{7,6},{8,9},{9,8},{10,11... | collective-permute-start | bytes 23048 | tf_op jit(solution)/shard_map/ppermute | solution.py:14
  21.6 1.4 %fusion.246 = (bf16[1,64,4,8,128]{4,1,3,2,0:T(8,128)(2,1)}, bf16[1,64,4,8,128]{4,1,3,2,0:T(8,128)(2,1)}, bf16[1,64,4,8,128]{4,1,3,2,0:T(8,128)(2,1)}, bf16[1,64,4,8,128]{4,1,3,2,0:T(8,128)(2,1)}) fusion(bf16[1,64,6,8,128]{4,1,3,2,0:T(8,128)(2,1)S(1)} %constant_dynamic-update-slice_fusion, bf16[1,64,6,1,128]{4,1,3,2,0:T(8,128)(2,1)S(1)} %collective-permute-done.2, ...), kind=kLoop, calls=%fused_computation.304 | loop fusion | flops 1048576 | bytes 3080192 | tf_op jit(solution)/shard_map/concatenate | solution.py:12
  23.5 1.5 %collective-permute-done.5 = bf16[1,64,6,10,1]{1,2,4,3,0:T(8,128)(2,1)} collective-permute-done((bf16[1,64,6,10,1]{1,2,4,3,0:T(8,128)(2,1)S(1)}, bf16[1,64,6,10,1]{1,2,4,3,0:T(8,128)(2,1)}, u32[]{:S(2)}, u32[]{:S(2)}) %collective-permute-start.5) | collective-permute-done | bytes 7712 | tf_op jit(solution)/shard_map/ppermute | solution.py:16
  25.0 1.2 %copy.109 = bf16[1,64,6,10,1]{4,1,3,2,0:T(8,128)(2,1)S(1)} copy(bf16[1,64,6,10,1]{1,2,4,3,0:T(8,128)(2,1)} %collective-permute-done.5) | data formatting | bytes 15360 | tf_op jit(solution)/shard_map/ppermute | solution.py:16
  26.2 1.8 %maximum_maximum_fusion = (bf16[1,64,6,10,129]{4,1,3,2,0:T(8,128)(2,1)S(1)}, bf16[1,64,6,10,129]{4,1,3,2,0:T(8,128)(2,1)S(1)}) fusion(bf16[1,64,6,1,128]{4,1,3,2,0:T(8,128)(2,1)S(1)} %collective-permute-done.3, bf16[1,64,6,8,128]{4,1,3,2,0:T(8,128)(2,1)S(1)} %constant_dynamic-update-slice_fusion, bf16[1,64,6,1,128]{4,1,3,2,0:T(8,128)(2,1)S(1)} %collective-permute-done.2, ...), kind=kLoop, calls=%fused_computation | loop fusion | flops 7925760 | bytes 2979840 | tf_op jit(solution)/shard_map/concatenate | solution.py:12
  28.0 2.7 %fusion.278 = (bf16[1,64,4,8,128]{4,1,3,2,0:T(8,128)(2,1)S(1)}, bf16[1,64,4,8,128]{4,1,3,2,0:T(8,128)(2,1)S(1)}, bf16[1,64,4,8,128]{4,1,3,2,0:T(8,128)(2,1)S(1)}...) fusion(bf16[1,64,6,10,129]{4,1,3,2,0:T(8,128)(2,1)S(1)} %get-tu, ...), kind=kLoop, calls=%fused_computation.372 | loop fusion | bytes 18874368 | tf_op jit(solution)/shard_map/slice | solution.py:35
  38.4 3.1 %fusion.191 = bf16[1,64,4,8,128]{4,1,3,2,0:T(8,128)(2,1)S(1)} fusion(f32[4,8,128,64]{2,3,1,0:T(8,128)S(1)} %fusion.27, f32[4,8,128,64]{2,3,1,0:T(8,128)S(1)} %fusion.33, f32[4,8,128,64]{2,3,1,0:T(8,128)S(1)} %fusion.39, f32[4,8,128,64]{2,3,1,0:T(8,128)S(1)} %fusion.70, f32[4,8,128,64]{2,3,1,0:T(8,128)S(1)} %fusion.65, f32[4,8,128,64]{2,3,1,0:T(8,128)S(1)} %fusion.60, ...), kind=kOutput, calls=%fused_computation.223 | convolution fusion | flops 124780544 | bytes 10510592 | tf_op jit(solution)/shard_map/oc,bcxyz->boxyz/dot_general | solution.py:46
  41.5 1.7 %collective-permute-start.7 = (bf16[1,64,1,8,128]{4,1,3,2,0:T(8,128)(2,1)S(1)}, bf16[1,64,1,8,128]{4,1,3,2,0:T(8,128)(2,1)S(1)}, u32[]{:S(2)}, u32[]{:S(2)}) collective-permute-start(bf16[1,64,1,8,128]{4,1,3,2,0:T(8,128)(2,1)S(1)} %get-tuple-element.102), channel_id=1, source_target_pairs={{8,0},{16,8},{24,16},{0,24},{9,1},{17,9},{25,17},{1,25},{10,2},{18... | collective-permute-start | bytes 393224 | tf_op jit(solution)/shard_map/ppermute | solution.py:16
  43.3 2.6 %collective-permute-done.6 = bf16[1,64,1,8,128]{4,1,3,2,0:T(8,128)(2,1)S(1)} collective-permute-done((bf16[1,64,1,8,128]{4,1,3,2,0:T(8,128)(2,1)S(1)}, bf16[1,64,1,8,128]{4,1,3,2,0:T(8,128)(2,1)S(1)}, u32[]{:S(2)}, u32[]{:S(2)}) %collective-permute-start.6) | collective-permute-done | bytes 131104 | tf_op jit(solution)/shard_map/ppermute | solution.py:14
  45.9 0.9 collective-permute-done.7
  46.9 3.8 %collective-permute-start.9 = (bf16[1,64,6,1,128]{4,1,3,2,0:T(8,128)(2,1)S(1)}, bf16[1,64,6,1,128]{4,1,3,2,0:T(8,128)(2,1)S(1)}, u32[]{:S(2)}, u32[]{:S(2)}) collective-permute-start(bf16[1,64,6,1,128]{4,1,3,2,0:T(8,128)(2,1)S(1)} %get-tuple-element.94), channel_id=1, source_target_pairs={{2,0},{4,2},{6,4},{0,6},{3,1},{5,3},{7,5},{1,7},{10,8},{12,10},{14... | collective-permute-start | bytes 294920 | tf_op jit(solution)/shard_map/ppermute | solution.py:16
  50.8 0.7 copy.139
  55.8 0.7 copy.135
  57.7 0.9 collective-permute-start.10
  59.1 1.2 %collective-permute-start.11 = (bf16[1,64,6,10,1]{1,2,4,3,0:T(8,128)(2,1)S(1)}, bf16[1,64,6,10,1]{1,2,4,3,0:T(8,128)(2,1)}, u32[]{:S(2)}, u32[]{:S(2)}) collective-permute-start(bf16[1,64,6,10,1]{1,2,4,3,0:T(8,128)(2,1)S(1)} %copy.133), channel_id=1, source_target_pairs={{1,0},{0,1},{3,2},{2,3},{5,4},{4,5},{7,6},{6,7},{9,8},{8,9},{11,10... | collective-permute-start | bytes 23048 | tf_op jit(solution)/shard_map/ppermute | solution.py:16
  60.5 1.2 %fusion.286 = (bf16[1,64,4,8,128]{4,1,3,2,0:T(8,128)(2,1)}, bf16[1,64,4,8,128]{4,1,3,2,0:T(8,128)(2,1)}, bf16[1,64,4,8,128]{4,1,3,2,0:T(8,128)(2,1)}) fusion(bf16[1,64,6,9,128]{4,1,3,2,0:T(8,128)(2,1)S(1)} %get-tuple-element.92), kind=kLoop, calls=%fused_computation.380 | loop fusion | bytes 3145728 | tf_op jit(solution)/shard_map/slice | solution.py:35
  61.7 1.3 %fusion.285 = (bf16[1,64,4,8,128]{4,1,3,2,0:T(8,128)(2,1)S(1)}, bf16[1,64,4,8,128]{4,1,3,2,0:T(8,128)(2,1)}, bf16[1,64,4,8,128]{4,1,3,2,0:T(8,128)(2,1)}) fusion(bf16[1,64,6,9,128]{4,1,3,2,0:T(8,128)(2,1)S(1)} %get-tuple-element.91), kind=kLoop, calls=%fused_computation.379 | loop fusion | bytes 3145728 | tf_op jit(solution)/shard_map/slice | solution.py:35
  63.6 1.2 %copy.134 = bf16[1,64,6,10,1]{4,1,3,2,0:T(8,128)(2,1)S(1)} copy(bf16[1,64,6,10,1]{1,2,4,3,0:T(8,128)(2,1)} %collective-permute-done.11) | data formatting | bytes 15360 | tf_op jit(solution)/shard_map/ppermute | solution.py:16
  64.8 2.8 %maximum_maximum_fusion.1 = (bf16[1,64,6,10,129]{4,1,3,2,0:T(8,128)(2,1)S(1)}, bf16[1,64,6,10,129]{4,1,3,2,0:T(8,128)(2,1)S(1)}) fusion(bf16[1,64,6,1,128]{4,1,3,2,0:T(8,128)(2,1)S(1)} %collective-permute-done.9, bf16[1,64,1,8,128]{4,1,3,2,0:T(8,128)(2,1)S(1)} %collective-permute-done.7, bf16[1,64,4,8,128]{4,1,3,2,0:T(8,128)(2,1)S(1)} %fusion.191, ...), kind=kLoop, calls=%fused_computation.2 | loop fusion | flops 11888640 | bytes 2979840 | tf_op jit(solution)/shard_map/concatenate | solution.py:12
  67.6 1.2 fusion.276
  68.8 1.4 %fusion.277 = (bf16[1,64,4,8,128]{4,1,3,2,0:T(8,128)(2,1)S(1)}, bf16[1,64,4,8,128]{4,1,3,2,0:T(8,128)(2,1)S(1)}, bf16[1,64,4,8,128]{4,1,3,2,0:T(8,128)(2,1)S(1)}...) fusion(bf16[1,64,6,10,129]{4,1,3,2,0:T(8,128)(2,1)S(1)} %get-tu, ...), kind=kLoop, calls=%fused_computation.371 | loop fusion | bytes 9437184 | tf_op jit(solution)/shard_map/slice | solution.py:35
  77.5 3.0 %fusion.194 = bf16[1,64,4,8,128]{4,1,3,2,0:T(8,128)(2,1)S(1)} fusion(f32[4,8,128,64]{2,3,1,0:T(8,128)S(1)} %fusion.115, f32[4,8,128,64]{2,3,1,0:T(8,128)S(1)} %fusion.15, f32[4,8,128,64]{2,3,1,0:T(8,128)S(1)} %fusion.108, f32[4,8,128,64]{2,3,1,0:T(8,128)S(1)} %fusion.103, f32[4,8,128,64]{2,3,1,0:T(8,128)S(1)} %fusion.98, ...), kind=kOutput, calls=%fused_computation.226 | convolution fusion | flops 124780544 | bytes 10510592 | tf_op jit(solution)/shard_map/oc,bcxyz->boxyz/dot_general | solution.py:46
  80.7 1.7 %collective-permute-start.13 = (bf16[1,64,1,8,128]{4,1,3,2,0:T(8,128)(2,1)S(1)}, bf16[1,64,1,8,128]{4,1,3,2,0:T(8,128)(2,1)S(1)}, u32[]{:S(2)}, u32[]{:S(2)}) collective-permute-start(bf16[1,64,1,8,128]{4,1,3,2,0:T(8,128)(2,1)S(1)} %get-tuple-element.100), channel_id=1, source_target_pairs={{8,0},{16,8},{24,16},{0,24},{9,1},{17,9},{25,17},{1,25},{10,2},{18... | collective-permute-start | bytes 393224 | tf_op jit(solution)/shard_map/ppermute | solution.py:16
  82.4 2.6 %collective-permute-done.12 = bf16[1,64,1,8,128]{4,1,3,2,0:T(8,128)(2,1)S(1)} collective-permute-done((bf16[1,64,1,8,128]{4,1,3,2,0:T(8,128)(2,1)S(1)}, bf16[1,64,1,8,128]{4,1,3,2,0:T(8,128)(2,1)S(1)}, u32[]{:S(2)}, u32[]{:S(2)}) %collective-permute-start.12) | collective-permute-done | bytes 131104 | tf_op jit(solution)/shard_map/ppermute | solution.py:14
  85.0 1.0 collective-permute-done.13
  86.1 3.8 %collective-permute-start.15 = (bf16[1,64,6,1,128]{4,1,3,2,0:T(8,128)(2,1)S(1)}, bf16[1,64,6,1,128]{4,1,3,2,0:T(8,128)(2,1)S(1)}, u32[]{:S(2)}, u32[]{:S(2)}) collective-permute-start(bf16[1,64,6,1,128]{4,1,3,2,0:T(8,128)(2,1)S(1)} %get-tuple-element.90), channel_id=1, source_target_pairs={{2,0},{4,2},{6,4},{0,6},{3,1},{5,3},{7,5},{1,7},{10,8},{12,10},{14... | collective-permute-start | bytes 294920 | tf_op jit(solution)/shard_map/ppermute | solution.py:16
  90.1 0.7 copy.161
  95.0 0.7 copy.157
  97.0 0.9 collective-permute-start.16
  98.4 1.2 %collective-permute-start.17 = (bf16[1,64,6,10,1]{1,2,4,3,0:T(8,128)(2,1)S(1)}, bf16[1,64,6,10,1]{1,2,4,3,0:T(8,128)(2,1)}, u32[]{:S(2)}, u32[]{:S(2)}) collective-permute-start(bf16[1,64,6,10,1]{1,2,4,3,0:T(8,128)(2,1)S(1)} %copy.155), channel_id=1, source_target_pairs={{1,0},{0,1},{3,2},{2,3},{5,4},{4,5},{7,6},{6,7},{9,8},{8,9},{11,10... | collective-permute-start | bytes 23048 | tf_op jit(solution)/shard_map/ppermute | solution.py:16
  99.8 1.2 %fusion.284 = (bf16[1,64,4,8,128]{4,1,3,2,0:T(8,128)(2,1)}, bf16[1,64,4,8,128]{4,1,3,2,0:T(8,128)(2,1)}, bf16[1,64,4,8,128]{4,1,3,2,0:T(8,128)(2,1)}) fusion(bf16[1,64,6,9,128]{4,1,3,2,0:T(8,128)(2,1)S(1)} %get-tuple-element.88), kind=kLoop, calls=%fused_computation.378 | loop fusion | bytes 3145728 | tf_op jit(solution)/shard_map/slice | solution.py:35
  101.0 1.3 %fusion.283 = (bf16[1,64,4,8,128]{4,1,3,2,0:T(8,128)(2,1)S(1)}, bf16[1,64,4,8,128]{4,1,3,2,0:T(8,128)(2,1)}, bf16[1,64,4,8,128]{4,1,3,2,0:T(8,128)(2,1)}) fusion(bf16[1,64,6,9,128]{4,1,3,2,0:T(8,128)(2,1)S(1)} %get-tuple-element.87), kind=kLoop, calls=%fused_computation.377 | loop fusion | bytes 3145728 | tf_op jit(solution)/shard_map/slice | solution.py:35
  102.9 1.2 %copy.156 = bf16[1,64,6,10,1]{4,1,3,2,0:T(8,128)(2,1)S(1)} copy(bf16[1,64,6,10,1]{1,2,4,3,0:T(8,128)(2,1)} %collective-permute-done.17) | data formatting | bytes 15360 | tf_op jit(solution)/shard_map/ppermute | solution.py:16
  104.1 2.8 %maximum_maximum_fusion.2 = (bf16[1,64,6,10,129]{4,1,3,2,0:T(8,128)(2,1)S(1)}, bf16[1,64,6,10,129]{4,1,3,2,0:T(8,128)(2,1)S(1)}) fusion(bf16[1,64,6,1,128]{4,1,3,2,0:T(8,128)(2,1)S(1)} %collective-permute-done.15, bf16[1,64,1,8,128]{4,1,3,2,0:T(8,128)(2,1)S(1)} %collective-permute-done.13, bf16[1,64,4,8,128]{4,1,3,2,0:T(8,128)(2,1)S(1)} %fusion.194, ...), kind=kLoop, calls=%fused_computation.4 | loop fusion | flops 11888640 | bytes 2979840 | tf_op jit(solution)/shard_map/concatenate | solution.py:12
  106.9 1.2 fusion.274
  108.1 1.4 %fusion.275 = (bf16[1,64,4,8,128]{4,1,3,2,0:T(8,128)(2,1)S(1)}, bf16[1,64,4,8,128]{4,1,3,2,0:T(8,128)(2,1)S(1)}, bf16[1,64,4,8,128]{4,1,3,2,0:T(8,128)(2,1)S(1)}...) fusion(bf16[1,64,6,10,129]{4,1,3,2,0:T(8,128)(2,1)S(1)} %get-tu, ...), kind=kLoop, calls=%fused_computation.369 | loop fusion | bytes 9437184 | tf_op jit(solution)/shard_map/slice | solution.py:35
  116.8 3.0 %fusion.197 = bf16[1,64,4,8,128]{4,1,3,2,0:T(8,128)(2,1)S(1)} fusion(f32[4,8,128,64]{2,3,1,0:T(8,128)S(1)} %fusion.154, f32[4,8,128,64]{2,3,1,0:T(8,128)S(1)} %fusion.3, f32[4,8,128,64]{2,3,1,0:T(8,128)S(1)} %fusion.147, f32[4,8,128,64]{2,3,1,0:T(8,128)S(1)} %fusion.142, f32[4,8,128,64]{2,3,1,0:T(8,128)S(1)} %fusion.137, ...), kind=kOutput, calls=%fused_computation.229 | convolution fusion | flops 124780544 | bytes 10510592 | tf_op jit(solution)/shard_map/oc,bcxyz->boxyz/dot_general | solution.py:46
  119.8 1.1 copy.175
  (187 shorter events, 42.4 us)
Async XLA Ops:
  0.0 6.5 %copy-start = (bf16[1,64,4,8,128]{4,3,2,1,0:T(8,128)(2,1)S(1)}, bf16[1,64,4,8,128]{4,3,2,1,0:T(8,128)(2,1)}, u32[]{:S(2)}) copy-start(bf16[1,64,4,8,128]{4,3,2,1,0:T(8,128)(2,1)} %param.7) | copy-start | bytes 1572868
  0.0 11.9 %copy-start.15 = (bf16[3,3,3,64,64]{4,3,2,1,0:T(8,128)(2,1)S(1)}, bf16[3,3,3,64,64]{4,3,2,1,0:T(8,128)(2,1)}, u32[]{:S(2)}) copy-start(bf16[3,3,3,64,64]{4,3,2,1,0:T(8,128)(2,1)} %param.8) | copy-start | bytes 663556
  1.4 5.1 %collective-permute-start = (bf16[1,64,1,8,128]{4,1,3,2,0:T(8,128)(2,1)S(1)}, bf16[1,64,1,8,128]{4,1,3,2,0:T(8,128)(2,1)S(1)}, u32[]{:S(2)}, u32[]{:S(2)}) collective-permute-start(bf16[1,64,1,8,128]{4,1,3,2,0:T(8,128)(2,1)S(1)} %get-tuple-element.104), channel_id=1, source_target_pairs={{0,8},{8,16},{16,24},{24,0},{1,9},{9,17},{17,25},{25,1},{2,10},{10... | collective-permute-start | bytes 393224 | tf_op jit(solution)/shard_map/ppermute | solution.py:14
  1.9 5.8 %collective-permute-start.1 = (bf16[1,64,1,8,128]{4,1,3,2,0:T(8,128)(2,1)S(1)}, bf16[1,64,1,8,128]{4,1,3,2,0:T(8,128)(2,1)S(1)}, u32[]{:S(2)}, u32[]{:S(2)}) collective-permute-start(bf16[1,64,1,8,128]{4,1,3,2,0:T(8,128)(2,1)S(1)} %get-tuple-element.103), channel_id=1, source_target_pairs={{8,0},{16,8},{24,16},{0,24},{9,1},{17,9},{25,17},{1,25},{10,2},{18... | collective-permute-start | bytes 393224 | tf_op jit(solution)/shard_map/ppermute | solution.py:16
  6.5 2.9 %copy-start.20 = (bf16[1,64,1,8,128]{4,1,3,2,0:T(8,128)(2,1)}, bf16[1,64,1,8,128]{4,1,3,2,0:T(8,128)(2,1)S(1)}, u32[]{:S(2)}) copy-start(bf16[1,64,1,8,128]{4,1,3,2,0:T(8,128)(2,1)S(1)} %collective-permute-done) | copy-start | bytes 393220
  7.7 1.7 %copy-start.18 = (bf16[1,64,1,8,128]{4,1,3,2,0:T(8,128)(2,1)}, bf16[1,64,1,8,128]{4,1,3,2,0:T(8,128)(2,1)S(1)}, u32[]{:S(2)}) copy-start(bf16[1,64,1,8,128]{4,1,3,2,0:T(8,128)(2,1)S(1)} %collective-permute-done.1) | copy-start | bytes 393220
  7.7 10.0 %collective-permute-start.2 = (bf16[1,64,6,1,128]{4,1,3,2,0:T(8,128)(2,1)S(1)}, bf16[1,64,6,1,128]{4,1,3,2,0:T(8,128)(2,1)S(1)}, u32[]{:S(2)}, u32[]{:S(2)}) collective-permute-start(bf16[1,64,6,1,128]{4,1,3,2,0:T(8,128)(2,1)S(1)} %get-tuple-element.97), channel_id=1, source_target_pairs={{0,2},{2,4},{4,6},{6,0},{1,3},{3,5},{5,7},{7,1},{8,10},{10,12},{12... | collective-permute-start | bytes 294920 | tf_op jit(solution)/shard_map/ppermute | solution.py:14
  9.4 8.4 %collective-permute-start.3 = (bf16[1,64,6,1,128]{4,1,3,2,0:T(8,128)(2,1)S(1)}, bf16[1,64,6,1,128]{4,1,3,2,0:T(8,128)(2,1)S(1)}, u32[]{:S(2)}, u32[]{:S(2)}) collective-permute-start(bf16[1,64,6,1,128]{4,1,3,2,0:T(8,128)(2,1)S(1)} %get-tuple-element.98), channel_id=1, source_target_pairs={{2,0},{4,2},{6,4},{0,6},{3,1},{5,3},{7,5},{1,7},{10,8},{12,10},{14... | collective-permute-start | bytes 294920 | tf_op jit(solution)/shard_map/ppermute | solution.py:16
  18.9 4.0 %collective-permute-start.4 = (bf16[1,64,6,10,1]{1,2,4,3,0:T(8,128)(2,1)S(1)}, bf16[1,64,6,10,1]{1,2,4,3,0:T(8,128)(2,1)S(1)}, u32[]{:S(2)}, u32[]{:S(2)}) collective-permute-start(bf16[1,64,6,10,1]{1,2,4,3,0:T(8,128)(2,1)S(1)} %copy.106), channel_id=1, source_target_pairs={{0,1},{1,0},{2,3},{3,2},{4,5},{5,4},{6,7},{7,6},{8,9},{9,8},{10,11... | collective-permute-start | bytes 23048 | tf_op jit(solution)/shard_map/ppermute | solution.py:14
  21.1 3.9 %collective-permute-start.5 = (bf16[1,64,6,10,1]{1,2,4,3,0:T(8,128)(2,1)S(1)}, bf16[1,64,6,10,1]{1,2,4,3,0:T(8,128)(2,1)}, u32[]{:S(2)}, u32[]{:S(2)}) collective-permute-start(bf16[1,64,6,10,1]{1,2,4,3,0:T(8,128)(2,1)S(1)} %copy.108), channel_id=1, source_target_pairs={{1,0},{0,1},{3,2},{2,3},{5,4},{4,5},{7,6},{6,7},{9,8},{8,9},{11,10... | collective-permute-start | bytes 23048 | tf_op jit(solution)/shard_map/ppermute | solution.py:16
  28.0 2.7 %copy-start.45 = (bf16[64,3,64]{0,2,1:T(8,128)(2,1)S(1)}, bf16[64,3,64]{0,2,1:T(8,128)(2,1)}, u32[]{:S(2)}) copy-start(bf16[64,3,64]{0,2,1:T(8,128)(2,1)} %copy.120) | copy-start | bytes 73732
  30.8 1.0 copy-start.14
  31.8 1.0 copy-start.13
  31.8 1.0 copy-start.43
  32.9 1.0 copy-start.10
  32.9 1.0 copy-start.40
  37.3 1.0 copy-start.46
  38.4 12.3 %copy-start.16 = (bf16[3,3,3,64,64]{4,3,2,1,0:T(8,128)(2,1)S(1)}, bf16[3,3,3,64,64]{4,3,2,1,0:T(8,128)(2,1)}, u32[]{:S(2)}) copy-start(bf16[3,3,3,64,64]{4,3,2,1,0:T(8,128)(2,1)} %param.10) | copy-start | bytes 663556
  41.5 4.4 %collective-permute-start.6 = (bf16[1,64,1,8,128]{4,1,3,2,0:T(8,128)(2,1)S(1)}, bf16[1,64,1,8,128]{4,1,3,2,0:T(8,128)(2,1)S(1)}, u32[]{:S(2)}, u32[]{:S(2)}) collective-permute-start(bf16[1,64,1,8,128]{4,1,3,2,0:T(8,128)(2,1)S(1)} %get-tuple-element.101), channel_id=1, source_target_pairs={{0,8},{8,16},{16,24},{24,0},{1,9},{9,17},{17,25},{25,1},{2,10},{10... | collective-permute-start | bytes 393224 | tf_op jit(solution)/shard_map/ppermute | solution.py:14
  41.5 5.2 %collective-permute-start.7 = (bf16[1,64,1,8,128]{4,1,3,2,0:T(8,128)(2,1)S(1)}, bf16[1,64,1,8,128]{4,1,3,2,0:T(8,128)(2,1)S(1)}, u32[]{:S(2)}, u32[]{:S(2)}) collective-permute-start(bf16[1,64,1,8,128]{4,1,3,2,0:T(8,128)(2,1)S(1)} %get-tuple-element.102), channel_id=1, source_target_pairs={{8,0},{16,8},{24,16},{0,24},{9,1},{17,9},{25,17},{1,25},{10,2},{18... | collective-permute-start | bytes 393224 | tf_op jit(solution)/shard_map/ppermute | solution.py:16
  46.8 9.7 %collective-permute-start.8 = (bf16[1,64,6,1,128]{4,1,3,2,0:T(8,128)(2,1)S(1)}, bf16[1,64,6,1,128]{4,1,3,2,0:T(8,128)(2,1)S(1)}, u32[]{:S(2)}, u32[]{:S(2)}) collective-permute-start(bf16[1,64,6,1,128]{4,1,3,2,0:T(8,128)(2,1)S(1)} %get-tuple-element.93), channel_id=1, source_target_pairs={{0,2},{2,4},{4,6},{6,0},{1,3},{3,5},{5,7},{7,1},{8,10},{10,12},{12... | collective-permute-start | bytes 294920 | tf_op jit(solution)/shard_map/ppermute | solution.py:14
  46.9 9.6 %collective-permute-start.9 = (bf16[1,64,6,1,128]{4,1,3,2,0:T(8,128)(2,1)S(1)}, bf16[1,64,6,1,128]{4,1,3,2,0:T(8,128)(2,1)S(1)}, u32[]{:S(2)}, u32[]{:S(2)}) collective-permute-start(bf16[1,64,6,1,128]{4,1,3,2,0:T(8,128)(2,1)S(1)} %get-tuple-element.94), channel_id=1, source_target_pairs={{2,0},{4,2},{6,4},{0,6},{3,1},{5,3},{7,5},{1,7},{10,8},{12,10},{14... | collective-permute-start | bytes 294920 | tf_op jit(solution)/shard_map/ppermute | solution.py:16
  57.7 5.4 %collective-permute-start.10 = (bf16[1,64,6,10,1]{1,2,4,3,0:T(8,128)(2,1)S(1)}, bf16[1,64,6,10,1]{1,2,4,3,0:T(8,128)(2,1)S(1)}, u32[]{:S(2)}, u32[]{:S(2)}) collective-permute-start(bf16[1,64,6,10,1]{1,2,4,3,0:T(8,128)(2,1)S(1)} %copy.131), channel_id=1, source_target_pairs={{0,1},{1,0},{2,3},{3,2},{4,5},{5,4},{6,7},{7,6},{8,9},{9,8},{10,11... | collective-permute-start | bytes 23048 | tf_op jit(solution)/shard_map/ppermute | solution.py:14
  59.1 4.5 %collective-permute-start.11 = (bf16[1,64,6,10,1]{1,2,4,3,0:T(8,128)(2,1)S(1)}, bf16[1,64,6,10,1]{1,2,4,3,0:T(8,128)(2,1)}, u32[]{:S(2)}, u32[]{:S(2)}) collective-permute-start(bf16[1,64,6,10,1]{1,2,4,3,0:T(8,128)(2,1)S(1)} %copy.133), channel_id=1, source_target_pairs={{1,0},{0,1},{3,2},{2,3},{5,4},{4,5},{7,6},{6,7},{9,8},{8,9},{11,10... | collective-permute-start | bytes 23048 | tf_op jit(solution)/shard_map/ppermute | solution.py:16
  68.8 1.4 %copy-start.41 = (bf16[64,3,64]{0,2,1:T(8,128)(2,1)S(1)}, bf16[64,3,64]{0,2,1:T(8,128)(2,1)}, u32[]{:S(2)}) copy-start(bf16[64,3,64]{0,2,1:T(8,128)(2,1)} %copy.143) | copy-start | bytes 73732
  70.3 1.0 copy-start.8
  71.3 1.0 copy-start.11
  71.3 1.0 copy-start.35
  72.4 1.0 copy-start.4
  72.4 1.0 copy-start.33
  73.4 1.0 copy-start.6
  73.4 1.0 copy-start.29
  74.4 1.0 copy-start.2
  74.4 1.0 copy-start.27
  77.5 12.4 %copy-start.17 = (bf16[3,3,3,64,64]{4,3,2,1,0:T(8,128)(2,1)S(1)}, bf16[3,3,3,64,64]{4,3,2,1,0:T(8,128)(2,1)}, u32[]{:S(2)}) copy-start(bf16[3,3,3,64,64]{4,3,2,1,0:T(8,128)(2,1)} %param.12) | copy-start | bytes 663556
  80.6 4.4 %collective-permute-start.12 = (bf16[1,64,1,8,128]{4,1,3,2,0:T(8,128)(2,1)S(1)}, bf16[1,64,1,8,128]{4,1,3,2,0:T(8,128)(2,1)S(1)}, u32[]{:S(2)}, u32[]{:S(2)}) collective-permute-start(bf16[1,64,1,8,128]{4,1,3,2,0:T(8,128)(2,1)S(1)} %get-tuple-element.99), channel_id=1, source_target_pairs={{0,8},{8,16},{16,24},{24,0},{1,9},{9,17},{17,25},{25,1},{2,10},{10... | collective-permute-start | bytes 393224 | tf_op jit(solution)/shard_map/ppermute | solution.py:14
  80.7 5.3 %collective-permute-start.13 = (bf16[1,64,1,8,128]{4,1,3,2,0:T(8,128)(2,1)S(1)}, bf16[1,64,1,8,128]{4,1,3,2,0:T(8,128)(2,1)S(1)}, u32[]{:S(2)}, u32[]{:S(2)}) collective-permute-start(bf16[1,64,1,8,128]{4,1,3,2,0:T(8,128)(2,1)S(1)} %get-tuple-element.100), channel_id=1, source_target_pairs={{8,0},{16,8},{24,16},{0,24},{9,1},{17,9},{25,17},{1,25},{10,2},{18... | collective-permute-start | bytes 393224 | tf_op jit(solution)/shard_map/ppermute | solution.py:16
  86.1 9.7 %collective-permute-start.14 = (bf16[1,64,6,1,128]{4,1,3,2,0:T(8,128)(2,1)S(1)}, bf16[1,64,6,1,128]{4,1,3,2,0:T(8,128)(2,1)S(1)}, u32[]{:S(2)}, u32[]{:S(2)}) collective-permute-start(bf16[1,64,6,1,128]{4,1,3,2,0:T(8,128)(2,1)S(1)} %get-tuple-element.89), channel_id=1, source_target_pairs={{0,2},{2,4},{4,6},{6,0},{1,3},{3,5},{5,7},{7,1},{8,10},{10,12},{12... | collective-permute-start | bytes 294920 | tf_op jit(solution)/shard_map/ppermute | solution.py:14
  86.1 9.6 %collective-permute-start.15 = (bf16[1,64,6,1,128]{4,1,3,2,0:T(8,128)(2,1)S(1)}, bf16[1,64,6,1,128]{4,1,3,2,0:T(8,128)(2,1)S(1)}, u32[]{:S(2)}, u32[]{:S(2)}) collective-permute-start(bf16[1,64,6,1,128]{4,1,3,2,0:T(8,128)(2,1)S(1)} %get-tuple-element.90), channel_id=1, source_target_pairs={{2,0},{4,2},{6,4},{0,6},{3,1},{5,3},{7,5},{1,7},{10,8},{12,10},{14... | collective-permute-start | bytes 294920 | tf_op jit(solution)/shard_map/ppermute | solution.py:16
  97.0 5.4 %collective-permute-start.16 = (bf16[1,64,6,10,1]{1,2,4,3,0:T(8,128)(2,1)S(1)}, bf16[1,64,6,10,1]{1,2,4,3,0:T(8,128)(2,1)S(1)}, u32[]{:S(2)}, u32[]{:S(2)}) collective-permute-start(bf16[1,64,6,10,1]{1,2,4,3,0:T(8,128)(2,1)S(1)} %copy.153), channel_id=1, source_target_pairs={{0,1},{1,0},{2,3},{3,2},{4,5},{5,4},{6,7},{7,6},{8,9},{9,8},{10,11... | collective-permute-start | bytes 23048 | tf_op jit(solution)/shard_map/ppermute | solution.py:14
  98.4 4.5 %collective-permute-start.17 = (bf16[1,64,6,10,1]{1,2,4,3,0:T(8,128)(2,1)S(1)}, bf16[1,64,6,10,1]{1,2,4,3,0:T(8,128)(2,1)}, u32[]{:S(2)}, u32[]{:S(2)}) collective-permute-start(bf16[1,64,6,10,1]{1,2,4,3,0:T(8,128)(2,1)S(1)} %copy.155), channel_id=1, source_target_pairs={{1,0},{0,1},{3,2},{2,3},{5,4},{4,5},{7,6},{6,7},{9,8},{8,9},{11,10... | collective-permute-start | bytes 23048 | tf_op jit(solution)/shard_map/ppermute | solution.py:16
  108.1 1.4 %copy-start.42 = (bf16[64,3,64]{0,2,1:T(8,128)(2,1)S(1)}, bf16[64,3,64]{0,2,1:T(8,128)(2,1)}, u32[]{:S(2)}) copy-start(bf16[64,3,64]{0,2,1:T(8,128)(2,1)} %copy.165) | copy-start | bytes 73732
  109.5 1.0 copy-start.9
  110.6 1.0 copy-start.36
  111.6 1.0 copy-start.34
  112.7 1.0 copy-start.30
  113.7 1.0 copy-start.3
  113.7 1.0 copy-start.28
  (19 other events, 17.3 us)
where the time goes:
time: 122 us; the launch traced here: 121 us
  local copies, waits for them, and re-layouts  53 us (43%)
  starting transfers between devices  24.4 us (20%)
  matrix products  21.2 us (17%)
  waiting for transfers between devices  12.2 us (10%)
  other arithmetic  9.56 us (8%)
    dot_general x27, matrix products, conv_valid(): jnp.einsum('oc,bcxyz->boxyz', matrix, stacked, preferred_element_type=jnp...  21.2 us
    ppermute x9, starting transfers between devices, extended(): lax.ppermute(head, axis, [((i + 1) % count, i) for i in range(count)])  18.6 us
    transpose x30, local copies, waits for them, and re-layouts, conv_valid(): jnp.transpose(kernel[along_x, along_y], (1, 0, 2))  17.4 us
    slice x9, local copies, waits for them, and re-layouts, conv_valid(): padded[:, :, along_x:along_x + width, along_y:along_y + height, along_z:a...  13.1 us
    unnamed x101, local copies, waits for them, and re-layouts  11.4 us
    concatenate x9, other arithmetic, extended(): jnp.concatenate([lax.ppermute(tail, axis, [(i, (i + 1) % count) for i in...  9.51 us
    ppermute x9, waiting for transfers between devices, extended(): lax.ppermute(tail, axis, [(i, (i + 1) % count) for i in range(count)])  7.9 us
    ppermute x9, starting transfers between devices, extended(): lax.ppermute(tail, axis, [(i, (i + 1) % count) for i in range(count)])  5.81 us
  transfers between devices with their start and end apart: 18, of which 7 were waited for; matrix products, arithmetic and copies ran while one was open for 23% of the time, Pallas kernels for 0%

commit v1 on v0

v1 whole, which is shorter than its diff:
```python
import jax
import jax.numpy as jnp
from jax import lax
from jax.experimental import pallas as pl
from jax.experimental.pallas import tpu as pltpu
from jax.sharding import PartitionSpec as P

HALO = 3
SQRT_HALF = 0.7071067811865476


def around(size):
    return -(-size // 16) * 16


def gelu(u):
    return 0.5 * u * (1.0 + lax.erf(u * SQRT_HALF))


def conv_line_block(source, x, first, lines, weight, bias):
    rows = source.shape[2]
    pieces = [
        source[x + a, first + e : first + e + lines].reshape(lines * rows, 128)
        for a in range(3)
        for e in range(3)
    ]
    stacked = jnp.concatenate(pieces, axis=1)
    both = lax.dot_general(
        stacked, weight, (((1,), (1,)), ((), ())), preferred_element_type=jnp.float32
    )
    here = both[:, :128]
    following = pltpu.roll(both[:, 128:], lines * rows - 1, 0)
    return gelu(here + following + bias).reshape(lines, rows, 128)


def layers_kernel(own, xm, xp, ym, yp, cm, cp, w1, w2, w3, b1, b2, b3, out, s0, s1, s2):
    nx, ny, rows, _ = own.shape
    h = HALO
    s0[h : h + nx, h : h + ny, :rows] = own[...]
    s0[:h, h : h + ny, :rows] = xm[...]
    s0[h + nx :, h : h + ny, :rows] = xp[...]
    s0[h : h + nx, :h, :rows] = ym[...]
    s0[h : h + nx, h + ny :, :rows] = yp[...]
    s0[:h, :h, :rows] = cm[:, :h]
    s0[:h, h + ny :, :rows] = cm[:, h:]
    s0[h + nx :, :h, :rows] = cp[:, :h]
    s0[h + nx :, h + ny :, :rows] = cp[:, h:]

    def layer(source, target, weight, bias, last):
        lines = source.shape[1] - 2

        def plane(x, carry):
            y = conv_line_block(source, x, 0, lines, weight[...], bias[...])
            y = y.astype(jnp.bfloat16)
            if last:
                target[x] = y[:, : target.shape[2]]
            else:
                target[x] = y
            return carry

        lax.fori_loop(0, source.shape[0] - 2, plane, 0)

    layer(s0, s1, w1, b1, False)
    layer(s1, s2, w2, b2, False)
    layer(s2, out, w3, b3, True)


def layers(own, xm, xp, ym, yp, cm, cp, ws, bs, pairs):
    nx, ny, rows, _ = own.shape
    pad = around(rows)
    h = HALO
    vm = pl.BlockSpec(memory_space=pltpu.VMEM)
    return pl.pallas_call(
        layers_kernel,
        out_shape=jax.ShapeDtypeStruct((nx, ny, pairs, 128), jnp.bfloat16),
        in_specs=[vm] * 13,
        out_specs=vm,
        scratch_shapes=[
            pltpu.VMEM((nx + 2 * k, ny + 2 * k, pad, 128), jnp.bfloat16)
            for k in (h, h - 1, h - 2)
        ],
        compiler_params=pltpu.CompilerParams(vmem_limit_bytes=60 * 1024 * 1024),
    )(own, xm, xp, ym, yp, cm, cp, *ws, *bs)


def folded(kernel):
    zero = jnp.zeros_like(kernel[:, :, 0])
    blocks = []
    for t in range(2):
        for q in range(2):
            taps = [p - q + 2 * t for p in range(2)]
            blocks.append(
                jnp.stack(
                    [kernel[:, :, f] if 0 <= f < 3 else zero for f in taps], axis=2
                )
            )
    w = jnp.stack(blocks, axis=0)
    _, _, _, _, o, c = w.shape
    return jnp.transpose(w, (0, 4, 1, 2, 3, 5)).reshape(4 * o, 18 * c)


def shift(x, axis, up):
    count = lax.axis_size(axis)
    pairs = [(i, (i + 1) % count) if up else ((i + 1) % count, i) for i in range(count)]
    return lax.ppermute(x, axis, pairs)


def swap_edges(tail, head, axis, dim):
    if lax.axis_size(axis) == 2:
        both = shift(jnp.concatenate([tail, head], axis=dim), axis, True)
        return jnp.split(both, 2, axis=dim)
    return shift(tail, axis, True), shift(head, axis, False)


def shards(field, kernel_one, bias_one, kernel_two, bias_two, kernel_three, bias_three):
    h = HALO
    ws = [folded(k) for k in (kernel_one, kernel_two, kernel_three)]
    bs = [jnp.concatenate([b, b])[None, :] for b in (bias_one, bias_two, bias_three)]
    _, c, nx, ny, nz = field.shape
    cells = jnp.transpose(field[0], (1, 2, 3, 0))
    left, right = swap_edges(cells[:, :, nz - h :], cells[:, :, :h], "gz", 2)
    own = jnp.concatenate([left, cells, right], axis=2)
    count = (nz + 2 * h) // 2
    rows = -(-count // 8) * 8
    own = own.reshape(nx, ny, count, 2 * c)
    own = jnp.pad(own, ((0, 0), (0, 0), (0, rows - count), (0, 0)))
    ym, yp = swap_edges(own[:, ny - h :], own[:, :h], "gy", 1)
    xm, xp = swap_edges(own[nx - h :], own[:h], "gx", 0)
    sides = jnp.concatenate([ym, yp], axis=1)
    cm, cp = swap_edges(sides[nx - h :], sides[:h], "gx", 0)
    out = layers(own, xm, xp, ym, yp, cm, cp, ws, bs, nz // 2)
    out = out.reshape(nx, ny, nz, c)
    return jnp.transpose(out, (3, 0, 1, 2))[None]


def solution(mesh):
    return jax.shard_map(
        shards,
        mesh=mesh,
        in_specs=(P(None, None, "gx", "gy", "gz"), P(), P(), P(), P(), P(), P()),
        out_specs=P(None, None, "gx", "gy", "gz"),
        check_vma=False,
    )
```

time: 122 us -> 62.1 us (0.51)
  local copies, waits for them, and re-layouts: 53 us -> 20.3 us
  matrix products: 21.2 us -> 0 us
  Pallas kernels: 0 us -> 17.1 us
  starting transfers between devices: 24.4 us -> 8.32 us
  other arithmetic: 9.56 us -> 3.03 us
    dot_general x27 -> x0, matrix products: 21.2 us -> none  [conv_valid(): jnp.einsum('oc,bcxyz->boxyz', matrix, stacked, preferred_element_type=jnp...]
    pallas_call x0 -> x1, Pallas kernels: none -> 17.1 us  [layers(): pl.pallas_call(layers_kernel, out_shape=jax.ShapeDtypeStruct((nx, ny, pai...]
    ppermute x18 -> x7, starting transfers between devices: 24.4 us -> 8.32 us  [shift(): return lax.ppermute(x, axis, pairs)]
    slice x22 -> x7, local copies, waits for them, and re-layouts: 17.8 us -> 1.83 us  [the longest x1 0.97 us: shards(): cm, cp = swap_edges(sides[nx - h:], sides[:h], 'gx', 0)]
    transpose x30 -> x3, local copies, waits for them, and re-layouts: 17.4 us -> 3.65 us  [folded(): return jnp.transpose(w, (0, 4, 1, 2, 3, 5)).reshape(4 * o, 18 * c)]
    concatenate x9 -> x2, other arithmetic: 9.51 us -> 0.89 us  [the longest x1 0.63 us: swap_edges(): both = shift(jnp.concatenate([tail, head], axis=dim), axis, True)]
    unnamed x101 -> x26, local copies, waits for them, and re-layouts: 11.4 us -> 3.05 us
    reshape x0 -> x5, local copies, waits for them, and re-layouts: none -> 6.87 us  [the longest x3 4.57 us: folded(): return jnp.transpose(w, (0, 4, 1, 2, 3, 5)).reshape(4 * o, 18 * c)]
  transfers between devices with their start and end apart: 18 -> 7, of which waited for: 7 -> 4; matrix products, arithmetic and copies ran while one was open for 23% -> 23% of each run, Pallas kernels for 0% -> 0%
where the time goes in v1:
time: 62.1 us; the launch traced here: 61.8 us
  local copies, waits for them, and re-layouts  20.3 us (33%)
  Pallas kernels  17.1 us (28%)
  waiting for transfers between devices  12.8 us (21%)
  starting transfers between devices  8.32 us (13%)
  other arithmetic  3.03 us (5%)
    pallas_call x1, Pallas kernels, layers(): pl.pallas_call(layers_kernel, out_shape=jax.ShapeDtypeStruct((nx, ny, pai...  17.1 us
    ppermute x7, waiting for transfers between devices, shift(): return lax.ppermute(x, axis, pairs)  12.8 us
    ppermute x7, starting transfers between devices, shift(): return lax.ppermute(x, axis, pairs)  8.32 us
    reshape x3, local copies, waits for them, and re-layouts, folded(): return jnp.transpose(w, (0, 4, 1, 2, 3, 5)).reshape(4 * o, 18 * c)  4.57 us
    transpose x3, local copies, waits for them, and re-layouts, folded(): return jnp.transpose(w, (0, 4, 1, 2, 3, 5)).reshape(4 * o, 18 * c)  3.65 us
    unnamed x26, local copies, waits for them, and re-layouts  3.05 us
    reshape x1, local copies, waits for them, and re-layouts, shards(): out = out.reshape(nx, ny, nz, c)  1.64 us
    broadcast_in_dim x1, local copies, waits for them, and re-layouts, shards(): return jnp.transpose(out, (3, 0, 1, 2))[None]  1.63 us
  transfers between devices with their start and end apart: 7, of which 4 were waited for; matrix products, arithmetic and copies ran while one was open for 23% of the time, Pallas kernels for 0%

profile of v1, /device:TPU:0, one launch (start us, length us, event | category | flops | bytes accessed | tf_op | source)
XLA Modules:
  0.0 61.8 jit_solution(1026314311528316077)
XLA Ops:
  0.0 2.1 %copy.18 = bf16[1,64,4,8,128]{1,3,4,2,0:T(8,128)(2,1)S(1)} copy(bf16[1,64,4,8,128]{4,3,2,1,0:T(8,128)(2,1)} %param.7) | data formatting | bytes 1048576 | tf_op args[0]
  2.1 0.0 copy-start.1
  2.1 0.6 %pad_maximum_fusion.1 = bf16[4,8,6,64]{3,1,2,0:T(8,128)(2,1)} fusion(bf16[4,8,3,64]{3,1,2,0:T(8,128)(2,1)S(1)} %get-tuple-element.6, bf16[4,8,3,64]{3,1,2,0:T(8,128)(2,1)S(1)} %get-tuple-element.5), kind=kLoop, calls=%fused_computation.16 | loop fusion | flops 12288 | bytes 49152 | tf_op jit(solution)/shard_map/concatenate | solution.py:110
  2.8 3.0 %collective-permute-start = (bf16[4,8,6,64]{3,1,2,0:T(8,128)(2,1)}, bf16[4,8,6,64]{3,1,2,0:T(8,128)(2,1)}, u32[]{:S(2)}, u32[]{:S(2)}) collective-permute-start(bf16[4,8,6,64]{3,1,2,0:T(8,128)(2,1)} %pad_maximum_fusion.1), channel_id=1, source_target_pairs={{0,1},{1,0},{2,3},{3,2},{4,5},{5,4},{6,7},{7,6},{8,9},{9,8},{10,11... | collective-permute-start | bytes 73736 | tf_op jit(solution)/shard_map/ppermute | solution.py:105
  5.8 0.1 slice_bitcast_fusion.5
  5.9 0.0 copy-start.2
  6.0 0.1 slice_bitcast_fusion.3
  6.1 0.9 %copy-done.2 = bf16[3,3,3,64,64]{4,3,2,1,0:T(8,128)(2,1)S(1)} copy-done((bf16[3,3,3,64,64]{4,3,2,1,0:T(8,128)(2,1)S(1)}, bf16[3,3,3,64,64]{4,3,2,1,0:T(8,128)(2,1)}, u32[]{:S(2)}) %copy-start.2) | copy-done | bytes 221208
  6.9 0.7 %fusion.1 = (bf16[3,3,1,64,64]{4,3,2,1,0:T(8,128)(2,1)S(1)}, bf16[3,3,1,64,64]{4,3,2,1,0:T(8,128)(2,1)}) fusion(bf16[3,3,3,64,64]{4,3,2,1,0:T(8,128)(2,1)S(1)} %copy-done.2), kind=kLoop, calls=%fused_computation.27 | loop fusion | bytes 294912 | tf_op jit(solution)/shard_map/slice | solution.py:94
  7.6 0.9 %slice_bitcast_fusion.1 = (bf16[1,3,3,2,64,64]{5,4,3,2,1,0:T(8,128)(2,1)}, bf16[1,3,3,2,64,64]{5,4,3,2,1,0:T(8,128)(2,1)}) fusion(bf16[3,3,3,64,64]{4,3,2,1,0:T(8,128)(2,1)S(1)} %copy-done.2), kind=kLoop, calls=%fused_computation.7 | loop fusion | bytes 589824 | tf_op jit(solution)/shard_map/stack | solution.py:97
  8.5 0.1 pad_bitcast_fusion.4
  8.6 0.1 pad_bitcast_fusion.2
  8.8 0.3 maximum_bitcast_fusion
  9.1 0.3 maximum_bitcast_fusion.1
  9.4 1.2 %copy.20 = bf16[4,64,3,3,2,64]{5,4,3,2,1,0:T(2,128)(2,1)S(1)} copy(bf16[4,64,3,3,2,64]{5,1,4,3,2,0:T(8,128)(2,1)S(1)} %maximum_bitcast_fusion) | data formatting | bytes 1179648 | tf_op jit(solution)/shard_map/transpose | solution.py:99
  10.6 1.5 %reshape.16.w1 = bf16[256,1152]{1,0:T(8,128)(2,1)} reshape(bf16[4,64,3,3,2,64]{5,4,3,2,1,0:T(2,128)(2,1)S(1)} %copy.20) | data formatting | bytes 1179648 | tf_op jit(solution)/shard_map/reshape | solution.py:99
  12.1 1.2 %copy.21 = bf16[4,64,3,3,2,64]{5,4,3,2,1,0:T(2,128)(2,1)S(1)} copy(bf16[4,64,3,3,2,64]{5,1,4,3,2,0:T(8,128)(2,1)S(1)} %maximum_bitcast_fusion.1) | data formatting | bytes 1179648 | tf_op jit(solution)/shard_map/transpose | solution.py:99
  13.4 1.5 %reshape.17.w2 = bf16[256,1152]{1,0:T(8,128)(2,1)} reshape(bf16[4,64,3,3,2,64]{5,4,3,2,1,0:T(2,128)(2,1)S(1)} %copy.21) | data formatting | bytes 1179648 | tf_op jit(solution)/shard_map/reshape | solution.py:99
  14.9 0.8 %fusion.5 = (bf16[4,8,3,64]{3,1,2,0:T(8,128)(2,1)S(1)}, bf16[4,8,3,64]{3,1,2,0:T(8,128)(2,1)S(1)}) fusion(bf16[4,8,6,64]{3,1,2,0:T(8,128)(2,1)} %collective-permute-done), kind=kLoop, calls=%fused_computation.31 | loop fusion | bytes 49152 | tf_op jit(solution)/shard_map/split | solution.py:111
  15.7 0.3 pad_maximum_fusion
  15.9 0.2 copy.19
  16.1 0.0 copy-start.7
  16.1 0.7 %reshape.15 = bf16[4,8,67,128]{3,2,1,0:T(8,128)(2,1)S(1)} reshape(bf16[4,8,134,64]{3,2,1,0:T(8,128)(2,1)S(1)} %copy.19) | data formatting | bytes 1097728 | tf_op jit(solution)/shard_map/reshape | solution.py:125
  16.8 1.6 %collective-permute-start.3 = (bf16[4,3,72,128]{3,2,1,0:T(8,128)(2,1)S(1)}, bf16[4,3,72,128]{3,2,1,0:T(8,128)(2,1)S(1)}, u32[]{:S(2)}, u32[]{:S(2)}) collective-permute-start(bf16[4,3,72,128]{3,2,1,0:T(8,128)(2,1)S(1)} %get-tuple-element.8), channel_id=1, source_target_pairs={{0,2},{2,4},{4,6},{6,0},{1,3},{3,5},{5,7},{7,1},{8,10},{10,12},{12... | collective-permute-start | bytes 663560 | tf_op jit(solution)/shard_map/ppermute | solution.py:105
  18.4 0.1 pad_bitcast_fusion
  18.6 2.3 %collective-permute-start.4 = (bf16[4,3,72,128]{3,2,1,0:T(8,128)(2,1)S(1)}, bf16[4,3,72,128]{3,2,1,0:T(8,128)(2,1)S(1)}, u32[]{:S(2)}, u32[]{:S(2)}) collective-permute-start(bf16[4,3,72,128]{3,2,1,0:T(8,128)(2,1)S(1)} %get-tuple-element.7), channel_id=1, source_target_pairs={{2,0},{4,2},{6,4},{0,6},{3,1},{5,3},{7,5},{1,7},{10,8},{12,10},{14... | collective-permute-start | bytes 663560 | tf_op jit(solution)/shard_map/ppermute | solution.py:105
  20.9 0.1 pad_slice_fusion.2
  21.0 0.3 collective-permute-start.2
  21.3 0.2 collective-permute-start.1
  21.5 5.5 %collective-permute-done.3.ym = bf16[4,3,72,128]{3,2,1,0:T(8,128)(2,1)S(1)} collective-permute-done((bf16[4,3,72,128]{3,2,1,0:T(8,128)(2,1)S(1)}, bf16[4,3,72,128]{3,2,1,0:T(8,128)(2,1)S(1)}, u32[]{:S(2)}, u32[]{:S(2)}) %collective-permute-start.3) | collective-permute-done | bytes 221216 | tf_op jit(solution)/shard_map/ppermute | solution.py:105
  27.0 2.9 %collective-permute-done.4.yp = bf16[4,3,72,128]{3,2,1,0:T(8,128)(2,1)S(1)} collective-permute-done((bf16[4,3,72,128]{3,2,1,0:T(8,128)(2,1)S(1)}, bf16[4,3,72,128]{3,2,1,0:T(8,128)(2,1)S(1)}, u32[]{:S(2)}, u32[]{:S(2)}) %collective-permute-start.4) | collective-permute-done | bytes 221216 | tf_op jit(solution)/shard_map/ppermute | solution.py:105
  30.0 1.0 %fusion.4 = (bf16[3,6,72,128]{3,2,1,0:T(8,128)(2,1)}, bf16[3,6,72,128]{3,2,1,0:T(8,128)(2,1)}) fusion(bf16[4,6,72,128]{3,2,1,0:T(8,128)(2,1)S(1)} %constant_dynamic-update-slice_fusion), kind=kLoop, calls=%fused_computation.30 | loop fusion | bytes 1327104 | tf_op jit(solution)/shard_map/slice | solution.py:130
  31.0 0.8 %collective-permute-start.6 = (bf16[3,6,72,128]{3,2,1,0:T(8,128)(2,1)}, bf16[3,6,72,128]{3,2,1,0:T(8,128)(2,1)}, u32[]{:S(2)}, u32[]{:S(2)}) collective-permute-start(bf16[3,6,72,128]{3,2,1,0:T(8,128)(2,1)} %get-tuple-element.23), channel_id=1, source_target_pairs={{8,0},{16,8},{24,16},{0,24},{9,1},{17,9},{25,17},{1,25},{10,2},{18... | collective-permute-start | bytes 995336 | tf_op jit(solution)/shard_map/ppermute | solution.py:105
  31.8 0.0 collective-permute-start.5
  31.8 0.3 maximum_bitcast_fusion.2
  32.1 1.2 %copy.22 = bf16[4,64,3,3,2,64]{5,4,3,2,1,0:T(2,128)(2,1)S(1)} copy(bf16[4,64,3,3,2,64]{5,1,4,3,2,0:T(8,128)(2,1)S(1)} %maximum_bitcast_fusion.2) | data formatting | bytes 1179648 | tf_op jit(solution)/shard_map/transpose | solution.py:99
  33.4 0.0 copy-start.11
  33.4 0.0 copy-start.9
  33.4 0.0 copy-start.10
  33.4 1.5 %reshape.18.w3 = bf16[256,1152]{1,0:T(8,128)(2,1)} reshape(bf16[4,64,3,3,2,64]{5,4,3,2,1,0:T(2,128)(2,1)S(1)} %copy.22) | data formatting | bytes 1179648 | tf_op jit(solution)/shard_map/reshape | solution.py:99
  34.9 0.6 maximum_bitcast_fusion.5.b3
  35.5 0.6 maximum_bitcast_fusion.3
  36.2 0.9 %pad.10.own = bf16[4,8,72,128]{3,2,1,0:T(8,128)(2,1)} pad(bf16[4,8,67,128]{3,2,1,0:T(8,128)(2,1)S(1)} %reshape.15, bf16[]{:T(256)} %constant.1.clone.1), padding=0_0x0_0x0_5x0_0 | pad | bytes 1138690 | tf_op jit(solution)/shard_map/jit(_pad)/pad | solution.py:126
  37.0 3.2 %collective-permute-done.6.cp = bf16[3,6,72,128]{3,2,1,0:T(8,128)(2,1)} collective-permute-done((bf16[3,6,72,128]{3,2,1,0:T(8,128)(2,1)}, bf16[3,6,72,128]{3,2,1,0:T(8,128)(2,1)}, u32[]{:S(2)}, u32[]{:S(2)}) %collective-permute-start.6) | collective-permute-done | bytes 331808 | tf_op jit(solution)/shard_map/ppermute | solution.py:105
  40.2 1.2 %collective-permute-done.5.cm = bf16[3,6,72,128]{3,2,1,0:T(8,128)(2,1)} collective-permute-done((bf16[3,6,72,128]{3,2,1,0:T(8,128)(2,1)}, bf16[3,6,72,128]{3,2,1,0:T(8,128)(2,1)}, u32[]{:S(2)}, u32[]{:S(2)}) %collective-permute-start.5) | collective-permute-done | bytes 331808 | tf_op jit(solution)/shard_map/ppermute | solution.py:105
  41.4 17.1 %shard_map.73 = bf16[4,8,64,128]{3,2,1,0:T(8,128)(2,1)} custom-call(bf16[4,8,72,128]{3,2,1,0:T(8,128)(2,1)} %pad.10.own, bf16[3,8,72,128]{3,2,1,0:T(8,128)(2,1)} %collective-permute-done.1.xm, bf16[3,8,72,128]{3,2,1,0:T(8,128)(2,1)} %copy-done.8, bf16[4,3,72,128]{3,2,1,0:T(8,128)(2,1)} %copy-done.5, bf16[4,3,72,128]{3,2,1,0:T(8,128)(2,1)} %copy-done.6, ...), custom_call_target="tpu_custom_call" | custom-call | tf_op jit(solution)/shard_map/pallas_call | solution.py:73
  58.5 1.6 %reshape.19 = bf16[4,8,128,64]{3,2,1,0:T(8,128)(2,1)S(1)} reshape(bf16[4,8,64,128]{3,2,1,0:T(8,128)(2,1)} %shard_map.73) | data formatting | bytes 1048576 | tf_op jit(solution)/shard_map/reshape | solution.py:132
  60.2 1.6 %copy.23 = bf16[1,64,4,8,128]{4,3,2,1,0:T(8,128)(2,1)} copy(bf16[1,64,4,8,128]{1,4,3,2,0:T(8,128)(2,1)S(1)} %bitcast.46) | data formatting | bytes 1048576 | tf_op jit(solution)/shard_map/broadcast_in_dim | solution.py:133
  (26 shorter events, 0.2 us)
Async XLA Ops:
  0.0 5.8 %copy-start = (bf16[3,3,3,64,64]{4,3,2,1,0:T(8,128)(2,1)S(1)}, bf16[3,3,3,64,64]{4,3,2,1,0:T(8,128)(2,1)}, u32[]{:S(2)}) copy-start(bf16[3,3,3,64,64]{4,3,2,1,0:T(8,128)(2,1)} %param.8) | copy-start | bytes 663556
  2.1 3.8 %copy-start.1 = (bf16[3,3,3,64,64]{4,3,2,1,0:T(8,128)(2,1)S(1)}, bf16[3,3,3,64,64]{4,3,2,1,0:T(8,128)(2,1)}, u32[]{:S(2)}) copy-start(bf16[3,3,3,64,64]{4,3,2,1,0:T(8,128)(2,1)} %param.10) | copy-start | bytes 663556
  2.8 12.1 %collective-permute-start = (bf16[4,8,6,64]{3,1,2,0:T(8,128)(2,1)}, bf16[4,8,6,64]{3,1,2,0:T(8,128)(2,1)}, u32[]{:S(2)}, u32[]{:S(2)}) collective-permute-start(bf16[4,8,6,64]{3,1,2,0:T(8,128)(2,1)} %pad_maximum_fusion.1), channel_id=1, source_target_pairs={{0,1},{1,0},{2,3},{3,2},{4,5},{5,4},{6,7},{7,6},{8,9},{9,8},{10,11... | collective-permute-start | bytes 73736 | tf_op jit(solution)/shard_map/ppermute | solution.py:105
  5.9 1.0 %copy-start.2 = (bf16[3,3,3,64,64]{4,3,2,1,0:T(8,128)(2,1)S(1)}, bf16[3,3,3,64,64]{4,3,2,1,0:T(8,128)(2,1)}, u32[]{:S(2)}) copy-start(bf16[3,3,3,64,64]{4,3,2,1,0:T(8,128)(2,1)} %param.12) | copy-start | bytes 663556
  16.1 2.4 %copy-start.7 = (bf16[3,3,1,64,64]{4,3,2,1,0:T(8,128)(2,1)S(1)}, bf16[3,3,1,64,64]{4,3,2,1,0:T(8,128)(2,1)}, u32[]{:S(2)}) copy-start(bf16[3,3,1,64,64]{4,3,2,1,0:T(8,128)(2,1)} %get-tuple-element.14) | copy-start | bytes 221188
  16.8 10.2 %collective-permute-start.3 = (bf16[4,3,72,128]{3,2,1,0:T(8,128)(2,1)S(1)}, bf16[4,3,72,128]{3,2,1,0:T(8,128)(2,1)S(1)}, u32[]{:S(2)}, u32[]{:S(2)}) collective-permute-start(bf16[4,3,72,128]{3,2,1,0:T(8,128)(2,1)S(1)} %get-tuple-element.8), channel_id=1, source_target_pairs={{0,2},{2,4},{4,6},{6,0},{1,3},{3,5},{5,7},{7,1},{8,10},{10,12},{12... | collective-permute-start | bytes 663560 | tf_op jit(solution)/shard_map/ppermute | solution.py:105
  18.6 11.4 %collective-permute-start.4 = (bf16[4,3,72,128]{3,2,1,0:T(8,128)(2,1)S(1)}, bf16[4,3,72,128]{3,2,1,0:T(8,128)(2,1)S(1)}, u32[]{:S(2)}, u32[]{:S(2)}) collective-permute-start(bf16[4,3,72,128]{3,2,1,0:T(8,128)(2,1)S(1)} %get-tuple-element.7), channel_id=1, source_target_pairs={{2,0},{4,2},{6,4},{0,6},{3,1},{5,3},{7,5},{1,7},{10,8},{12,10},{14... | collective-permute-start | bytes 663560 | tf_op jit(solution)/shard_map/ppermute | solution.py:105
  21.0 10.8 %copy-start.3 = (bf16[1,3,3,2,64,64]{5,4,3,2,1,0:T(8,128)(2,1)S(1)}, bf16[1,3,3,2,64,64]{5,4,3,2,1,0:T(8,128)(2,1)}, u32[]{:S(2)}) copy-start(bf16[1,3,3,2,64,64]{5,4,3,2,1,0:T(8,128)(2,1)} %get-tuple-element.11) | copy-start | bytes 442372
  21.0 10.8 %copy-start.4 = (bf16[1,3,3,2,64,64]{5,4,3,2,1,0:T(8,128)(2,1)S(1)}, bf16[1,3,3,2,64,64]{5,4,3,2,1,0:T(8,128)(2,1)}, u32[]{:S(2)}) copy-start(bf16[1,3,3,2,64,64]{5,4,3,2,1,0:T(8,128)(2,1)} %get-tuple-element.12) | copy-start | bytes 442372
  21.0 16.1 %collective-permute-start.2 = (bf16[3,8,72,128]{3,2,1,0:T(8,128)(2,1)S(1)}, bf16[3,8,72,128]{3,2,1,0:T(8,128)(2,1)S(1)}, u32[]{:S(2)}, u32[]{:S(2)}) collective-permute-start(bf16[3,8,72,128]{3,2,1,0:T(8,128)(2,1)S(1)} %get-tuple-element.9), channel_id=1, source_target_pairs={{8,0},{16,8},{24,16},{0,24},{9,1},{17,9},{25,17},{1,25},{10,2},{18... | collective-permute-start | bytes 1327112 | tf_op jit(solution)/shard_map/ppermute | solution.py:105
  21.3 15.7 %collective-permute-start.1 = (bf16[3,8,72,128]{3,2,1,0:T(8,128)(2,1)S(1)}, bf16[3,8,72,128]{3,2,1,0:T(8,128)(2,1)}, u32[]{:S(2)}, u32[]{:S(2)}) collective-permute-start(bf16[3,8,72,128]{3,2,1,0:T(8,128)(2,1)S(1)} %get-tuple-element.10), channel_id=1, source_target_pairs={{0,8},{8,16},{16,24},{24,0},{1,9},{9,17},{17,25},{25,1},{2,10},{10... | collective-permute-start | bytes 1327112 | tf_op jit(solution)/shard_map/ppermute | solution.py:105
  27.0 5.1 %copy-start.5 = (bf16[4,3,72,128]{3,2,1,0:T(8,128)(2,1)}, bf16[4,3,72,128]{3,2,1,0:T(8,128)(2,1)S(1)}, u32[]{:S(2)}) copy-start(bf16[4,3,72,128]{3,2,1,0:T(8,128)(2,1)S(1)} %collective-permute-done.3.ym) | copy-start | bytes 663556
  30.0 2.2 %copy-start.6 = (bf16[4,3,72,128]{3,2,1,0:T(8,128)(2,1)}, bf16[4,3,72,128]{3,2,1,0:T(8,128)(2,1)S(1)}, u32[]{:S(2)}) copy-start(bf16[4,3,72,128]{3,2,1,0:T(8,128)(2,1)S(1)} %collective-permute-done.4.yp) | copy-start | bytes 663556
  31.0 9.3 %collective-permute-start.6 = (bf16[3,6,72,128]{3,2,1,0:T(8,128)(2,1)}, bf16[3,6,72,128]{3,2,1,0:T(8,128)(2,1)}, u32[]{:S(2)}, u32[]{:S(2)}) collective-permute-start(bf16[3,6,72,128]{3,2,1,0:T(8,128)(2,1)} %get-tuple-element.23), channel_id=1, source_target_pairs={{8,0},{16,8},{24,16},{0,24},{9,1},{17,9},{25,17},{1,25},{10,2},{18... | collective-permute-start | bytes 995336 | tf_op jit(solution)/shard_map/ppermute | solution.py:105
  31.8 9.6 %collective-permute-start.5 = (bf16[3,6,72,128]{3,2,1,0:T(8,128)(2,1)}, bf16[3,6,72,128]{3,2,1,0:T(8,128)(2,1)}, u32[]{:S(2)}, u32[]{:S(2)}) collective-permute-start(bf16[3,6,72,128]{3,2,1,0:T(8,128)(2,1)} %get-tuple-element.24), channel_id=1, source_target_pairs={{0,8},{8,16},{16,24},{24,0},{1,9},{9,17},{17,25},{25,1},{2,10},{10... | collective-permute-start | bytes 995336 | tf_op jit(solution)/shard_map/ppermute | solution.py:105
  33.4 1.6 %copy-start.11 = (f32[64]{0:T(128)S(1)}, f32[64]{0:T(128)}, u32[]{:S(2)}) copy-start(f32[64]{0:T(128)} %param.13) | copy-start | bytes 772
  33.4 2.2 %copy-start.9 = (f32[64]{0:T(128)S(1)}, f32[64]{0:T(128)}, u32[]{:S(2)}) copy-start(f32[64]{0:T(128)} %param.9) | copy-start | bytes 772
  33.4 2.1 %copy-start.10 = (f32[64]{0:T(128)S(1)}, f32[64]{0:T(128)}, u32[]{:S(2)}) copy-start(f32[64]{0:T(128)} %param.11) | copy-start | bytes 772
  37.0 4.4 %copy-start.8 = (bf16[3,8,72,128]{3,2,1,0:T(8,128)(2,1)}, bf16[3,8,72,128]{3,2,1,0:T(8,128)(2,1)S(1)}, u32[]{:S(2)}) copy-start(bf16[3,8,72,128]{3,2,1,0:T(8,128)(2,1)S(1)} %collective-permute-done.2.xp) | copy-start | bytes 1327108

commit v2 on v0

v2 whole, which is shorter than its diff:
```python
import functools

import jax
import jax.numpy as jnp
from jax import lax
from jax.experimental import pallas as pl
from jax.experimental.pallas import tpu as pltpu
from jax.sharding import PartitionSpec as P

HALO = 3
SQRT_HALF = 0.7071067811865476
BF16 = jnp.bfloat16
F32 = jnp.float32
VMEM = pl.BlockSpec(memory_space=pltpu.VMEM)


def around(size, step):
    return -(-size // step) * step


def call(kernel, outs, scratch=(), name=None, flops=0, nbytes=0):
    outs = [jax.ShapeDtypeStruct(s, d) for s, d in outs]

    def run(*args):
        return pl.pallas_call(
            kernel,
            out_shape=outs,
            in_specs=[VMEM] * len(args),
            out_specs=[VMEM] * len(outs),
            scratch_shapes=list(scratch),
            name=name,
            cost_estimate=pl.CostEstimate(
                flops=flops, bytes_accessed=nbytes, transcendentals=0
            ),
            compiler_params=pltpu.CompilerParams(vmem_limit_bytes=48 * 1024 * 1024),
        )(*args)

    return run


def gelu(u):
    return 0.5 * u * (1.0 + lax.erf(u * SQRT_HALF))


def iota(shape, dim):
    return lax.broadcasted_iota(jnp.int32, shape, dim)


def rows_kernel(field, pairs, edges, planes):
    c, nx, ny, nz = field.shape
    rows = pairs.shape[2]
    m = iota((rows + 8, 2 * nz), 0)
    j = iota((rows + 8, 2 * nz), 1)
    half = nz // 2
    first = jnp.where(m < rows + 2, m - rows + half, m - rows - 1)
    m = jnp.where(m < rows, m, jnp.where(m < rows + 4, first, -8))
    second = (j >= nz).astype(jnp.int32)
    pick = (j - nz * second == 2 * m - 3 + second).astype(F32).astype(BF16)
    blank = jnp.zeros((c, nz), BF16)
    for x in range(nx):
        planes[x] = field[:, x].astype(F32).reshape(c * ny, nz)
        for y in range(0, ny, 2):
            blocks = []
            for k in range(2):
                b = planes[x, pl.ds(y + k, c, stride=ny), :].astype(BF16)
                blocks.append(jnp.concatenate([b, blank], axis=1))
                blocks.append(jnp.concatenate([blank, b], axis=1))
            r = lax.dot_general(
                pick,
                jnp.concatenate(blocks, axis=0),
                (((1,), (1,)), ((), ())),
                preferred_element_type=F32,
            ).astype(BF16)
            for k in range(2):
                lanes = slice(2 * c * k, 2 * c * (k + 1))
                pairs[x, y + k] = r[:rows, lanes]
                edges[x, y + k] = r[rows : rows + 4, lanes]


def faces_kernel(pairs, edges, own, xu, xd, yu, yd, wide):
    nx, ny, rows, _ = pairs.shape
    h = HALO
    wide[:, :, :4] = edges[...].astype(F32)
    got = wide[...]
    row = iota(got.shape, 2)
    low = jnp.where(row < 2, got, 0.0)
    moved = pltpu.roll(got, got.shape[2] - 1, 2)
    high = jnp.where((row >= 1) & (row < 3), moved, 0.0)
    e = pairs[...].astype(F32)
    e = jnp.concatenate(
        [e[:, :, :8] + low, e[:, :, 8 : rows - 8], e[:, :, rows - 8 :] + high], axis=2
    ).astype(BF16)
    own[...] = e
    xu[...] = e[nx - h :]
    xd[...] = e[:h]
    yu[...] = e[:, ny - h :]
    yd[...] = e[:, :h]


def weights_kernel(k1, k2, k3, b1, b2, b3, w1, w2, w3, bias):
    _, _, taps, o, c = k1.shape
    j = iota((taps * o, 8 * o), 0)
    n = iota((taps * o, 8 * o), 1)
    p = n // (4 * o)
    t = n // (2 * o) % 2
    q = n // o % 2
    pick = (j == (p - q + 2 * t) * o + n % o).astype(F32).astype(BF16)
    for k, w in ((k1, w1), (k2, w2), (k3, w3)):
        for a in range(3):
            for e in range(3):
                r = lax.dot_general(
                    k[a, e].reshape(taps * o, c),
                    pick,
                    (((0,), (0,)), ((), ())),
                    preferred_element_type=F32,
                ).astype(BF16)
                at = (a * 3 + e) * 2 * c
                w[at : at + c] = r[:, : 4 * o]
                w[at + c : at + 2 * c] = r[:, 4 * o :]
    for i, b in enumerate((b1, b2, b3)):
        bias[i : i + 1] = jnp.concatenate([b[...], b[...]], axis=1)


def conv(source, planes, starts, lines, weight, bias):
    rows = source.shape[2]
    height = lines * rows
    columns = []
    for a in range(3):
        for e in range(3):
            columns.append(
                jnp.concatenate(
                    [
                        source[x + a, s + e : s + e + lines].reshape(height, 128)
                        for x in planes
                        for s in starts
                    ],
                    axis=0,
                )
            )
    both = jnp.dot(
        jnp.concatenate(columns, axis=1), weight, preferred_element_type=F32
    )
    total = both.shape[0]
    u = both[:, :128] + pltpu.roll(both[:, 128:], total - 1, 0) + bias
    y = gelu(u).astype(BF16)
    return y.reshape(len(planes), len(starts) * lines, rows, 128)


def groups(count, size):
    return [list(range(i, min(i + size, count))) for i in range(0, count, size)]


def middle_kernel(own, xm, xp, w1, w2, w3, bias, l1, l2, l3, s0, s1):
    nx, ny, rows, _ = own.shape
    h = HALO
    s0[:h, :, :rows] = xm[...]
    s0[h : h + nx, :, :rows] = own[...]
    s0[h + nx :, :, :rows] = xp[...]
    for g in groups(nx + 4, 2):
        y = conv(s0, g, [0], ny - 2, w1[...], bias[0:1])
        for i, x in enumerate(g):
            s1[x] = y[i]
            l1[x, :2] = y[i, :2]
            l1[x, 2:] = y[i, ny - 4 :]
    for g in groups(nx + 2, 3):
        y = conv(s1, g, [0], ny - 4, w2[...], bias[1:2])
        for i, x in enumerate(g):
            l2[x] = y[i]
    for g in groups(nx, 4):
        y = conv(l2, g, [0], ny - 6, w3[...], bias[2:3])
        for i, x in enumerate(g):
            l3[x] = y[i, :, : l3.shape[2]]


def outer_kernel(
    own, xm, xp, ym, yp, cmm, cpm, cmp, cpp, l1, l2, l3, w1, w2, w3, bias,
    out, s0, s1, s2, stage,
):
    nx, ny, rows, _ = own.shape
    h = HALO
    for planes, below, core, above in (
        (slice(0, h), cmm, xm, cmp),
        (slice(h, h + nx), ym, own, yp),
        (slice(h + nx, h + nx + h), cpm, xp, cpp),
    ):
        s0[planes, :3, :rows] = below[...]
        s0[planes, 3:5, :rows] = core[:, :2]
        s0[planes, 5:7, :rows] = core[:, ny - 2 :]
        s0[planes, 7:, :rows] = above[...]
    s1[:, 3:7] = l1[...]
    inner = l2.shape[1]
    s2[:, 3:5] = l2[:, :2]
    s2[:, 5:7] = l2[:, inner - 2 :]
    for source, target, w, i in ((s0, s1, w1, 0), (s1, s2, w2, 1)):
        for g in groups(source.shape[0] - 2, 2):
            y = conv(source, g, [0, 5], 3, w[...], bias[i : i + 1])
            for k, x in enumerate(g):
                target[x, :3] = y[k, :3]
                target[x, 7:] = y[k, 3:]
    half = l3.shape[2]
    c = out.shape[0]
    nz = out.shape[3]
    deep, wide = 4 * half, 8 * nz
    r = iota((deep, wide), 0)
    n = iota((deep, wide), 1)
    side = n // (4 * nz)
    spread = (r // half == n // nz % 4) & (n % nz == 2 * (r % half) + side)
    spread = spread.astype(F32).astype(BF16)
    for g in groups(nx, 2):
        y = conv(s2, g, [0, 5], 3, w3[...], bias[2:3])
        for k, x in enumerate(g):
            lines = [y[k, i, :half] for i in range(3)]
            lines += [l3[x, i] for i in range(ny - 6)]
            lines += [y[k, i, :half] for i in range(3, 6)]
            for first in range(0, ny, 4):
                r = lax.dot_general(
                    jnp.concatenate(lines[first : first + 4], axis=0),
                    spread,
                    (((0,), (0,)), ((), ())),
                    preferred_element_type=F32,
                )
                r = r[:c, : 4 * nz] + r[c:, 4 * nz :]
                for i in range(4):
                    stage[x, pl.ds(first + i, c, stride=ny), :] = r[
                        :, i * nz : (i + 1) * nz
                    ]
            out[:, x] = stage[x].reshape(c, ny, nz).astype(BF16)


def shift(x, axis, up):
    count = lax.axis_size(axis)
    pairs = [(i, (i + 1) % count) if up else ((i + 1) % count, i) for i in range(count)]
    return lax.ppermute(x, axis, pairs)


def shards(field, kernel_one, bias_one, kernel_two, bias_two, kernel_three, bias_three):
    h = HALO
    field = field[0]
    c, nx, ny, nz = field.shape
    rows = around((nz + 2 * h) // 2, 8)
    pad = around(rows, 16)
    half = nz // 2
    line = 2 * c

    pairs, edges = call(
        rows_kernel,
        [((nx, ny, rows, line), BF16), ((nx, ny, 4, line), BF16)],
        [pltpu.VMEM((nx, c * ny, nz), F32)],
        name="rows",
    )(field)
    if lax.axis_size("gz") == 2:
        edges = shift(edges, "gz", True)
    else:
        edges = jnp.concatenate(
            [shift(edges[:, :, :2], "gz", True), shift(edges[:, :, 2:], "gz", False)],
            axis=2,
        )
    xface = ((h, ny, rows, line), BF16)
    yface = ((nx, h, rows, line), BF16)
    own, xu, xd, yu, yd = call(
        faces_kernel,
        [((nx, ny, rows, line), BF16), xface, xface, yface, yface],
        [pltpu.VMEM((nx, ny, 8, line), F32)],
        name="faces",
    )(pairs, edges)
    xm, xp = shift(xu, "gx", True), shift(xd, "gx", False)
    ym, yp = shift(yu, "gy", True), shift(yd, "gy", False)
    cmm, cpm = shift(ym[nx - h :], "gx", True), shift(ym[:h], "gx", False)
    cmp, cpp = shift(yp[nx - h :], "gx", True), shift(yp[:h], "gx", False)
    w1, w2, w3, bias = call(
        weights_kernel,
        [((18 * c, 4 * c), BF16)] * 3 + [((3, line), F32)],
        name="weights",
        flops=2 * 10**9,
        nbytes=10**6,
    )(
        kernel_one, kernel_two, kernel_three,
        bias_one[None], bias_two[None], bias_three[None],
    )
    ws = (w1, w2, w3, bias)
    l1, l2, l3 = call(
        middle_kernel,
        [
            ((nx + 4, 4, pad, line), BF16),
            ((nx + 2, ny - 4, pad, line), BF16),
            ((nx, ny - 6, half, line), BF16),
        ],
        [
            pltpu.VMEM((nx + 6, ny, pad, line), BF16),
            pltpu.VMEM((nx + 4, ny - 2, pad, line), BF16),
        ],
        name="middle",
        flops=6 * 10**9,
        nbytes=10**6,
    )(own, xm, xp, *ws)
    (out,) = call(
        outer_kernel,
        [((c, nx, ny, nz), BF16)],
        [
            pltpu.VMEM((nx + 6, 10, pad, line), BF16),
            pltpu.VMEM((nx + 4, 10, pad, line), BF16),
            pltpu.VMEM((nx + 2, 10, pad, line), BF16),
            pltpu.VMEM((nx, c * ny, nz), F32),
        ],
        name="outer",
        flops=8 * 10**9,
        nbytes=10**6,
    )(own, xm, xp, ym, yp, cmm, cpm, cmp, cpp, l1, l2, l3, *ws)
    return out[None]


def solution(mesh):
    return jax.shard_map(
        shards,
        mesh=mesh,
        in_specs=(P(None, None, "gx", "gy", "gz"), P(), P(), P(), P(), P(), P()),
        out_specs=P(None, None, "gx", "gy", "gz"),
        check_vma=False,
    )
```

time: 122 us -> 42 us (0.34)
  local copies, waits for them, and re-layouts: 53 us -> 2.81 us
  matrix products: 21.2 us -> 0 us
  Pallas kernels: 0 us -> 15.9 us
  starting transfers between devices: 24.4 us -> 9.77 us
  other arithmetic: 9.56 us -> 0 us
    dot_general x27 -> x0, matrix products: 21.2 us -> none  [conv_valid(): jnp.einsum('oc,bcxyz->boxyz', matrix, stacked, preferred_element_type=jnp...]
    slice x22 -> x2, local copies, waits for them, and re-layouts: 17.8 us -> 0.07 us  [the longest x1 0.04 us: shards(): cmp, cpp = (shift(yp[nx - h:], 'gx', True), shift(yp[:h], 'gx', False))]
    transpose x30 -> x0, local copies, waits for them, and re-layouts: 17.4 us -> none  [conv_valid(): jnp.transpose(kernel[along_x, along_y], (1, 0, 2))]
    pallas_call x0 -> x5, Pallas kernels: none -> 15.9 us  [run(): pl.pallas_call(kernel, out_shape=outs, in_specs=[VMEM] * len(args), out_s...]
    ppermute x18 -> x9, starting transfers between devices: 24.4 us -> 9.77 us  [shift(): return lax.ppermute(x, axis, pairs)]
    concatenate x9 -> x0, other arithmetic: 9.51 us -> none  [extended(): jnp.concatenate([lax.ppermute(tail, axis, [(i, (i + 1) % count) for i in...]
    unnamed x101 -> x14, local copies, waits for them, and re-layouts: 11.4 us -> 2.73 us
    ppermute x6 -> x0, local copies, waits for them, and re-layouts: 5.17 us -> none  [the longest x3 3.67 us: extended(): lax.ppermute(head, axis, [((i + 1) % count, i) for i in range(count)])]
  transfers between devices with their start and end apart: 18 -> 9, of which waited for: 7 -> 6; matrix products, arithmetic and copies ran while one was open for 23% -> 0% of each run, Pallas kernels for 0% -> 15%
where the time goes in v2:
time: 42 us; the launch traced here: 41.4 us
  Pallas kernels  15.9 us (38%)
  waiting for transfers between devices  12.8 us (30%)
  starting transfers between devices  9.77 us (23%)
  local copies, waits for them, and re-layouts  2.81 us (7%)
    pallas_call x5, Pallas kernels, run(): pl.pallas_call(kernel, out_shape=outs, in_specs=[VMEM] * len(args), out_s...  15.9 us
    ppermute x9, waiting for transfers between devices, shift(): return lax.ppermute(x, axis, pairs)  12.8 us
    ppermute x9, starting transfers between devices, shift(): return lax.ppermute(x, axis, pairs)  9.77 us
    unnamed x14, local copies, waits for them, and re-layouts  2.73 us
  transfers between devices with their start and end apart: 9, of which 6 were waited for; matrix products, arithmetic and copies ran while one was open for 0% of the time, Pallas kernels for 15%

profile of v2, /device:TPU:0, one launch (start us, length us, event | category | flops | bytes accessed | tf_op | source)
XLA Modules:
  0.0 41.4 jit_solution(15164349530872084134)
XLA Ops:
  0.0 0.0 copy-start
  0.0 1.0 %copy-done = bf16[1,64,4,8,128]{4,3,2,1,0:T(8,128)(2,1)S(1)} copy-done((bf16[1,64,4,8,128]{4,3,2,1,0:T(8,128)(2,1)S(1)}, bf16[1,64,4,8,128]{4,3,2,1,0:T(8,128)(2,1)}, u32[]{:S(2)}) %copy-start) | copy-done | bytes 524312
  1.0 0.0 copy-start.2
  1.0 0.8 %rows.1 = (bf16[4,8,72,128]{3,2,1,0:T(8,128)(2,1)S(1)}, bf16[4,8,4,128]{3,2,1,0:T(4,128)(2,1)S(1)}) custom-call(bf16[64,4,8,128]{3,2,1,0:T(8,128)(2,1)S(1)} %bitcast.5), custom_call_target="tpu_custom_call" | custom-call | tf_op jit(solution)/shard_map/rows/pallas_call | solution.py:25
  1.8 0.0 copy-start.1
  1.8 3.1 %collective-permute-start = (bf16[4,8,4,128]{3,2,1,0:T(4,128)(2,1)S(1)}, bf16[4,8,4,128]{3,2,1,0:T(4,128)(2,1)S(1)}, u32[]{:S(2)}, u32[]{:S(2)}) collective-permute-start(bf16[4,8,4,128]{3,2,1,0:T(4,128)(2,1)S(1)} %get-tuple-element.20), channel_id=1, source_target_pairs={{0,1},{1,0},{2,3},{3,2},{4,5},{5,4},{6,7},{7,6},{8,9},{9,8},{10,11... | collective-permute-start | bytes 98312 | tf_op jit(solution)/shard_map/ppermute | solution.py:233
  4.9 1.9 %collective-permute-done.edges = bf16[4,8,4,128]{3,2,1,0:T(4,128)(2,1)S(1)} collective-permute-done((bf16[4,8,4,128]{3,2,1,0:T(4,128)(2,1)S(1)}, bf16[4,8,4,128]{3,2,1,0:T(4,128)(2,1)S(1)}, u32[]{:S(2)}, u32[]{:S(2)}) %collective-permute-start) | collective-permute-done | bytes 32800 | tf_op jit(solution)/shard_map/ppermute | solution.py:233
  6.8 0.2 faces.1
  7.0 4.2 %collective-permute-start.4 = (bf16[4,3,72,128]{3,2,1,0:T(8,128)(2,1)S(1)}, bf16[4,3,72,128]{3,2,1,0:T(8,128)(2,1)S(1)}, u32[]{:S(2)}, u32[]{:S(2)}) collective-permute-start(bf16[4,3,72,128]{3,2,1,0:T(8,128)(2,1)S(1)} %get-tuple-element.25), channel_id=1, source_target_pairs={{2,0},{4,2},{6,4},{0,6},{3,1},{5,3},{7,5},{1,7},{10,8},{12,10},{14... | collective-permute-start | bytes 663560 | tf_op jit(solution)/shard_map/ppermute | solution.py:233
  11.2 0.0 copy-start.4
  11.2 0.0 copy-start.5
  11.2 0.0 copy-start.6
  11.2 0.0 copy-done.2
  11.2 0.0 copy-done.1
  11.2 0.6 %copy-done.4 = f32[64]{0:T(128)S(1)} copy-done((f32[64]{0:T(128)S(1)}, f32[64]{0:T(128)}, u32[]{:S(2)}) %copy-start.4) | copy-done | bytes 280
  11.9 0.0 copy-done.5
  11.9 0.0 copy-done.6
  11.9 0.0 copy-start.3
  11.9 1.0 %copy-done.3 = bf16[3,3,3,64,64]{4,3,2,1,0:T(8,128)(2,1)S(1)} copy-done((bf16[3,3,3,64,64]{4,3,2,1,0:T(8,128)(2,1)S(1)}, bf16[3,3,3,64,64]{4,3,2,1,0:T(8,128)(2,1)}, u32[]{:S(2)}) %copy-start.3) | copy-done | bytes 221208
  12.9 1.1 %weights.1 = (bf16[1152,256]{1,0:T(8,128)(2,1)S(1)}, bf16[1152,256]{1,0:T(8,128)(2,1)S(1)}, bf16[1152,256]{1,0:T(8,128)(2,1)S(1)}, f32[3,128]{1,0:T(4,128)S(1)}) custom-call(bf16[3,3,3,64,64]{4,3,2,1,0:T(8,128)(2,1)S(1)} %copy-done.1, bf16[3,3,3,64,64]{4,3,2,1,0:T(8,128)(2,1)S(1)} %copy-done.2, bf16[3,3,3,64,64]{4,3,2,1,0:T(8,128)(2,1)S(1)} %copy-done.3, ...), custom_call_target="tpu_custom_call" | custom-call | flops 2000000000 | bytes 1000000 | tf_op jit(solution)/shard_map/weights/pallas_call | solution.py:25
  14.1 0.1 collective-permute-start.3
  14.1 0.1 collective-permute-start.1
  14.2 1.7 %collective-permute-start.2 = (bf16[3,8,72,128]{3,2,1,0:T(8,128)(2,1)S(1)}, bf16[3,8,72,128]{3,2,1,0:T(8,128)(2,1)S(1)}, u32[]{:S(2)}, u32[]{:S(2)}) collective-permute-start(bf16[3,8,72,128]{3,2,1,0:T(8,128)(2,1)S(1)} %get-tuple-element.23), channel_id=1, source_target_pairs={{8,0},{16,8},{24,16},{0,24},{9,1},{17,9},{25,17},{1,25},{10,2},{18... | collective-permute-start | bytes 1327112 | tf_op jit(solution)/shard_map/ppermute | solution.py:233
  15.9 0.7 %collective-permute-done.4.yp = bf16[4,3,72,128]{3,2,1,0:T(8,128)(2,1)S(1)} collective-permute-done((bf16[4,3,72,128]{3,2,1,0:T(8,128)(2,1)S(1)}, bf16[4,3,72,128]{3,2,1,0:T(8,128)(2,1)S(1)}, u32[]{:S(2)}, u32[]{:S(2)}) %collective-permute-start.4) | collective-permute-done | bytes 221216 | tf_op jit(solution)/shard_map/ppermute | solution.py:233
  16.6 0.1 collective-permute-start.8
  16.7 0.5 %collective-permute-start.7 = (bf16[3,3,72,128]{3,2,1,0:T(8,128)(2,1)S(1)}, bf16[3,3,72,128]{3,2,1,0:T(8,128)(2,1)S(1)}, u32[]{:S(2)}, u32[]{:S(2)}) collective-permute-start(bf16[3,3,72,128]{3,2,1,0:T(8,128)(2,1)S(1)} %get-tuple-element.34), channel_id=1, source_target_pairs={{0,8},{8,16},{16,24},{24,0},{1,9},{9,17},{17,25},{25,1},{2,10},{10... | collective-permute-start | bytes 497672 | tf_op jit(solution)/shard_map/ppermute | solution.py:233
  17.2 4.6 %collective-permute-done.3.ym = bf16[4,3,72,128]{3,2,1,0:T(8,128)(2,1)S(1)} collective-permute-done((bf16[4,3,72,128]{3,2,1,0:T(8,128)(2,1)S(1)}, bf16[4,3,72,128]{3,2,1,0:T(8,128)(2,1)S(1)}, u32[]{:S(2)}, u32[]{:S(2)}) %collective-permute-start.3) | collective-permute-done | bytes 221216 | tf_op jit(solution)/shard_map/ppermute | solution.py:233
  21.9 0.1 collective-permute-start.6
  21.9 2.9 %collective-permute-done.1.xm = bf16[3,8,72,128]{3,2,1,0:T(8,128)(2,1)S(1)} collective-permute-done((bf16[3,8,72,128]{3,2,1,0:T(8,128)(2,1)S(1)}, bf16[3,8,72,128]{3,2,1,0:T(8,128)(2,1)S(1)}, u32[]{:S(2)}, u32[]{:S(2)}) %collective-permute-start.1) | collective-permute-done | bytes 442400 | tf_op jit(solution)/shard_map/ppermute | solution.py:233
  24.8 0.1 collective-permute-start.5
  24.9 1.5 %collective-permute-done.2.xp = bf16[3,8,72,128]{3,2,1,0:T(8,128)(2,1)S(1)} collective-permute-done((bf16[3,8,72,128]{3,2,1,0:T(8,128)(2,1)S(1)}, bf16[3,8,72,128]{3,2,1,0:T(8,128)(2,1)S(1)}, u32[]{:S(2)}, u32[]{:S(2)}) %collective-permute-start.2) | collective-permute-done | bytes 442400 | tf_op jit(solution)/shard_map/ppermute | solution.py:233
  26.5 5.1 %middle.1 = (bf16[8,4,80,128]{3,2,1,0:T(8,128)(2,1)S(1)}, bf16[6,4,80,128]{3,2,1,0:T(8,128)(2,1)S(1)}, bf16[4,2,64,128]{3,2,1,0:T(8,128)(2,1)S(1)}) custom-call(bf16[4,8,72,128]{3,2,1,0:T(8,128)(2,1)S(1)} %get-tuple-element.21.own, bf16[3,8,72,128]{3,2,1,0:T(8,128)(2,1)S(1)} %collective-permute-done.1.xm, ...), custom_call_target="tpu_custom_call" | custom-call | flops 6000000000 | bytes 1000000 | tf_op jit(solution)/shard_map/middle/pallas_call | solution.py:25
  31.6 0.0 collective-permute-done.8.cpp
  31.6 0.0 collective-permute-done.7.cmp
  31.6 1.1 %collective-permute-done.6.cpm = bf16[3,3,72,128]{3,2,1,0:T(8,128)(2,1)S(1)} collective-permute-done((bf16[3,3,72,128]{3,2,1,0:T(8,128)(2,1)S(1)}, bf16[3,3,72,128]{3,2,1,0:T(8,128)(2,1)S(1)}, u32[]{:S(2)}, u32[]{:S(2)}) %collective-permute-start.6) | collective-permute-done | bytes 165920 | tf_op jit(solution)/shard_map/ppermute | solution.py:233
  32.8 0.0 collective-permute-done.5.cmm
  32.8 8.6 %outer.1 = bf16[64,4,8,128]{3,2,1,0:T(8,128)(2,1)} custom-call(bf16[4,8,72,128]{3,2,1,0:T(8,128)(2,1)S(1)} %get-tuple-element.21.own, bf16[3,8,72,128]{3,2,1,0:T(8,128)(2,1)S(1)} %collective-permute-done.1.xm, bf16[3,8,72,128]{3,2,1,0:T(8,128)(2,1)S(1)} %collective-permute-done.2.xp, bf16[4,3,72,128]{3,2,1,0:T(8,128)(2,1)S(1)} %collective-permute-done.3.ym, ...), custom_call_target="tpu_custom_call" | custom-call | flops 8000000000 | bytes 1000000 | tf_op jit(solution)/shard_map/outer/pallas_call | solution.py:25
  (2 shorter events, 0.1 us)
Async XLA Ops:
  0.0 1.0 %copy-start = (bf16[1,64,4,8,128]{4,3,2,1,0:T(8,128)(2,1)S(1)}, bf16[1,64,4,8,128]{4,3,2,1,0:T(8,128)(2,1)}, u32[]{:S(2)}) copy-start(bf16[1,64,4,8,128]{4,3,2,1,0:T(8,128)(2,1)} %param.7) | copy-start | bytes 1572868
  1.0 10.2 %copy-start.2 = (bf16[3,3,3,64,64]{4,3,2,1,0:T(8,128)(2,1)S(1)}, bf16[3,3,3,64,64]{4,3,2,1,0:T(8,128)(2,1)}, u32[]{:S(2)}) copy-start(bf16[3,3,3,64,64]{4,3,2,1,0:T(8,128)(2,1)} %k2.1) | copy-start | bytes 663556
  1.8 9.4 %copy-start.1 = (bf16[3,3,3,64,64]{4,3,2,1,0:T(8,128)(2,1)S(1)}, bf16[3,3,3,64,64]{4,3,2,1,0:T(8,128)(2,1)}, u32[]{:S(2)}) copy-start(bf16[3,3,3,64,64]{4,3,2,1,0:T(8,128)(2,1)} %k1.1) | copy-start | bytes 663556
  1.8 5.0 %collective-permute-start = (bf16[4,8,4,128]{3,2,1,0:T(4,128)(2,1)S(1)}, bf16[4,8,4,128]{3,2,1,0:T(4,128)(2,1)S(1)}, u32[]{:S(2)}, u32[]{:S(2)}) collective-permute-start(bf16[4,8,4,128]{3,2,1,0:T(4,128)(2,1)S(1)} %get-tuple-element.20), channel_id=1, source_target_pairs={{0,1},{1,0},{2,3},{3,2},{4,5},{5,4},{6,7},{7,6},{8,9},{9,8},{10,11... | collective-permute-start | bytes 98312 | tf_op jit(solution)/shard_map/ppermute | solution.py:233
  7.0 9.6 %collective-permute-start.4 = (bf16[4,3,72,128]{3,2,1,0:T(8,128)(2,1)S(1)}, bf16[4,3,72,128]{3,2,1,0:T(8,128)(2,1)S(1)}, u32[]{:S(2)}, u32[]{:S(2)}) collective-permute-start(bf16[4,3,72,128]{3,2,1,0:T(8,128)(2,1)S(1)} %get-tuple-element.25), channel_id=1, source_target_pairs={{2,0},{4,2},{6,4},{0,6},{3,1},{5,3},{7,5},{1,7},{10,8},{12,10},{14... | collective-permute-start | bytes 663560 | tf_op jit(solution)/shard_map/ppermute | solution.py:233
  11.2 0.7 %copy-start.4 = (f32[64]{0:T(128)S(1)}, f32[64]{0:T(128)}, u32[]{:S(2)}) copy-start(f32[64]{0:T(128)} %param.9) | copy-start | bytes 772
  11.2 0.7 %copy-start.5 = (f32[64]{0:T(128)S(1)}, f32[64]{0:T(128)}, u32[]{:S(2)}) copy-start(f32[64]{0:T(128)} %param.11) | copy-start | bytes 772
  11.2 0.7 %copy-start.6 = (f32[64]{0:T(128)S(1)}, f32[64]{0:T(128)}, u32[]{:S(2)}) copy-start(f32[64]{0:T(128)} %param.13) | copy-start | bytes 772
  11.9 1.0 %copy-start.3 = (bf16[3,3,3,64,64]{4,3,2,1,0:T(8,128)(2,1)S(1)}, bf16[3,3,3,64,64]{4,3,2,1,0:T(8,128)(2,1)}, u32[]{:S(2)}) copy-start(bf16[3,3,3,64,64]{4,3,2,1,0:T(8,128)(2,1)} %k3.1) | copy-start | bytes 663556
  14.1 7.8 %collective-permute-start.3 = (bf16[4,3,72,128]{3,2,1,0:T(8,128)(2,1)S(1)}, bf16[4,3,72,128]{3,2,1,0:T(8,128)(2,1)S(1)}, u32[]{:S(2)}, u32[]{:S(2)}) collective-permute-start(bf16[4,3,72,128]{3,2,1,0:T(8,128)(2,1)S(1)} %get-tuple-element.24), channel_id=1, source_target_pairs={{0,2},{2,4},{4,6},{6,0},{1,3},{3,5},{5,7},{7,1},{8,10},{10,12},{12... | collective-permute-start | bytes 663560 | tf_op jit(solution)/shard_map/ppermute | solution.py:233
  14.1 10.7 %collective-permute-start.1 = (bf16[3,8,72,128]{3,2,1,0:T(8,128)(2,1)S(1)}, bf16[3,8,72,128]{3,2,1,0:T(8,128)(2,1)S(1)}, u32[]{:S(2)}, u32[]{:S(2)}) collective-permute-start(bf16[3,8,72,128]{3,2,1,0:T(8,128)(2,1)S(1)} %get-tuple-element.22), channel_id=1, source_target_pairs={{0,8},{8,16},{16,24},{24,0},{1,9},{9,17},{17,25},{25,1},{2,10},{10... | collective-permute-start | bytes 1327112 | tf_op jit(solution)/shard_map/ppermute | solution.py:233
  14.2 12.3 %collective-permute-start.2 = (bf16[3,8,72,128]{3,2,1,0:T(8,128)(2,1)S(1)}, bf16[3,8,72,128]{3,2,1,0:T(8,128)(2,1)S(1)}, u32[]{:S(2)}, u32[]{:S(2)}) collective-permute-start(bf16[3,8,72,128]{3,2,1,0:T(8,128)(2,1)S(1)} %get-tuple-element.23), channel_id=1, source_target_pairs={{8,0},{16,8},{24,16},{0,24},{9,1},{17,9},{25,17},{1,25},{10,2},{18... | collective-permute-start | bytes 1327112 | tf_op jit(solution)/shard_map/ppermute | solution.py:233
  16.6 15.0 %collective-permute-start.8 = (bf16[3,3,72,128]{3,2,1,0:T(8,128)(2,1)S(1)}, bf16[3,3,72,128]{3,2,1,0:T(8,128)(2,1)S(1)}, u32[]{:S(2)}, u32[]{:S(2)}) collective-permute-start(bf16[3,3,72,128]{3,2,1,0:T(8,128)(2,1)S(1)} %get-tuple-element.33), channel_id=1, source_target_pairs={{8,0},{16,8},{24,16},{0,24},{9,1},{17,9},{25,17},{1,25},{10,2},{18... | collective-permute-start | bytes 497672 | tf_op jit(solution)/shard_map/ppermute | solution.py:233
  16.7 14.9 %collective-permute-start.7 = (bf16[3,3,72,128]{3,2,1,0:T(8,128)(2,1)S(1)}, bf16[3,3,72,128]{3,2,1,0:T(8,128)(2,1)S(1)}, u32[]{:S(2)}, u32[]{:S(2)}) collective-permute-start(bf16[3,3,72,128]{3,2,1,0:T(8,128)(2,1)S(1)} %get-tuple-element.34), channel_id=1, source_target_pairs={{0,8},{8,16},{16,24},{24,0},{1,9},{9,17},{17,25},{25,1},{2,10},{10... | collective-permute-start | bytes 497672 | tf_op jit(solution)/shard_map/ppermute | solution.py:233
  21.9 10.9 %collective-permute-start.6 = (bf16[3,3,72,128]{3,2,1,0:T(8,128)(2,1)S(1)}, bf16[3,3,72,128]{3,2,1,0:T(8,128)(2,1)S(1)}, u32[]{:S(2)}, u32[]{:S(2)}) collective-permute-start(bf16[3,3,72,128]{3,2,1,0:T(8,128)(2,1)S(1)} %get-tuple-element.35), channel_id=1, source_target_pairs={{8,0},{16,8},{24,16},{0,24},{9,1},{17,9},{25,17},{1,25},{10,2},{18... | collective-permute-start | bytes 497672 | tf_op jit(solution)/shard_map/ppermute | solution.py:233
  24.8 7.9 %collective-permute-start.5 = (bf16[3,3,72,128]{3,2,1,0:T(8,128)(2,1)S(1)}, bf16[3,3,72,128]{3,2,1,0:T(8,128)(2,1)S(1)}, u32[]{:S(2)}, u32[]{:S(2)}) collective-permute-start(bf16[3,3,72,128]{3,2,1,0:T(8,128)(2,1)S(1)} %get-tuple-element.36), channel_id=1, source_target_pairs={{0,8},{8,16},{16,24},{24,0},{1,9},{9,17},{17,25},{25,1},{2,10},{10... | collective-permute-start | bytes 497672 | tf_op jit(solution)/shard_map/ppermute | solution.py:233

commit v3 on v2

v3 whole, which is shorter than its diff:
```python
import jax
import jax.numpy as jnp
from jax import lax
from jax.experimental import pallas as pl
from jax.experimental.pallas import tpu as pltpu
from jax.sharding import PartitionSpec as P


HALO = 3
SQRT_HALF = 0.7071067811865476
BF16 = jnp.bfloat16
F32 = jnp.float32
VMEM = pl.BlockSpec(memory_space=pltpu.VMEM)


def around(size, step):
    return -(-size // step) * step


def call(kernel, outs, scratch=(), flops=0, nbytes=0):
    outs = [jax.ShapeDtypeStruct(s, d) for s, d in outs]

    def run(*args):
        return pl.pallas_call(
            kernel,
            out_shape=outs,
            in_specs=[VMEM] * len(args),
            out_specs=[VMEM] * len(outs),
            scratch_shapes=list(scratch),
            cost_estimate=pl.CostEstimate(
                flops=flops, bytes_accessed=nbytes, transcendentals=0
            ),
            compiler_params=pltpu.CompilerParams(vmem_limit_bytes=48 * 1024 * 1024),
        )(*args)

    return run


def gelu(u):
    return 0.5 * u * (1.0 + lax.erf(u * SQRT_HALF))


def iota(shape, dim):
    return lax.broadcasted_iota(jnp.int32, shape, dim)


def rows_kernel(field, pairs, edges, planes):
    c, nx, ny, nz = field.shape
    rows = pairs.shape[2]
    m = iota((rows + 8, 2 * nz), 0)
    j = iota((rows + 8, 2 * nz), 1)
    half = nz // 2
    first = jnp.where(m < rows + 2, m - rows + half, m - rows - 1)
    m = jnp.where(m < rows, m, jnp.where(m < rows + 4, first, -8))
    second = (j >= nz).astype(jnp.int32)
    pick = (j - nz * second == 2 * m - 3 + second).astype(F32).astype(BF16)
    blank = jnp.zeros((c, nz), BF16)
    for x in range(nx):
        planes[x] = field[:, x].astype(F32).reshape(c * ny, nz)
        for y in range(0, ny, 2):
            blocks = []
            for k in range(2):
                b = planes[x, pl.ds(y + k, c, stride=ny), :].astype(BF16)
                blocks.append(jnp.concatenate([b, blank], axis=1))
                blocks.append(jnp.concatenate([blank, b], axis=1))
            r = lax.dot_general(
                pick,
                jnp.concatenate(blocks, axis=0),
                (((1,), (1,)), ((), ())),
                preferred_element_type=F32,
            ).astype(BF16)
            for k in range(2):
                lanes = slice(2 * c * k, 2 * c * (k + 1))
                pairs[x, y + k] = r[:rows, lanes]
                edges[x, y + k] = r[rows : rows + 4, lanes]


def faces_kernel(pairs, edges, own, xu, xd, yu, yd, wide):
    nx, ny, rows, _ = pairs.shape
    h = HALO
    wide[:, :, :4] = edges[...].astype(F32)
    got = wide[...]
    row = iota(got.shape, 2)
    low = jnp.where(row < 2, got, 0.0)
    moved = pltpu.roll(got, got.shape[2] - 1, 2)
    high = jnp.where((row >= 1) & (row < 3), moved, 0.0)
    e = pairs[...].astype(F32)
    e = jnp.concatenate(
        [e[:, :, :8] + low, e[:, :, 8 : rows - 8], e[:, :, rows - 8 :] + high], axis=2
    ).astype(BF16)
    own[...] = e
    xu[...] = e[nx - h :]
    xd[...] = e[:h]
    yu[...] = e[:, ny - h :]
    yd[...] = e[:, :h]


def weights_kernel(k1, k2, k3, b1, b2, b3, w1, w2, w3, bias):
    _, _, taps, o, c = k1.shape
    j = iota((taps * o, 8 * o), 0)
    n = iota((taps * o, 8 * o), 1)
    p = n // (4 * o)
    t = n // (2 * o) % 2
    q = n // o % 2
    pick = (j == (p - q + 2 * t) * o + n % o).astype(F32).astype(BF16)
    for k, w in ((k1, w1), (k2, w2), (k3, w3)):
        for a in range(3):
            for e in range(3):
                r = lax.dot_general(
                    k[a, e].reshape(taps * o, c),
                    pick,
                    (((0,), (0,)), ((), ())),
                    preferred_element_type=F32,
                ).astype(BF16)
                at = (a * 3 + e) * 2 * c
                w[at : at + c] = r[:, : 4 * o]
                w[at + c : at + 2 * c] = r[:, 4 * o :]
    for i, b in enumerate((b1, b2, b3)):
        bias[i : i + 1] = jnp.concatenate([b[...], b[...]], axis=1)


def conv(source, x, lines, weight, bias):
    rows = source.shape[2]
    height = lines * rows
    taps = [
        source[x + a, e : e + lines].reshape(height, 128)
        for a in range(3)
        for e in range(3)
    ]
    both = jnp.dot(jnp.concatenate(taps, axis=1), weight, preferred_element_type=F32)
    u = both[:, :128] + pltpu.roll(both[:, 128:], height - 1, 0) + bias
    return gelu(u).astype(BF16).reshape(lines, rows, 128)


def strip_kernel(own, xm, xp, l1, w1, bias, s0):
    nx, ny, rows, _ = own.shape
    h = HALO
    s0[:h, :, :rows] = xm[...]
    s0[h : h + nx, :, :rows] = own[...]
    s0[h + nx :, :, :rows] = xp[...]
    for x in range(nx + 4):
        l1[x] = conv(s0, x, ny - 2, w1[...], bias[0:1])


def middle_first(own, xm, xp, w1, bias, l1, s0):
    strip_kernel(own, xm, xp, l1, w1, bias, s0)


def middle_second(l1, w2, w3, bias, l2, l3):
    lines = l1.shape[1]
    for x in range(l2.shape[0]):
        l2[x] = conv(l1, x, lines - 2, w2[...], bias[1:2])
    for x in range(l3.shape[0]):
        l3[x] = conv(l2, x, lines - 4, w3[...], bias[2:3])[:, : l3.shape[2]]


def spread_pattern(half, nz):
    r = iota((4 * half, 8 * nz), 0)
    n = iota((4 * half, 8 * nz), 1)
    hit = (r // half == n // nz % 4) & (n % nz == 2 * (r % half) + n // (4 * nz))
    return hit.astype(F32).astype(BF16)


def edge_strip(below, own, xm, xp, ym, cm, cp, l1, l2, ws, bias, s0, s1, s2):
    nx, ny, rows, _ = own.shape
    h = HALO
    inner = slice(0, 2) if below else slice(ny - 2, ny)
    near = slice(3, 5) if below else slice(0, 2)
    far = slice(0, 3) if below else slice(2, 5)
    for planes, core, side in (
        (slice(0, h), xm, cm),
        (slice(h, h + nx), own, ym),
        (slice(h + nx, h + nx + h), xp, cp),
    ):
        s0[planes, near, :rows] = core[:, inner]
        s0[planes, far, :rows] = side[...]
    n1, n2 = l1.shape[1], l2.shape[1]
    s1[:, near] = l1[:, :2] if below else l1[:, n1 - 2 :]
    s2[:, near] = l2[:, :2] if below else l2[:, n2 - 2 :]
    for source, target, i in ((s0, s1, 0), (s1, s2, 1)):
        for x in range(source.shape[0] - 2):
            target[x, far] = conv(source, x, 3, ws[i][...], bias[i : i + 1])
    return [conv(s2, x, 3, ws[2][...], bias[2:3]) for x in range(nx)]


def lower_kernel(own, xm, xp, ym, cm, cp, l1, l2, w1, w2, w3, bias, low, s0, s1, s2):
    y = edge_strip(
        True, own, xm, xp, ym, cm, cp, l1, l2, (w1, w2, w3), bias, s0, s1, s2
    )
    for x, lines in enumerate(y):
        low[x] = lines[:, : low.shape[2]]


def upper_kernel(
    own, xm, xp, yp, cm, cp, l1, l2, low, mid, w1, w2, w3, bias, out, s0, s1, s2, stage
):
    c, nx, ny, nz = out.shape
    half = nz // 2
    y = edge_strip(
        False, own, xm, xp, yp, cm, cp, l1, l2, (w1, w2, w3), bias, s0, s1, s2
    )
    pattern = spread_pattern(half, nz)
    for x in range(nx):
        lines = [low[x, i] for i in range(3)] + [mid[x, i] for i in range(ny - 6)]
        lines += [y[x][i, :half] for i in range(3)]
        for first in range(0, ny, 4):
            r = lax.dot_general(
                jnp.concatenate(lines[first : first + 4], axis=0),
                pattern,
                (((0,), (0,)), ((), ())),
                preferred_element_type=F32,
            )
            r = r[:c, : 4 * nz] + r[c:, 4 * nz :]
            for i in range(4):
                stage[x, pl.ds(first + i, c, stride=ny), :] = r[
                    :, i * nz : (i + 1) * nz
                ]
        out[:, x] = stage[x].reshape(c, ny, nz).astype(BF16)


def shift(x, axis, up):
    count = lax.axis_size(axis)
    pairs = [(i, (i + 1) % count) if up else ((i + 1) % count, i) for i in range(count)]
    return lax.ppermute(x, axis, pairs)


def shards(field, kernel_one, bias_one, kernel_two, bias_two, kernel_three, bias_three):
    h = HALO
    field = field[0]
    c, nx, ny, nz = field.shape
    rows = around((nz + 2 * h) // 2, 8)
    pad = around(rows, 16)
    half = nz // 2
    line = 2 * c

    pairs, edges = call(
        rows_kernel,
        [((nx, ny, rows, line), BF16), ((nx, ny, 4, line), BF16)],
        [pltpu.VMEM((nx, c * ny, nz), F32)],
    )(field)
    if lax.axis_size("gz") == 2:
        edges = shift(edges, "gz", True)
    else:
        edges = jnp.concatenate(
            [shift(edges[:, :, :2], "gz", True), shift(edges[:, :, 2:], "gz", False)],
            axis=2,
        )
    xface = ((h, ny, rows, line), BF16)
    yface = ((nx, h, rows, line), BF16)
    own, xu, xd, yu, yd = call(
        faces_kernel,
        [((nx, ny, rows, line), BF16), xface, xface, yface, yface],
        [pltpu.VMEM((nx, ny, 8, line), F32)],
    )(pairs, edges)
    xm = shift(xu, "gx", True)
    xp = shift(xd, "gx", False)
    ym = shift(yu, "gy", True)
    yp = shift(yd, "gy", False)
    cmm = shift(ym[nx - h :], "gx", True)
    cpm = shift(ym[:h], "gx", False)
    cmp = shift(yp[nx - h :], "gx", True)
    cpp = shift(yp[:h], "gx", False)
    w1, w2, w3, bias = call(
        weights_kernel,
        [((18 * c, 4 * c), BF16)] * 3 + [((3, line), F32)],
        flops=2 * 10**9,
        nbytes=10**6,
    )(
        kernel_one, kernel_two, kernel_three,
        bias_one[None], bias_two[None], bias_three[None],
    )
    (l1,) = call(
        middle_first,
        [((nx + 4, ny - 2, pad, line), BF16)],
        [pltpu.VMEM((nx + 6, ny, pad, line), BF16)],
        flops=3 * 10**9,
        nbytes=10**6,
    )(own, xm, xp, w1, bias)
    l2, l3 = call(
        middle_second,
        [((nx + 2, ny - 4, pad, line), BF16), ((nx, ny - 6, half, line), BF16)],
        flops=2 * 10**9,
        nbytes=10**6,
    )(l1, w2, w3, bias)
    strips = [pltpu.VMEM((nx + k, 5, pad, line), BF16) for k in (6, 4, 2)]
    (low,) = call(
        lower_kernel, [((nx, 3, half, line), BF16)], strips,
        flops=4 * 10**9, nbytes=10**6,
    )(own, xm, xp, ym, cmm, cpm, l1, l2, w1, w2, w3, bias)
    (out,) = call(
        upper_kernel,
        [((c, nx, ny, nz), BF16)],
        strips + [pltpu.VMEM((nx, c * ny, nz), F32)],
        flops=4 * 10**9, nbytes=10**6,
    )(own, xm, xp, yp, cmp, cpp, l1, l2, low, l3, w1, w2, w3, bias)
    return out[None]


def solution(mesh):
    return jax.shard_map(
        shards,
        mesh=mesh,
        in_specs=(P(None, None, "gx", "gy", "gz"), P(), P(), P(), P(), P(), P()),
        out_specs=P(None, None, "gx", "gy", "gz"),
        check_vma=False,
    )
```

time: 42 us -> 38.6 us (0.919)
  the two profiles are of different devices: /device:TPU:0 before, /device:TPU:1 now
where the time goes in v3:
time: 38.6 us; the launch traced here: 38.4 us
  Pallas kernels  14.6 us (38%)
  starting transfers between devices  13.3 us (34%)
  waiting for transfers between devices  7.64 us (20%)
  local copies, waits for them, and re-layouts  2.81 us (7%)
    pallas_call x7, Pallas kernels, run(): pl.pallas_call(kernel, out_shape=outs, in_specs=[VMEM] * len(args), out_s...  14.6 us
    ppermute x9, starting transfers between devices, shift(): return lax.ppermute(x, axis, pairs)  13.3 us
    ppermute x9, waiting for transfers between devices, shift(): return lax.ppermute(x, axis, pairs)  7.64 us
    unnamed x14, local copies, waits for them, and re-layouts  2.73 us
  transfers between devices with their start and end apart: 9, of which 4 were waited for; matrix products, arithmetic and copies ran while one was open for 0% of the time, Pallas kernels for 23%

profile of v3, /device:TPU:1, one launch (start us, length us, event | category | flops | bytes accessed | tf_op | source)
XLA Modules:
  0.0 38.4 jit_solution(12094379414028980831)
XLA Ops:
  0.0 0.0 copy-start
  0.0 1.0 %copy-done = bf16[1,64,4,8,128]{4,3,2,1,0:T(8,128)(2,1)S(1)} copy-done((bf16[1,64,4,8,128]{4,3,2,1,0:T(8,128)(2,1)S(1)}, bf16[1,64,4,8,128]{4,3,2,1,0:T(8,128)(2,1)}, u32[]{:S(2)}) %copy-start) | copy-done | bytes 524312
  1.0 0.0 copy-start.2
  1.0 0.8 %shard_map.73 = (bf16[4,8,72,128]{3,2,1,0:T(8,128)(2,1)S(1)}, bf16[4,8,4,128]{3,2,1,0:T(4,128)(2,1)S(1)}) custom-call(bf16[64,4,8,128]{3,2,1,0:T(8,128)(2,1)S(1)} %bitcast.5), custom_call_target="tpu_custom_call" | custom-call | tf_op jit(solution)/shard_map/pallas_call | solution.py:24
  1.8 0.0 copy-start.1
  1.8 2.1 %collective-permute-start = (bf16[4,8,4,128]{3,2,1,0:T(4,128)(2,1)S(1)}, bf16[4,8,4,128]{3,2,1,0:T(4,128)(2,1)S(1)}, u32[]{:S(2)}, u32[]{:S(2)}) collective-permute-start(bf16[4,8,4,128]{3,2,1,0:T(4,128)(2,1)S(1)} %get-tuple-element.19), channel_id=1, source_target_pairs={{0,1},{1,0},{2,3},{3,2},{4,5},{5,4},{6,7},{7,6},{8,9},{9,8},{10,11... | collective-permute-start | bytes 98312 | tf_op jit(solution)/shard_map/ppermute | solution.py:224
  4.0 1.3 %collective-permute-done.edges = bf16[4,8,4,128]{3,2,1,0:T(4,128)(2,1)S(1)} collective-permute-done((bf16[4,8,4,128]{3,2,1,0:T(4,128)(2,1)S(1)}, bf16[4,8,4,128]{3,2,1,0:T(4,128)(2,1)S(1)}, u32[]{:S(2)}, u32[]{:S(2)}) %collective-permute-start) | collective-permute-done | bytes 32800 | tf_op jit(solution)/shard_map/ppermute | solution.py:224
  5.3 0.2 shard_map.74
  5.5 1.6 %collective-permute-start.6 = (bf16[4,3,72,128]{3,2,1,0:T(8,128)(2,1)S(1)}, bf16[4,3,72,128]{3,2,1,0:T(8,128)(2,1)S(1)}, u32[]{:S(2)}, u32[]{:S(2)}) collective-permute-start(bf16[4,3,72,128]{3,2,1,0:T(8,128)(2,1)S(1)} %get-tuple-element.29), channel_id=1, source_target_pairs={{0,2},{2,4},{4,6},{6,0},{1,3},{3,5},{5,7},{7,1},{8,10},{10,12},{12... | collective-permute-start | bytes 663560 | tf_op jit(solution)/shard_map/ppermute | solution.py:224
  7.1 0.0 copy-start.4
  7.1 0.0 copy-start.5
  7.1 0.0 copy-start.6
  7.1 0.0 copy-done.2
  7.1 0.0 copy-done.1
  7.1 0.6 %copy-done.4 = f32[64]{0:T(128)S(1)} copy-done((f32[64]{0:T(128)S(1)}, f32[64]{0:T(128)}, u32[]{:S(2)}) %copy-start.4) | copy-done | bytes 280
  7.7 0.0 copy-done.5
  7.8 0.0 copy-done.6
  7.8 0.0 copy-start.3
  7.8 1.0 %copy-done.3 = bf16[3,3,3,64,64]{4,3,2,1,0:T(8,128)(2,1)S(1)} copy-done((bf16[3,3,3,64,64]{4,3,2,1,0:T(8,128)(2,1)S(1)}, bf16[3,3,3,64,64]{4,3,2,1,0:T(8,128)(2,1)}, u32[]{:S(2)}) %copy-start.3) | copy-done | bytes 221208
  8.8 1.1 %shard_map.75 = (bf16[1152,256]{1,0:T(8,128)(2,1)S(1)}, bf16[1152,256]{1,0:T(8,128)(2,1)S(1)}, bf16[1152,256]{1,0:T(8,128)(2,1)S(1)}, f32[3,128]{1,0:T(4,128)S(1)}) custom-call(bf16[3,3,3,64,64]{4,3,2,1,0:T(8,128)(2,1)S(1)} %copy-done.1, bf16[3,3,3,64,64]{4,3,2,1,0:T(8,128)(2,1)S(1)} %copy-done.2, bf16[3,3,3,64,64]{4,3,2,1,0:T(8,128)(2,1)S(1)} %copy-done.3, ...), custom_call_target="tpu_custom_call" | custom-call | flops 2000000000 | bytes 1000000 | tf_op jit(solution)/shard_map/pallas_call | solution.py:24
  9.9 3.3 %collective-permute-start.1 = (bf16[3,8,72,128]{3,2,1,0:T(8,128)(2,1)S(1)}, bf16[3,8,72,128]{3,2,1,0:T(8,128)(2,1)S(1)}, u32[]{:S(2)}, u32[]{:S(2)}) collective-permute-start(bf16[3,8,72,128]{3,2,1,0:T(8,128)(2,1)S(1)} %get-tuple-element.21), channel_id=1, source_target_pairs={{0,8},{8,16},{16,24},{24,0},{1,9},{9,17},{17,25},{25,1},{2,10},{10... | collective-permute-start | bytes 1327112 | tf_op jit(solution)/shard_map/ppermute | solution.py:224
  13.2 0.0 collective-permute-start.2
  13.2 2.0 %collective-permute-start.3 = (bf16[4,3,72,128]{3,2,1,0:T(8,128)(2,1)S(1)}, bf16[4,3,72,128]{3,2,1,0:T(8,128)(2,1)S(1)}, u32[]{:S(2)}, u32[]{:S(2)}) collective-permute-start(bf16[4,3,72,128]{3,2,1,0:T(8,128)(2,1)S(1)} %get-tuple-element.23), channel_id=1, source_target_pairs={{2,0},{4,2},{6,4},{0,6},{3,1},{5,3},{7,5},{1,7},{10,8},{12,10},{14... | collective-permute-start | bytes 663560 | tf_op jit(solution)/shard_map/ppermute | solution.py:224
  15.2 0.0 collective-permute-done.6.ym
  15.2 2.1 %collective-permute-start.7 = (bf16[3,3,72,128]{3,2,1,0:T(8,128)(2,1)S(1)}, bf16[3,3,72,128]{3,2,1,0:T(8,128)(2,1)S(1)}, u32[]{:S(2)}, u32[]{:S(2)}) collective-permute-start(bf16[3,3,72,128]{3,2,1,0:T(8,128)(2,1)S(1)} %get-tuple-element.32), channel_id=1, source_target_pairs={{0,8},{8,16},{16,24},{24,0},{1,9},{9,17},{17,25},{25,1},{2,10},{10... | collective-permute-start | bytes 497672 | tf_op jit(solution)/shard_map/ppermute | solution.py:224
  17.3 0.0 collective-permute-start.8
  17.3 2.2 %collective-permute-done.3.yp = bf16[4,3,72,128]{3,2,1,0:T(8,128)(2,1)S(1)} collective-permute-done((bf16[4,3,72,128]{3,2,1,0:T(8,128)(2,1)S(1)}, bf16[4,3,72,128]{3,2,1,0:T(8,128)(2,1)S(1)}, u32[]{:S(2)}, u32[]{:S(2)}) %collective-permute-start.3) | collective-permute-done | bytes 221216 | tf_op jit(solution)/shard_map/ppermute | solution.py:224
  19.6 1.8 %collective-permute-start.4 = (bf16[3,3,72,128]{3,2,1,0:T(8,128)(2,1)S(1)}, bf16[3,3,72,128]{3,2,1,0:T(8,128)(2,1)S(1)}, u32[]{:S(2)}, u32[]{:S(2)}) collective-permute-start(bf16[3,3,72,128]{3,2,1,0:T(8,128)(2,1)S(1)} %get-tuple-element.34), channel_id=1, source_target_pairs={{0,8},{8,16},{16,24},{24,0},{1,9},{9,17},{17,25},{25,1},{2,10},{10... | collective-permute-start | bytes 497672 | tf_op jit(solution)/shard_map/ppermute | solution.py:224
  21.4 0.9 %collective-permute-done.1.xm = bf16[3,8,72,128]{3,2,1,0:T(8,128)(2,1)S(1)} collective-permute-done((bf16[3,8,72,128]{3,2,1,0:T(8,128)(2,1)S(1)}, bf16[3,8,72,128]{3,2,1,0:T(8,128)(2,1)S(1)}, u32[]{:S(2)}, u32[]{:S(2)}) %collective-permute-start.1) | collective-permute-done | bytes 442400 | tf_op jit(solution)/shard_map/ppermute | solution.py:224
  22.3 0.4 %collective-permute-start.5 = (bf16[3,3,72,128]{3,2,1,0:T(8,128)(2,1)S(1)}, bf16[3,3,72,128]{3,2,1,0:T(8,128)(2,1)S(1)}, u32[]{:S(2)}, u32[]{:S(2)}) collective-permute-start(bf16[3,3,72,128]{3,2,1,0:T(8,128)(2,1)S(1)} %get-tuple-element.33), channel_id=1, source_target_pairs={{8,0},{16,8},{24,16},{0,24},{9,1},{17,9},{25,17},{1,25},{10,2},{18... | collective-permute-start | bytes 497672 | tf_op jit(solution)/shard_map/ppermute | solution.py:224
  22.8 3.2 %collective-permute-done.2.xp = bf16[3,8,72,128]{3,2,1,0:T(8,128)(2,1)S(1)} collective-permute-done((bf16[3,8,72,128]{3,2,1,0:T(8,128)(2,1)S(1)}, bf16[3,8,72,128]{3,2,1,0:T(8,128)(2,1)S(1)}, u32[]{:S(2)}, u32[]{:S(2)}) %collective-permute-start.2) | collective-permute-done | bytes 442400 | tf_op jit(solution)/shard_map/ppermute | solution.py:224
  25.9 2.9 %shard_map.76.l1 = bf16[8,6,80,128]{3,2,1,0:T(8,128)(2,1)S(1)} custom-call(bf16[4,8,72,128]{3,2,1,0:T(8,128)(2,1)S(1)} %get-tuple-element.20.own, bf16[3,8,72,128]{3,2,1,0:T(8,128)(2,1)S(1)} %collective-permute-done.1.xm, bf16[3,8,72,128]{3,2,1,0:T(8,128)(2,1)S(1)} %collective-permute-done.2.xp, bf16[1152,256]{1,0:T(8,128)(2,1)S(1)} %get-tuple-element.24.w1, ...), custom_call_target="tpu_custom_call" | custom-call | flops 3000000000 | bytes 1000000 | tf_op jit(solution)/shard_map/pallas_call | solution.py:24
  28.8 1.9 %shard_map.77 = (bf16[6,4,80,128]{3,2,1,0:T(8,128)(2,1)S(1)}, bf16[4,2,64,128]{3,2,1,0:T(8,128)(2,1)S(1)}) custom-call(bf16[8,6,80,128]{3,2,1,0:T(8,128)(2,1)S(1)} %shard_map.76.l1, bf16[1152,256]{1,0:T(8,128)(2,1)S(1)} %get-tuple-element.26.w2, bf16[1152,256]{1,0:T(8,128)(2,1)S(1)} %get-tuple-element.27.w3, f32[3,128]{1,0:T(4,128)S(1)} %get-tuple-element.25.bias), custom_call_target="tpu_custom_call" | custom-call | flops 2000000000 | bytes 1000000 | tf_op jit(solution)/shard_map/pallas_call | solution.py:24
  30.7 0.0 collective-permute-done.7.cm
  30.7 0.0 collective-permute-done.8.cp
  30.7 3.1 %shard_map.78.low = bf16[4,3,64,128]{3,2,1,0:T(8,128)(2,1)S(1)} custom-call(bf16[4,8,72,128]{3,2,1,0:T(8,128)(2,1)S(1)} %get-tuple-element.20.own, bf16[3,8,72,128]{3,2,1,0:T(8,128)(2,1)S(1)} %collective-permute-done.1.xm, bf16[3,8,72,128]{3,2,1,0:T(8,128)(2,1)S(1)} %collective-permute-done.2.xp, bf16[4,3,72,128]{3,2,1,0:T(8,128)(2,1)S(1)} %collective-permute-done.6.ym, ...), custom_call_target="tpu_custom_call" | custom-call | flops 4000000000 | bytes 1000000 | tf_op jit(solution)/shard_map/pallas_call | solution.py:24
  33.9 0.0 collective-permute-done.4.cm
  33.9 0.0 collective-permute-done.5.cp
  33.9 4.5 %shard_map.79 = bf16[64,4,8,128]{3,2,1,0:T(8,128)(2,1)} custom-call(bf16[4,8,72,128]{3,2,1,0:T(8,128)(2,1)S(1)} %get-tuple-element.20.own, bf16[3,8,72,128]{3,2,1,0:T(8,128)(2,1)S(1)} %collective-permute-done.1.xm, bf16[3,8,72,128]{3,2,1,0:T(8,128)(2,1)S(1)} %collective-permute-done.2.xp, bf16[4,3,72,128]{3,2,1,0:T(8,128)(2,1)S(1)} %collective-permute-done.3.yp, ...), custom_call_target="tpu_custom_call" | custom-call | flops 4000000000 | bytes 1000000 | tf_op jit(solution)/shard_map/pallas_call | solution.py:24
  (2 shorter events, 0.1 us)
Async XLA Ops:
  0.0 1.0 %copy-start = (bf16[1,64,4,8,128]{4,3,2,1,0:T(8,128)(2,1)S(1)}, bf16[1,64,4,8,128]{4,3,2,1,0:T(8,128)(2,1)}, u32[]{:S(2)}) copy-start(bf16[1,64,4,8,128]{4,3,2,1,0:T(8,128)(2,1)} %param.7) | copy-start | bytes 1572868
  1.0 6.0 %copy-start.2 = (bf16[3,3,3,64,64]{4,3,2,1,0:T(8,128)(2,1)S(1)}, bf16[3,3,3,64,64]{4,3,2,1,0:T(8,128)(2,1)}, u32[]{:S(2)}) copy-start(bf16[3,3,3,64,64]{4,3,2,1,0:T(8,128)(2,1)} %k2.1) | copy-start | bytes 663556
  1.8 5.3 %copy-start.1 = (bf16[3,3,3,64,64]{4,3,2,1,0:T(8,128)(2,1)S(1)}, bf16[3,3,3,64,64]{4,3,2,1,0:T(8,128)(2,1)}, u32[]{:S(2)}) copy-start(bf16[3,3,3,64,64]{4,3,2,1,0:T(8,128)(2,1)} %k1.1) | copy-start | bytes 663556
  1.8 3.4 %collective-permute-start = (bf16[4,8,4,128]{3,2,1,0:T(4,128)(2,1)S(1)}, bf16[4,8,4,128]{3,2,1,0:T(4,128)(2,1)S(1)}, u32[]{:S(2)}, u32[]{:S(2)}) collective-permute-start(bf16[4,8,4,128]{3,2,1,0:T(4,128)(2,1)S(1)} %get-tuple-element.19), channel_id=1, source_target_pairs={{0,1},{1,0},{2,3},{3,2},{4,5},{5,4},{6,7},{7,6},{8,9},{9,8},{10,11... | collective-permute-start | bytes 98312 | tf_op jit(solution)/shard_map/ppermute | solution.py:224
  5.5 9.7 %collective-permute-start.6 = (bf16[4,3,72,128]{3,2,1,0:T(8,128)(2,1)S(1)}, bf16[4,3,72,128]{3,2,1,0:T(8,128)(2,1)S(1)}, u32[]{:S(2)}, u32[]{:S(2)}) collective-permute-start(bf16[4,3,72,128]{3,2,1,0:T(8,128)(2,1)S(1)} %get-tuple-element.29), channel_id=1, source_target_pairs={{0,2},{2,4},{4,6},{6,0},{1,3},{3,5},{5,7},{7,1},{8,10},{10,12},{12... | collective-permute-start | bytes 663560 | tf_op jit(solution)/shard_map/ppermute | solution.py:224
  7.1 0.7 %copy-start.4 = (f32[64]{0:T(128)S(1)}, f32[64]{0:T(128)}, u32[]{:S(2)}) copy-start(f32[64]{0:T(128)} %param.9) | copy-start | bytes 772
  7.1 0.7 %copy-start.5 = (f32[64]{0:T(128)S(1)}, f32[64]{0:T(128)}, u32[]{:S(2)}) copy-start(f32[64]{0:T(128)} %param.11) | copy-start | bytes 772
  7.1 0.7 %copy-start.6 = (f32[64]{0:T(128)S(1)}, f32[64]{0:T(128)}, u32[]{:S(2)}) copy-start(f32[64]{0:T(128)} %param.13) | copy-start | bytes 772
  7.8 1.0 %copy-start.3 = (bf16[3,3,3,64,64]{4,3,2,1,0:T(8,128)(2,1)S(1)}, bf16[3,3,3,64,64]{4,3,2,1,0:T(8,128)(2,1)}, u32[]{:S(2)}) copy-start(bf16[3,3,3,64,64]{4,3,2,1,0:T(8,128)(2,1)} %k3.1) | copy-start | bytes 663556
  9.9 12.4 %collective-permute-start.1 = (bf16[3,8,72,128]{3,2,1,0:T(8,128)(2,1)S(1)}, bf16[3,8,72,128]{3,2,1,0:T(8,128)(2,1)S(1)}, u32[]{:S(2)}, u32[]{:S(2)}) collective-permute-start(bf16[3,8,72,128]{3,2,1,0:T(8,128)(2,1)S(1)} %get-tuple-element.21), channel_id=1, source_target_pairs={{0,8},{8,16},{16,24},{24,0},{1,9},{9,17},{17,25},{25,1},{2,10},{10... | collective-permute-start | bytes 1327112 | tf_op jit(solution)/shard_map/ppermute | solution.py:224
  13.2 12.8 %collective-permute-start.2 = (bf16[3,8,72,128]{3,2,1,0:T(8,128)(2,1)S(1)}, bf16[3,8,72,128]{3,2,1,0:T(8,128)(2,1)S(1)}, u32[]{:S(2)}, u32[]{:S(2)}) collective-permute-start(bf16[3,8,72,128]{3,2,1,0:T(8,128)(2,1)S(1)} %get-tuple-element.22), channel_id=1, source_target_pairs={{8,0},{16,8},{24,16},{0,24},{9,1},{17,9},{25,17},{1,25},{10,2},{18... | collective-permute-start | bytes 1327112 | tf_op jit(solution)/shard_map/ppermute | solution.py:224
  13.2 6.3 %collective-permute-start.3 = (bf16[4,3,72,128]{3,2,1,0:T(8,128)(2,1)S(1)}, bf16[4,3,72,128]{3,2,1,0:T(8,128)(2,1)S(1)}, u32[]{:S(2)}, u32[]{:S(2)}) collective-permute-start(bf16[4,3,72,128]{3,2,1,0:T(8,128)(2,1)S(1)} %get-tuple-element.23), channel_id=1, source_target_pairs={{2,0},{4,2},{6,4},{0,6},{3,1},{5,3},{7,5},{1,7},{10,8},{12,10},{14... | collective-permute-start | bytes 663560 | tf_op jit(solution)/shard_map/ppermute | solution.py:224
  15.2 15.5 %collective-permute-start.7 = (bf16[3,3,72,128]{3,2,1,0:T(8,128)(2,1)S(1)}, bf16[3,3,72,128]{3,2,1,0:T(8,128)(2,1)S(1)}, u32[]{:S(2)}, u32[]{:S(2)}) collective-permute-start(bf16[3,3,72,128]{3,2,1,0:T(8,128)(2,1)S(1)} %get-tuple-element.32), channel_id=1, source_target_pairs={{0,8},{8,16},{16,24},{24,0},{1,9},{9,17},{17,25},{25,1},{2,10},{10... | collective-permute-start | bytes 497672 | tf_op jit(solution)/shard_map/ppermute | solution.py:224
  17.3 13.4 %collective-permute-start.8 = (bf16[3,3,72,128]{3,2,1,0:T(8,128)(2,1)S(1)}, bf16[3,3,72,128]{3,2,1,0:T(8,128)(2,1)S(1)}, u32[]{:S(2)}, u32[]{:S(2)}) collective-permute-start(bf16[3,3,72,128]{3,2,1,0:T(8,128)(2,1)S(1)} %get-tuple-element.31), channel_id=1, source_target_pairs={{8,0},{16,8},{24,16},{0,24},{9,1},{17,9},{25,17},{1,25},{10,2},{18... | collective-permute-start | bytes 497672 | tf_op jit(solution)/shard_map/ppermute | solution.py:224
  19.6 14.3 %collective-permute-start.4 = (bf16[3,3,72,128]{3,2,1,0:T(8,128)(2,1)S(1)}, bf16[3,3,72,128]{3,2,1,0:T(8,128)(2,1)S(1)}, u32[]{:S(2)}, u32[]{:S(2)}) collective-permute-start(bf16[3,3,72,128]{3,2,1,0:T(8,128)(2,1)S(1)} %get-tuple-element.34), channel_id=1, source_target_pairs={{0,8},{8,16},{16,24},{24,0},{1,9},{9,17},{17,25},{25,1},{2,10},{10... | collective-permute-start | bytes 497672 | tf_op jit(solution)/shard_map/ppermute | solution.py:224
  22.3 11.5 %collective-permute-start.5 = (bf16[3,3,72,128]{3,2,1,0:T(8,128)(2,1)S(1)}, bf16[3,3,72,128]{3,2,1,0:T(8,128)(2,1)S(1)}, u32[]{:S(2)}, u32[]{:S(2)}) collective-permute-start(bf16[3,3,72,128]{3,2,1,0:T(8,128)(2,1)S(1)} %get-tuple-element.33), channel_id=1, source_target_pairs={{8,0},{16,8},{24,16},{0,24},{9,1},{17,9},{25,17},{1,25},{10,2},{18... | collective-permute-start | bytes 497672 | tf_op jit(solution)/shard_map/ppermute | solution.py:224

commit v4 on v3

--- a/solution.py
+++ b/solution.py
@@ -44,9 +44,10 @@
     return lax.broadcasted_iota(jnp.int32, shape, dim)
 
 
-def rows_kernel(field, pairs, edges, planes):
+def rows_kernel(field, pairs, edges, xu, xd, planes):
     c, nx, ny, nz = field.shape
     rows = pairs.shape[2]
+    h = HALO
     m = iota((rows + 8, 2 * nz), 0)
     j = iota((rows + 8, 2 * nz), 1)
     half = nz // 2
@@ -73,26 +74,38 @@
                 lanes = slice(2 * c * k, 2 * c * (k + 1))
                 pairs[x, y + k] = r[:rows, lanes]
                 edges[x, y + k] = r[rows : rows + 4, lanes]
-
-
-def faces_kernel(pairs, edges, own, xu, xd, yu, yd, wide):
-    nx, ny, rows, _ = pairs.shape
-    h = HALO
+                if x >= nx - h:
+                    xu[x - nx + h, y + k] = r[:rows, lanes]
+                if x < h:
+                    xd[x, y + k] = r[:rows, lanes]
+
+
+def end_rows(lines, edges, wide):
+    rows = lines.shape[2]
     wide[:, :, :4] = edges[...].astype(F32)
     got = wide[...]
     row = iota(got.shape, 2)
     low = jnp.where(row < 2, got, 0.0)
     moved = pltpu.roll(got, got.shape[2] - 1, 2)
     high = jnp.where((row >= 1) & (row < 3), moved, 0.0)
-    e = pairs[...].astype(F32)
+    first = lines[:, :, :8].astype(F32) + low
+    last = lines[:, :, rows - 8 :].astype(F32) + high
+    return first, last
+
+
+def faces_kernel(pairs, edges, own, yu, yd, eu, ed, wide):
+    nx, ny, rows, line = pairs.shape
+    h = HALO
+    first, last = end_rows(pairs, edges, wide)
     e = jnp.concatenate(
-        [e[:, :, :8] + low, e[:, :, 8 : rows - 8], e[:, :, rows - 8 :] + high], axis=2
-    ).astype(BF16)
-    own[...] = e
-    xu[...] = e[nx - h :]
-    xd[...] = e[:h]
+        [first, pairs[:, :, 8 : rows - 8].astype(F32), last], axis=2
+    )
+    own[...] = e.reshape(nx, ny * rows, line).astype(BF16)
+    e = e.astype(BF16)
     yu[...] = e[:, ny - h :]
     yd[...] = e[:, :h]
+    eu[...] = edges[nx - h :]
+    ed[...] = edges[:h]
 
 
 def weights_kernel(k1, k2, k3, b1, b2, b3, w1, w2, w3, bias):
@@ -119,39 +132,53 @@
         bias[i : i + 1] = jnp.concatenate([b[...], b[...]], axis=1)
 
 
-def conv(source, x, lines, weight, bias):
-    rows = source.shape[2]
-    height = lines * rows
+def conv(source, x, rows, lines, weight, bias):
+    height = around(lines * rows, 16)
     taps = [
-        source[x + a, e : e + lines].reshape(height, 128)
-        for a in range(3)
-        for e in range(3)
+        source[x + a, e * rows : e * rows + height] for a in range(3) for e in range(3)
     ]
     both = jnp.dot(jnp.concatenate(taps, axis=1), weight, preferred_element_type=F32)
     u = both[:, :128] + pltpu.roll(both[:, 128:], height - 1, 0) + bias
-    return gelu(u).astype(BF16).reshape(lines, rows, 128)
-
-
-def strip_kernel(own, xm, xp, l1, w1, bias, s0):
-    nx, ny, rows, _ = own.shape
-    h = HALO
-    s0[:h, :, :rows] = xm[...]
-    s0[h : h + nx, :, :rows] = own[...]
-    s0[h + nx :, :, :rows] = xp[...]
+    return gelu(u).astype(BF16)[: lines * rows]
+
+
+def middle_own(own, w1, bias, rows, l1):
+    lines = own.shape[1] // rows - 2
+    for x in range(l1.shape[0]):
+        l1[x] = conv(own, x, rows, lines, w1[...], bias[0:1])
+
+
+def middle_first(own, xm, xp, em, ep, l1own, w1, bias, l1, near, s0, wide):
+    h, ny, rows, line = xm.shape
+    nx = own.shape[0]
+    for at, face, edges in ((0, xm, em), (h + nx, xp, ep)):
+        s0[at : at + h] = face[...].reshape(h, ny * rows, line)
+        first, last = end_rows(face, edges, wide)
+        for i in range(h):
+            for y in range(ny):
+                s0[at + i, y * rows : y * rows + 8] = first[i, y].astype(BF16)
+                s0[at + i, y * rows + rows - 8 : (y + 1) * rows] = last[i, y].astype(
+                    BF16
+                )
+    s0[h : h + nx] = own[...]
+    near[:, : 2 * rows] = s0[:, : 2 * rows]
+    near[:, 2 * rows :] = s0[:, (ny - 2) * rows :]
     for x in range(nx + 4):
-        l1[x] = conv(s0, x, ny - 2, w1[...], bias[0:1])
-
-
-def middle_first(own, xm, xp, w1, bias, l1, s0):
-    strip_kernel(own, xm, xp, l1, w1, bias, s0)
-
-
-def middle_second(l1, w2, w3, bias, l2, l3):
-    lines = l1.shape[1]
+        if 3 <= x < nx + 1:
+            l1[x] = l1own[x - 3]
+        else:
+            l1[x] = conv(s0, x, rows, ny - 2, w1[...], bias[0:1])
+
+
+def middle_second(l1, w2, w3, bias, rows, l2, l3):
+    lines = l1.shape[1] // rows - 2
+    half = l3.shape[2]
     for x in range(l2.shape[0]):
-        l2[x] = conv(l1, x, lines - 2, w2[...], bias[1:2])
+        l2[x] = conv(l1, x, rows, lines, w2[...], bias[1:2])
     for x in range(l3.shape[0]):
-        l3[x] = conv(l2, x, lines - 4, w3[...], bias[2:3])[:, : l3.shape[2]]
+        y = conv(l2, x, rows, lines - 2, w3[...], bias[2:3])
+        for i in range(lines - 2):
+            l3[x, i] = y[i * rows : i * rows + half]
 
 
 def spread_pattern(half, nz):
@@ -161,48 +188,45 @@
     return hit.astype(F32).astype(BF16)
 
 
-def edge_strip(below, own, xm, xp, ym, cm, cp, l1, l2, ws, bias, s0, s1, s2):
-    nx, ny, rows, _ = own.shape
-    h = HALO
-    inner = slice(0, 2) if below else slice(ny - 2, ny)
-    near = slice(3, 5) if below else slice(0, 2)
-    far = slice(0, 3) if below else slice(2, 5)
-    for planes, core, side in (
-        (slice(0, h), xm, cm),
-        (slice(h, h + nx), own, ym),
-        (slice(h + nx, h + nx + h), xp, cp),
-    ):
-        s0[planes, near, :rows] = core[:, inner]
-        s0[planes, far, :rows] = side[...]
-    n1, n2 = l1.shape[1], l2.shape[1]
-    s1[:, near] = l1[:, :2] if below else l1[:, n1 - 2 :]
-    s2[:, near] = l2[:, :2] if below else l2[:, n2 - 2 :]
+def edge_strip(below, near, side, cm, cp, l1, l2, ws, bias, s0, s1, s2):
+    nx, h, rows, line = side.shape
+    close = slice(3 * rows, 5 * rows) if below else slice(0, 2 * rows)
+    far = slice(0, 3 * rows) if below else slice(2 * rows, 5 * rows)
+    part = slice(0, 2 * rows) if below else slice(2 * rows, 4 * rows)
+    end1 = part if below else slice(l1.shape[1] - 2 * rows, l1.shape[1])
+    end2 = part if below else slice(l2.shape[1] - 2 * rows, l2.shape[1])
+    s0[:, close] = near[:, part]
+    s0[:h, far] = cm[...].reshape(h, h * rows, line)
+    s0[h : h + nx, far] = side[...].reshape(nx, h * rows, line)
+    s0[h + nx :, far] = cp[...].reshape(h, h * rows, line)
+    s1[:, close] = l1[:, end1]
+    s2[:, close] = l2[:, end2]
     for source, target, i in ((s0, s1, 0), (s1, s2, 1)):
         for x in range(source.shape[0] - 2):
-            target[x, far] = conv(source, x, 3, ws[i][...], bias[i : i + 1])
-    return [conv(s2, x, 3, ws[2][...], bias[2:3]) for x in range(nx)]
-
-
-def lower_kernel(own, xm, xp, ym, cm, cp, l1, l2, w1, w2, w3, bias, low, s0, s1, s2):
-    y = edge_strip(
-        True, own, xm, xp, ym, cm, cp, l1, l2, (w1, w2, w3), bias, s0, s1, s2
-    )
+            target[x, far] = conv(source, x, rows, 3, ws[i][...], bias[i : i + 1])
+    return [conv(s2, x, rows, 3, ws[2][...], bias[2:3]) for x in range(nx)]
+
+
+def lower_kernel(near, ym, cm, cp, l1, l2, w1, w2, w3, bias, low, s0, s1, s2):
+    rows = ym.shape[2]
+    half = low.shape[2]
+    y = edge_strip(True, near, ym, cm, cp, l1, l2, (w1, w2, w3), bias, s0, s1, s2)
     for x, lines in enumerate(y):
-        low[x] = lines[:, : low.shape[2]]
+        for i in range(3):
+            low[x, i] = lines[i * rows : i * rows + half]
 
 
 def upper_kernel(
-    own, xm, xp, yp, cm, cp, l1, l2, low, mid, w1, w2, w3, bias, out, s0, s1, s2, stage
+    near, yp, cm, cp, l1, l2, low, mid, w1, w2, w3, bias, out, s0, s1, s2, stage
 ):
     c, nx, ny, nz = out.shape
+    rows = yp.shape[2]
     half = nz // 2
-    y = edge_strip(
-        False, own, xm, xp, yp, cm, cp, l1, l2, (w1, w2, w3), bias, s0, s1, s2
-    )
+    y = edge_strip(False, near, yp, cm, cp, l1, l2, (w1, w2, w3), bias, s0, s1, s2)
     pattern = spread_pattern(half, nz)
     for x in range(nx):
         lines = [low[x, i] for i in range(3)] + [mid[x, i] for i in range(ny - 6)]
-        lines += [y[x][i, :half] for i in range(3)]
+        lines += [y[x][i * rows : i * rows + half] for i in range(3)]
         for first in range(0, ny, 4):
             r = lax.dot_general(
                 jnp.concatenate(lines[first : first + 4], axis=0),
@@ -229,13 +253,14 @@
     field = field[0]
     c, nx, ny, nz = field.shape
     rows = around((nz + 2 * h) // 2, 8)
-    pad = around(rows, 16)
     half = nz // 2
     line = 2 * c
 
-    pairs, edges = call(
+    xface = ((h, ny, rows, line), BF16)
+    yface = ((nx, h, rows, line), BF16)
+    pairs, edges, xu, xd = call(
         rows_kernel,
-        [((nx, ny, rows, line), BF16), ((nx, ny, 4, line), BF16)],
+        [((nx, ny, rows, line), BF16), ((nx, ny, 4, line), BF16), xface, xface],
         [pltpu.VMEM((nx, c * ny, nz), F32)],
     )(field)
     if lax.axis_size("gz") == 2:
@@ -245,15 +270,18 @@
             [shift(edges[:, :, :2], "gz", True), shift(edges[:, :, 2:], "gz", False)],
             axis=2,
         )
-    xface = ((h, ny, rows, line), BF16)
-    yface = ((nx, h, rows, line), BF16)
-    own, xu, xd, yu, yd = call(
+    xm = shift(xu, "gx", True)
+    xp = shift(xd, "gx", False)
+    own, yu, yd, eu, ed = call(
         faces_kernel,
-        [((nx, ny, rows, line), BF16), xface, xface, yface, yface],
+        [
+            ((nx, ny * rows, line), BF16), yface, yface,
+            ((h, ny, 4, line), BF16), ((h, ny, 4, line), BF16),
+        ],
         [pltpu.VMEM((nx, ny, 8, line), F32)],
     )(pairs, edges)
-    xm = shift(xu, "gx", True)
-    xp = shift(xd, "gx", False)
+    em = shift(eu, "gx", True)
+    ep = shift(ed, "gx", False)
     ym = shift(yu, "gy", True)
     yp = shift(yd, "gy", False)
     cmm = shift(ym[nx - h :], "gx", True)
@@ -269,30 +297,46 @@
         kernel_one, kernel_two, kernel_three,
         bias_one[None], bias_two[None], bias_three[None],
     )
-    (l1,) = call(
+    (l1own,) = call(
+        lambda o, w, b, l: middle_own(o, w, b, rows, l),
+        [((nx - 2, (ny - 2) * rows, line), BF16)],
+        flops=10**9,
+        nbytes=10**6,
+    )(own, w1, bias)
+    l1, near = call(
         middle_first,
-        [((nx + 4, ny - 2, pad, line), BF16)],
-        [pltpu.VMEM((nx + 6, ny, pad, line), BF16)],
-        flops=3 * 10**9,
+        [
+            ((nx + 4, (ny - 2) * rows, line), BF16),
+            ((nx + 6, 4 * rows, line), BF16),
+        ],
+        [
+            pltpu.VMEM((nx + 6, ny * rows, line), BF16),
+            pltpu.VMEM((h, ny, 8, line), F32),
+        ],
+        flops=2 * 10**9,
         nbytes=10**6,
-    )(own, xm, xp, w1, bias)
+    )(own, xm, xp, em, ep, l1own, w1, bias)
     l2, l3 = call(
-        middle_second,
-        [((nx + 2, ny - 4, pad, line), BF16), ((nx, ny - 6, half, line), BF16)],
+        lambda a, v, w, b, o, p: middle_second(a, v, w, b, rows, o, p),
+        [
+            ((nx + 2, (ny - 4) * rows, line), BF16),
+            ((nx, ny - 6, half, line), BF16),
+        ],
         flops=2 * 10**9,
         nbytes=10**6,
     )(l1, w2, w3, bias)
-    strips = [pltpu.VMEM((nx + k, 5, pad, line), BF16) for k in (6, 4, 2)]
+    deep = around(3 * rows, 16) + 2 * rows
+    strips = [pltpu.VMEM((nx + k, deep, line), BF16) for k in (6, 4, 2)]
     (low,) = call(
         lower_kernel, [((nx, 3, half, line), BF16)], strips,
         flops=4 * 10**9, nbytes=10**6,
-    )(own, xm, xp, ym, cmm, cpm, l1, l2, w1, w2, w3, bias)
+    )(near, ym, cmm, cpm, l1, l2, w1, w2, w3, bias)
     (out,) = call(
         upper_kernel,
         [((c, nx, ny, nz), BF16)],
         strips + [pltpu.VMEM((nx, c * ny, nz), F32)],
         flops=4 * 10**9, nbytes=10**6,
-    )(own, xm, xp, yp, cmp, cpp, l1, l2, low, l3, w1, w2, w3, bias)
+    )(near, yp, cmp, cpp, l1, l2, low, l3, w1, w2, w3, bias)
     return out[None]
 
 

time: 38.6 us -> 36.1 us (0.935)
  the two profiles are of different devices: /device:TPU:1 before, /device:TPU:0 now
where the time goes in v4:
time: 36.1 us; the launch traced here: 35.9 us
  Pallas kernels  14.2 us (39%)
  starting transfers between devices  12.8 us (35%)
  waiting for transfers between devices  6.02 us (17%)
  local copies, waits for them, and re-layouts  2.81 us (8%)
    pallas_call x8, Pallas kernels, run(): pl.pallas_call(kernel, out_shape=outs, in_specs=[VMEM] * len(args), out_s...  14.2 us
    ppermute x11, starting transfers between devices, shift(): return lax.ppermute(x, axis, pairs)  12.8 us
    ppermute x11, waiting for transfers between devices, shift(): return lax.ppermute(x, axis, pairs)  6.02 us
    unnamed x14, local copies, waits for them, and re-layouts  2.73 us
  transfers between devices with their start and end apart: 11, of which 4 were waited for; matrix products, arithmetic and copies ran while one was open for 0% of the time, Pallas kernels for 25%

profile of v4, /device:TPU:0, one launch (start us, length us, event | category | flops | bytes accessed | tf_op | source)
XLA Modules:
  0.0 35.9 jit_solution(7462890594908587230)
XLA Ops:
  0.0 0.0 copy-start
  0.0 1.0 %copy-done = bf16[1,64,4,8,128]{4,3,2,1,0:T(8,128)(2,1)S(1)} copy-done((bf16[1,64,4,8,128]{4,3,2,1,0:T(8,128)(2,1)S(1)}, bf16[1,64,4,8,128]{4,3,2,1,0:T(8,128)(2,1)}, u32[]{:S(2)}) %copy-start) | copy-done | bytes 524312
  1.0 0.0 copy-start.2
  1.0 0.8 %shard_map.73 = (bf16[4,8,72,128]{3,2,1,0:T(8,128)(2,1)S(1)}, bf16[4,8,4,128]{3,2,1,0:T(4,128)(2,1)S(1)}, bf16[3,8,72,128]{3,2,1,0:T(8,128)(2,1)S(1)}, bf16[3,8,72,128]{3,2,1,0:T(8,128)(2,1)S(1)}) custom-call(bf16[64,4,8,128]{3,2,1,0:T(8,128)(2,1)S(1)} %bitcast.5), custom_call_target="tpu_custom_call" | custom-call | tf_op jit(solution)/shard_map/pallas_call | solution.py:24
  1.8 0.0 copy-start.1
  1.8 3.1 %collective-permute-start = (bf16[4,8,4,128]{3,2,1,0:T(4,128)(2,1)S(1)}, bf16[4,8,4,128]{3,2,1,0:T(4,128)(2,1)S(1)}, u32[]{:S(2)}, u32[]{:S(2)}) collective-permute-start(bf16[4,8,4,128]{3,2,1,0:T(4,128)(2,1)S(1)} %get-tuple-element.23), channel_id=1, source_target_pairs={{0,1},{1,0},{2,3},{3,2},{4,5},{5,4},{6,7},{7,6},{8,9},{9,8},{10,11... | collective-permute-start | bytes 98312 | tf_op jit(solution)/shard_map/ppermute | solution.py:248
  4.9 0.0 collective-permute-start.1
  4.9 1.7 %collective-permute-start.2 = (bf16[3,8,72,128]{3,2,1,0:T(8,128)(2,1)S(1)}, bf16[3,8,72,128]{3,2,1,0:T(8,128)(2,1)S(1)}, u32[]{:S(2)}, u32[]{:S(2)}) collective-permute-start(bf16[3,8,72,128]{3,2,1,0:T(8,128)(2,1)S(1)} %get-tuple-element.26), channel_id=1, source_target_pairs={{8,0},{16,8},{24,16},{0,24},{9,1},{17,9},{25,17},{1,25},{10,2},{18... | collective-permute-start | bytes 1327112 | tf_op jit(solution)/shard_map/ppermute | solution.py:248
  6.7 0.1 collective-permute-done.edges
  6.8 0.2 shard_map.74
  7.0 2.1 %collective-permute-start.8 = (bf16[4,3,72,128]{3,2,1,0:T(8,128)(2,1)S(1)}, bf16[4,3,72,128]{3,2,1,0:T(8,128)(2,1)S(1)}, u32[]{:S(2)}, u32[]{:S(2)}) collective-permute-start(bf16[4,3,72,128]{3,2,1,0:T(8,128)(2,1)S(1)} %get-tuple-element.37), channel_id=1, source_target_pairs={{0,2},{2,4},{4,6},{6,0},{1,3},{3,5},{5,7},{7,1},{8,10},{10,12},{12... | collective-permute-start | bytes 663560 | tf_op jit(solution)/shard_map/ppermute | solution.py:248
  9.1 0.0 copy-start.4
  9.1 0.0 copy-start.5
  9.1 0.0 copy-start.6
  9.1 0.0 copy-done.2
  9.1 0.0 copy-done.1
  9.1 0.6 %copy-done.4 = f32[64]{0:T(128)S(1)} copy-done((f32[64]{0:T(128)S(1)}, f32[64]{0:T(128)}, u32[]{:S(2)}) %copy-start.4) | copy-done | bytes 280
  9.8 0.0 copy-done.5
  9.8 0.0 copy-done.6
  9.8 0.0 copy-start.3
  9.8 1.0 %copy-done.3 = bf16[3,3,3,64,64]{4,3,2,1,0:T(8,128)(2,1)S(1)} copy-done((bf16[3,3,3,64,64]{4,3,2,1,0:T(8,128)(2,1)S(1)}, bf16[3,3,3,64,64]{4,3,2,1,0:T(8,128)(2,1)}, u32[]{:S(2)}) %copy-start.3) | copy-done | bytes 221208
  10.8 1.1 %shard_map.75 = (bf16[1152,256]{1,0:T(8,128)(2,1)S(1)}, bf16[1152,256]{1,0:T(8,128)(2,1)S(1)}, bf16[1152,256]{1,0:T(8,128)(2,1)S(1)}, f32[3,128]{1,0:T(4,128)S(1)}) custom-call(bf16[3,3,3,64,64]{4,3,2,1,0:T(8,128)(2,1)S(1)} %copy-done.1, bf16[3,3,3,64,64]{4,3,2,1,0:T(8,128)(2,1)S(1)} %copy-done.2, bf16[3,3,3,64,64]{4,3,2,1,0:T(8,128)(2,1)S(1)} %copy-done.3, ...), custom_call_target="tpu_custom_call" | custom-call | flops 2000000000 | bytes 1000000 | tf_op jit(solution)/shard_map/pallas_call | solution.py:24
  12.0 0.1 collective-permute-start.3
  12.0 1.7 %collective-permute-start.4 = (bf16[3,8,4,128]{3,2,1,0:T(4,128)(2,1)S(1)}, bf16[3,8,4,128]{3,2,1,0:T(4,128)(2,1)S(1)}, u32[]{:S(2)}, u32[]{:S(2)}) collective-permute-start(bf16[3,8,4,128]{3,2,1,0:T(4,128)(2,1)S(1)} %get-tuple-element.28), channel_id=1, source_target_pairs={{8,0},{16,8},{24,16},{0,24},{9,1},{17,9},{25,17},{1,25},{10,2},{18... | collective-permute-start | bytes 73736 | tf_op jit(solution)/shard_map/ppermute | solution.py:248
  13.8 0.8 %shard_map.76.l1own = bf16[2,432,128]{2,1,0:T(8,128)(2,1)S(1)} custom-call(bf16[4,576,128]{2,1,0:T(8,128)(2,1)S(1)} %get-tuple-element.24.o.own, bf16[1152,256]{1,0:T(8,128)(2,1)S(1)} %get-tuple-element.29.w.w1, f32[3,128]{1,0:T(4,128)S(1)} %get-tuple-element.30.b.bias), custom_call_target="tpu_custom_call" | custom-call | flops 1000000000 | bytes 1000000 | tf_op jit(solution)/shard_map/pallas_call | solution.py:24
  14.5 1.4 %collective-permute-done.8.ym = bf16[4,3,72,128]{3,2,1,0:T(8,128)(2,1)S(1)} collective-permute-done((bf16[4,3,72,128]{3,2,1,0:T(8,128)(2,1)S(1)}, bf16[4,3,72,128]{3,2,1,0:T(8,128)(2,1)S(1)}, u32[]{:S(2)}, u32[]{:S(2)}) %collective-permute-start.8) | collective-permute-done | bytes 221216 | tf_op jit(solution)/shard_map/ppermute | solution.py:248
  15.9 1.7 %collective-permute-start.5 = (bf16[4,3,72,128]{3,2,1,0:T(8,128)(2,1)S(1)}, bf16[4,3,72,128]{3,2,1,0:T(8,128)(2,1)S(1)}, u32[]{:S(2)}, u32[]{:S(2)}) collective-permute-start(bf16[4,3,72,128]{3,2,1,0:T(8,128)(2,1)S(1)} %get-tuple-element.32), channel_id=1, source_target_pairs={{2,0},{4,2},{6,4},{0,6},{3,1},{5,3},{7,5},{1,7},{10,8},{12,10},{14... | collective-permute-start | bytes 663560 | tf_op jit(solution)/shard_map/ppermute | solution.py:248
  17.7 4.2 %collective-permute-done.5.yp = bf16[4,3,72,128]{3,2,1,0:T(8,128)(2,1)S(1)} collective-permute-done((bf16[4,3,72,128]{3,2,1,0:T(8,128)(2,1)S(1)}, bf16[4,3,72,128]{3,2,1,0:T(8,128)(2,1)S(1)}, u32[]{:S(2)}, u32[]{:S(2)}) %collective-permute-start.5) | collective-permute-done | bytes 221216 | tf_op jit(solution)/shard_map/ppermute | solution.py:248
  21.9 0.0 collective-permute-start.10
  22.0 0.0 collective-permute-done.3.em
  22.0 0.6 %collective-permute-start.9 = (bf16[3,3,72,128]{3,2,1,0:T(8,128)(2,1)S(1)}, bf16[3,3,72,128]{3,2,1,0:T(8,128)(2,1)S(1)}, u32[]{:S(2)}, u32[]{:S(2)}) collective-permute-start(bf16[3,3,72,128]{3,2,1,0:T(8,128)(2,1)S(1)} %get-tuple-element.40), channel_id=1, source_target_pairs={{0,8},{8,16},{16,24},{24,0},{1,9},{9,17},{17,25},{25,1},{2,10},{10... | collective-permute-start | bytes 497672 | tf_op jit(solution)/shard_map/ppermute | solution.py:248
  22.5 0.0 collective-permute-done.4.ep
  22.5 0.5 %collective-permute-start.6 = (bf16[3,3,72,128]{3,2,1,0:T(8,128)(2,1)S(1)}, bf16[3,3,72,128]{3,2,1,0:T(8,128)(2,1)S(1)}, u32[]{:S(2)}, u32[]{:S(2)}) collective-permute-start(bf16[3,3,72,128]{3,2,1,0:T(8,128)(2,1)S(1)} %get-tuple-element.42), channel_id=1, source_target_pairs={{0,8},{8,16},{16,24},{24,0},{1,9},{9,17},{17,25},{25,1},{2,10},{10... | collective-permute-start | bytes 497672 | tf_op jit(solution)/shard_map/ppermute | solution.py:248
  23.1 0.0 collective-permute-done.1.xm
  23.1 1.2 %collective-permute-start.7 = (bf16[3,3,72,128]{3,2,1,0:T(8,128)(2,1)S(1)}, bf16[3,3,72,128]{3,2,1,0:T(8,128)(2,1)S(1)}, u32[]{:S(2)}, u32[]{:S(2)}) collective-permute-start(bf16[3,3,72,128]{3,2,1,0:T(8,128)(2,1)S(1)} %get-tuple-element.41), channel_id=1, source_target_pairs={{8,0},{16,8},{24,16},{0,24},{9,1},{17,9},{25,17},{1,25},{10,2},{18... | collective-permute-start | bytes 497672 | tf_op jit(solution)/shard_map/ppermute | solution.py:248
  24.3 0.0 collective-permute-done.2.xp
  24.3 2.2 %shard_map.77 = (bf16[8,432,128]{2,1,0:T(8,128)(2,1)S(1)}, bf16[10,288,128]{2,1,0:T(8,128)(2,1)S(1)}) custom-call(bf16[4,576,128]{2,1,0:T(8,128)(2,1)S(1)} %get-tuple-element.24.o.own, bf16[3,8,72,128]{3,2,1,0:T(8,128)(2,1)S(1)} %collective-permute-done.1.xm, bf16[3,8,72,128]{3,2,1,0:T(8,128)(2,1)S(1)} %collective-permute-done.2.xp, ...), custom_call_target="tpu_custom_call" | custom-call | flops 2000000000 | bytes 1000000 | tf_op jit(solution)/shard_map/pallas_call | solution.py:24
  26.5 1.8 %shard_map.78 = (bf16[6,288,128]{2,1,0:T(8,128)(2,1)S(1)}, bf16[4,2,64,128]{3,2,1,0:T(8,128)(2,1)S(1)}) custom-call(bf16[8,432,128]{2,1,0:T(8,128)(2,1)S(1)} %get-tuple-element.33.a.l1, bf16[1152,256]{1,0:T(8,128)(2,1)S(1)} %get-tuple-element.34.v.w2, bf16[1152,256]{1,0:T(8,128)(2,1)S(1)} %get-tuple-element.35.w.w3, f32[3,128]{1,0:T(4,128)S(1)} %get-tuple-element.30.b.bias), custom_call_target="tpu_custom_call" | custom-call | flops 2000000000 | bytes 1000000 | tf_op jit(solution)/shard_map/pallas_call | solution.py:24
  28.3 0.0 collective-permute-done.10.cp
  28.3 0.3 collective-permute-done.9.cm
  28.6 3.0 %shard_map.79.low = bf16[4,3,64,128]{3,2,1,0:T(8,128)(2,1)S(1)} custom-call(bf16[10,288,128]{2,1,0:T(8,128)(2,1)S(1)} %get-tuple-element.31.near, bf16[4,3,72,128]{3,2,1,0:T(8,128)(2,1)S(1)} %collective-permute-done.8.ym, bf16[3,3,72,128]{3,2,1,0:T(8,128)(2,1)S(1)} %collective-permute-done.9.cm, bf16[3,3,72,128]{3,2,1,0:T(8,128)(2,1)S(1)} %collective-permute-done.10.cp, ...), custom_call_target="tpu_custom_call" | custom-call | flops 4000000000 | bytes 1000000 | tf_op jit(solution)/shard_map/pallas_call | solution.py:24
  31.5 0.0 collective-permute-done.6.cm
  31.6 0.0 collective-permute-done.7.cp
  31.6 4.3 %shard_map.80 = bf16[64,4,8,128]{3,2,1,0:T(8,128)(2,1)} custom-call(bf16[10,288,128]{2,1,0:T(8,128)(2,1)S(1)} %get-tuple-element.31.near, bf16[4,3,72,128]{3,2,1,0:T(8,128)(2,1)S(1)} %collective-permute-done.5.yp, bf16[3,3,72,128]{3,2,1,0:T(8,128)(2,1)S(1)} %collective-permute-done.6.cm, bf16[3,3,72,128]{3,2,1,0:T(8,128)(2,1)S(1)} %collective-permute-done.7.cp, ...), custom_call_target="tpu_custom_call" | custom-call | flops 4000000000 | bytes 1000000 | tf_op jit(solution)/shard_map/pallas_call | solution.py:24
  (2 shorter events, 0.1 us)
Async XLA Ops:
  0.0 1.0 %copy-start = (bf16[1,64,4,8,128]{4,3,2,1,0:T(8,128)(2,1)S(1)}, bf16[1,64,4,8,128]{4,3,2,1,0:T(8,128)(2,1)}, u32[]{:S(2)}) copy-start(bf16[1,64,4,8,128]{4,3,2,1,0:T(8,128)(2,1)} %param.7) | copy-start | bytes 1572868
  1.0 8.1 %copy-start.2 = (bf16[3,3,3,64,64]{4,3,2,1,0:T(8,128)(2,1)S(1)}, bf16[3,3,3,64,64]{4,3,2,1,0:T(8,128)(2,1)}, u32[]{:S(2)}) copy-start(bf16[3,3,3,64,64]{4,3,2,1,0:T(8,128)(2,1)} %k2.1) | copy-start | bytes 663556
  1.8 7.3 %copy-start.1 = (bf16[3,3,3,64,64]{4,3,2,1,0:T(8,128)(2,1)S(1)}, bf16[3,3,3,64,64]{4,3,2,1,0:T(8,128)(2,1)}, u32[]{:S(2)}) copy-start(bf16[3,3,3,64,64]{4,3,2,1,0:T(8,128)(2,1)} %k1.1) | copy-start | bytes 663556
  1.8 5.0 %collective-permute-start = (bf16[4,8,4,128]{3,2,1,0:T(4,128)(2,1)S(1)}, bf16[4,8,4,128]{3,2,1,0:T(4,128)(2,1)S(1)}, u32[]{:S(2)}, u32[]{:S(2)}) collective-permute-start(bf16[4,8,4,128]{3,2,1,0:T(4,128)(2,1)S(1)} %get-tuple-element.23), channel_id=1, source_target_pairs={{0,1},{1,0},{2,3},{3,2},{4,5},{5,4},{6,7},{7,6},{8,9},{9,8},{10,11... | collective-permute-start | bytes 98312 | tf_op jit(solution)/shard_map/ppermute | solution.py:248
  4.9 18.2 %collective-permute-start.1 = (bf16[3,8,72,128]{3,2,1,0:T(8,128)(2,1)S(1)}, bf16[3,8,72,128]{3,2,1,0:T(8,128)(2,1)S(1)}, u32[]{:S(2)}, u32[]{:S(2)}) collective-permute-start(bf16[3,8,72,128]{3,2,1,0:T(8,128)(2,1)S(1)} %get-tuple-element.25), channel_id=1, source_target_pairs={{0,8},{8,16},{16,24},{24,0},{1,9},{9,17},{17,25},{25,1},{2,10},{10... | collective-permute-start | bytes 1327112 | tf_op jit(solution)/shard_map/ppermute | solution.py:248
  4.9 19.4 %collective-permute-start.2 = (bf16[3,8,72,128]{3,2,1,0:T(8,128)(2,1)S(1)}, bf16[3,8,72,128]{3,2,1,0:T(8,128)(2,1)S(1)}, u32[]{:S(2)}, u32[]{:S(2)}) collective-permute-start(bf16[3,8,72,128]{3,2,1,0:T(8,128)(2,1)S(1)} %get-tuple-element.26), channel_id=1, source_target_pairs={{8,0},{16,8},{24,16},{0,24},{9,1},{17,9},{25,17},{1,25},{10,2},{18... | collective-permute-start | bytes 1327112 | tf_op jit(solution)/shard_map/ppermute | solution.py:248
  7.0 9.0 %collective-permute-start.8 = (bf16[4,3,72,128]{3,2,1,0:T(8,128)(2,1)S(1)}, bf16[4,3,72,128]{3,2,1,0:T(8,128)(2,1)S(1)}, u32[]{:S(2)}, u32[]{:S(2)}) collective-permute-start(bf16[4,3,72,128]{3,2,1,0:T(8,128)(2,1)S(1)} %get-tuple-element.37), channel_id=1, source_target_pairs={{0,2},{2,4},{4,6},{6,0},{1,3},{3,5},{5,7},{7,1},{8,10},{10,12},{12... | collective-permute-start | bytes 663560 | tf_op jit(solution)/shard_map/ppermute | solution.py:248
  9.1 0.7 %copy-start.4 = (f32[64]{0:T(128)S(1)}, f32[64]{0:T(128)}, u32[]{:S(2)}) copy-start(f32[64]{0:T(128)} %param.9) | copy-start | bytes 772
  9.1 0.7 %copy-start.5 = (f32[64]{0:T(128)S(1)}, f32[64]{0:T(128)}, u32[]{:S(2)}) copy-start(f32[64]{0:T(128)} %param.11) | copy-start | bytes 772
  9.1 0.7 %copy-start.6 = (f32[64]{0:T(128)S(1)}, f32[64]{0:T(128)}, u32[]{:S(2)}) copy-start(f32[64]{0:T(128)} %param.13) | copy-start | bytes 772
  9.8 1.0 %copy-start.3 = (bf16[3,3,3,64,64]{4,3,2,1,0:T(8,128)(2,1)S(1)}, bf16[3,3,3,64,64]{4,3,2,1,0:T(8,128)(2,1)}, u32[]{:S(2)}) copy-start(bf16[3,3,3,64,64]{4,3,2,1,0:T(8,128)(2,1)} %k3.1) | copy-start | bytes 663556
  12.0 10.0 %collective-permute-start.3 = (bf16[3,8,4,128]{3,2,1,0:T(4,128)(2,1)S(1)}, bf16[3,8,4,128]{3,2,1,0:T(4,128)(2,1)S(1)}, u32[]{:S(2)}, u32[]{:S(2)}) collective-permute-start(bf16[3,8,4,128]{3,2,1,0:T(4,128)(2,1)S(1)} %get-tuple-element.27), channel_id=1, source_target_pairs={{0,8},{8,16},{16,24},{24,0},{1,9},{9,17},{17,25},{25,1},{2,10},{10... | collective-permute-start | bytes 73736 | tf_op jit(solution)/shard_map/ppermute | solution.py:248
  12.0 10.5 %collective-permute-start.4 = (bf16[3,8,4,128]{3,2,1,0:T(4,128)(2,1)S(1)}, bf16[3,8,4,128]{3,2,1,0:T(4,128)(2,1)S(1)}, u32[]{:S(2)}, u32[]{:S(2)}) collective-permute-start(bf16[3,8,4,128]{3,2,1,0:T(4,128)(2,1)S(1)} %get-tuple-element.28), channel_id=1, source_target_pairs={{8,0},{16,8},{24,16},{0,24},{9,1},{17,9},{25,17},{1,25},{10,2},{18... | collective-permute-start | bytes 73736 | tf_op jit(solution)/shard_map/ppermute | solution.py:248
  15.9 6.0 %collective-permute-start.5 = (bf16[4,3,72,128]{3,2,1,0:T(8,128)(2,1)S(1)}, bf16[4,3,72,128]{3,2,1,0:T(8,128)(2,1)S(1)}, u32[]{:S(2)}, u32[]{:S(2)}) collective-permute-start(bf16[4,3,72,128]{3,2,1,0:T(8,128)(2,1)S(1)} %get-tuple-element.32), channel_id=1, source_target_pairs={{2,0},{4,2},{6,4},{0,6},{3,1},{5,3},{7,5},{1,7},{10,8},{12,10},{14... | collective-permute-start | bytes 663560 | tf_op jit(solution)/shard_map/ppermute | solution.py:248
  21.9 6.4 %collective-permute-start.10 = (bf16[3,3,72,128]{3,2,1,0:T(8,128)(2,1)S(1)}, bf16[3,3,72,128]{3,2,1,0:T(8,128)(2,1)S(1)}, u32[]{:S(2)}, u32[]{:S(2)}) collective-permute-start(bf16[3,3,72,128]{3,2,1,0:T(8,128)(2,1)S(1)} %get-tuple-element.39), channel_id=1, source_target_pairs={{8,0},{16,8},{24,16},{0,24},{9,1},{17,9},{25,17},{1,25},{10,2},{18... | collective-permute-start | bytes 497672 | tf_op jit(solution)/shard_map/ppermute | solution.py:248
  22.0 6.6 %collective-permute-start.9 = (bf16[3,3,72,128]{3,2,1,0:T(8,128)(2,1)S(1)}, bf16[3,3,72,128]{3,2,1,0:T(8,128)(2,1)S(1)}, u32[]{:S(2)}, u32[]{:S(2)}) collective-permute-start(bf16[3,3,72,128]{3,2,1,0:T(8,128)(2,1)S(1)} %get-tuple-element.40), channel_id=1, source_target_pairs={{0,8},{8,16},{16,24},{24,0},{1,9},{9,17},{17,25},{25,1},{2,10},{10... | collective-permute-start | bytes 497672 | tf_op jit(solution)/shard_map/ppermute | solution.py:248
  22.5 9.0 %collective-permute-start.6 = (bf16[3,3,72,128]{3,2,1,0:T(8,128)(2,1)S(1)}, bf16[3,3,72,128]{3,2,1,0:T(8,128)(2,1)S(1)}, u32[]{:S(2)}, u32[]{:S(2)}) collective-permute-start(bf16[3,3,72,128]{3,2,1,0:T(8,128)(2,1)S(1)} %get-tuple-element.42), channel_id=1, source_target_pairs={{0,8},{8,16},{16,24},{24,0},{1,9},{9,17},{17,25},{25,1},{2,10},{10... | collective-permute-start | bytes 497672 | tf_op jit(solution)/shard_map/ppermute | solution.py:248
  23.1 8.5 %collective-permute-start.7 = (bf16[3,3,72,128]{3,2,1,0:T(8,128)(2,1)S(1)}, bf16[3,3,72,128]{3,2,1,0:T(8,128)(2,1)S(1)}, u32[]{:S(2)}, u32[]{:S(2)}) collective-permute-start(bf16[3,3,72,128]{3,2,1,0:T(8,128)(2,1)S(1)} %get-tuple-element.41), channel_id=1, source_target_pairs={{8,0},{16,8},{24,16},{0,24},{9,1},{17,9},{25,17},{1,25},{10,2},{18... | collective-permute-start | bytes 497672 | tf_op jit(solution)/shard_map/ppermute | solution.py:248

commit v5 on v4

--- a/solution.py
+++ b/solution.py
@@ -17,20 +17,24 @@
     return -(-size // step) * step
 
 
-def call(kernel, outs, scratch=(), flops=0, nbytes=0):
+def call(kernel, outs, scratch=(), flops=0, nbytes=0, far=0):
     outs = [jax.ShapeDtypeStruct(s, d) for s, d in outs]
 
     def run(*args):
+        args = list(args)
+        for i in range(len(args) - far, len(args)):
+            args[i] = pltpu.with_memory_space_constraint(args[i], pltpu.HBM)
         return pl.pallas_call(
             kernel,
             out_shape=outs,
-            in_specs=[VMEM] * len(args),
+            in_specs=[VMEM] * (len(args) - far)
+            + [pl.BlockSpec(memory_space=pltpu.HBM)] * far,
             out_specs=[VMEM] * len(outs),
             scratch_shapes=list(scratch),
             cost_estimate=pl.CostEstimate(
                 flops=flops, bytes_accessed=nbytes, transcendentals=0
             ),
-            compiler_params=pltpu.CompilerParams(vmem_limit_bytes=48 * 1024 * 1024),
+            compiler_params=pltpu.CompilerParams(vmem_limit_bytes=24 * 1024 * 1024),
         )(*args)
 
     return run
@@ -42,6 +46,10 @@
 
 def iota(shape, dim):
     return lax.broadcasted_iota(jnp.int32, shape, dim)
+
+
+def is_even(axis):
+    return lax.rem(lax.axis_index(axis), 2) == 0
 
 
 def rows_kernel(field, pairs, edges, xu, xd, planes):
@@ -93,7 +101,7 @@
     return first, last
 
 
-def faces_kernel(pairs, edges, own, yu, yd, eu, ed, wide):
+def faces_kernel(pairs, edges, own, ya, yb, eu, ed, wide):
     nx, ny, rows, line = pairs.shape
     h = HALO
     first, last = end_rows(pairs, edges, wide)
@@ -102,14 +110,35 @@
     )
     own[...] = e.reshape(nx, ny * rows, line).astype(BF16)
     e = e.astype(BF16)
-    yu[...] = e[:, ny - h :]
-    yd[...] = e[:, :h]
+    even = is_even("gy")
+    head, tail = e[:, :h], e[:, ny - h :]
+
+    @pl.when(even)
+    def _():
+        ya[...] = tail
+        yb[...] = head
+
+    @pl.when(jnp.logical_not(even))
+    def _():
+        ya[...] = head
+        yb[...] = tail
+
     eu[...] = edges[nx - h :]
     ed[...] = edges[:h]
 
 
-def weights_kernel(k1, k2, k3, b1, b2, b3, w1, w2, w3, bias):
+def weights_kernel(
+    k1, k2, k3, b1, b2, b3, w1, w2, w3, bias, pattern, thin, sems
+):
     _, _, taps, o, c = k1.shape
+    copies = [
+        pltpu.make_async_copy(b, thin.at[i], sems.at[i])
+        for i, b in enumerate((b1, b2, b3))
+    ]
+    for copy in copies:
+        copy.start()
+    nz = pattern.shape[1] // 4
+    pattern[...] = spread_pattern(nz // 2, nz)
     j = iota((taps * o, 8 * o), 0)
     n = iota((taps * o, 8 * o), 1)
     p = n // (4 * o)
@@ -128,8 +157,10 @@
                 at = (a * 3 + e) * 2 * c
                 w[at : at + c] = r[:, : 4 * o]
                 w[at + c : at + 2 * c] = r[:, 4 * o :]
-    for i, b in enumerate((b1, b2, b3)):
-        bias[i : i + 1] = jnp.concatenate([b[...], b[...]], axis=1)
+    for copy in copies:
+        copy.wait()
+    for i in range(3):
+        bias[i : i + 1] = jnp.concatenate([thin[i], thin[i]], axis=1)
 
 
 def conv(source, x, rows, lines, weight, bias):
@@ -182,23 +213,25 @@
 
 
 def spread_pattern(half, nz):
-    r = iota((4 * half, 8 * nz), 0)
-    n = iota((4 * half, 8 * nz), 1)
-    hit = (r // half == n // nz % 4) & (n % nz == 2 * (r % half) + n // (4 * nz))
+    r = iota((8 * half, 4 * nz), 0)
+    n = iota((8 * half, 4 * nz), 1)
+    line = r // half % 4
+    hit = (line == n // nz) & (n % nz == 2 * (r % half) + r // (4 * half))
     return hit.astype(F32).astype(BF16)
 
 
-def edge_strip(below, near, side, cm, cp, l1, l2, ws, bias, s0, s1, s2):
+def edge_strip(below, near, side, ca, cb, l1, l2, ws, bias, s0, s1, s2):
     nx, h, rows, line = side.shape
     close = slice(3 * rows, 5 * rows) if below else slice(0, 2 * rows)
     far = slice(0, 3 * rows) if below else slice(2 * rows, 5 * rows)
     part = slice(0, 2 * rows) if below else slice(2 * rows, 4 * rows)
     end1 = part if below else slice(l1.shape[1] - 2 * rows, l1.shape[1])
     end2 = part if below else slice(l2.shape[1] - 2 * rows, l2.shape[1])
+    first = jnp.where(is_even("gx"), h + nx, 0)
     s0[:, close] = near[:, part]
-    s0[:h, far] = cm[...].reshape(h, h * rows, line)
+    s0[pl.ds(first, h), far] = ca[...].reshape(h, h * rows, line)
+    s0[pl.ds(h + nx - first, h), far] = cb[...].reshape(h, h * rows, line)
     s0[h : h + nx, far] = side[...].reshape(nx, h * rows, line)
-    s0[h + nx :, far] = cp[...].reshape(h, h * rows, line)
     s1[:, close] = l1[:, end1]
     s2[:, close] = l2[:, end2]
     for source, target, i in ((s0, s1, 0), (s1, s2, 1)):
@@ -207,44 +240,82 @@
     return [conv(s2, x, rows, 3, ws[2][...], bias[2:3]) for x in range(nx)]
 
 
-def lower_kernel(near, ym, cm, cp, l1, l2, w1, w2, w3, bias, low, s0, s1, s2):
-    rows = ym.shape[2]
-    half = low.shape[2]
-    y = edge_strip(True, near, ym, cm, cp, l1, l2, (w1, w2, w3), bias, s0, s1, s2)
-    for x, lines in enumerate(y):
-        for i in range(3):
-            low[x, i] = lines[i * rows : i * rows + half]
-
-
-def upper_kernel(
-    near, yp, cm, cp, l1, l2, low, mid, w1, w2, w3, bias, out, s0, s1, s2, stage
+def by_side(even_below, body):
+    even = is_even("gy")
+
+    @pl.when(even)
+    def _():
+        body(even_below)
+
+    @pl.when(jnp.logical_not(even))
+    def _():
+        body(not even_below)
+
+
+def first_kernel(near, side, ca, cb, l1, l2, w1, w2, w3, bias, out, s0, s1, s2):
+    rows = side.shape[2]
+    half = out.shape[2]
+
+    def body(below):
+        ws = (w1, w2, w3)
+        y = edge_strip(below, near, side, ca, cb, l1, l2, ws, bias, s0, s1, s2)
+        for x, lines in enumerate(y):
+            for i in range(3):
+                out[x, i] = lines[i * rows : i * rows + half]
+
+    by_side(False, body)
+
+
+def second_kernel(
+    near, side, ca, cb, l1, l2, other, mid, w1, w2, w3, bias, pattern, out,
+    s0, s1, s2, stage,
 ):
     c, nx, ny, nz = out.shape
-    rows = yp.shape[2]
+    rows = side.shape[2]
     half = nz // 2
-    y = edge_strip(False, near, yp, cm, cp, l1, l2, (w1, w2, w3), bias, s0, s1, s2)
-    pattern = spread_pattern(half, nz)
-    for x in range(nx):
-        lines = [low[x, i] for i in range(3)] + [mid[x, i] for i in range(ny - 6)]
-        lines += [y[x][i * rows : i * rows + half] for i in range(3)]
-        for first in range(0, ny, 4):
+
+    def body(below):
+        ws = (w1, w2, w3)
+        y = edge_strip(below, near, side, ca, cb, l1, l2, ws, bias, s0, s1, s2)
+        for x in range(nx):
+            mine = [y[x][i * rows : i * rows + half] for i in range(3)]
+            theirs = [other[x, i] for i in range(3)]
+            inner = [mid[x, i] for i in range(ny - 6)]
+            lines = mine + inner + theirs if below else theirs + inner + mine
+            parts = [
+                jnp.concatenate(lines[first : first + 4], axis=0)
+                for first in range(0, ny, 4)
+            ]
+            sides = [
+                jnp.concatenate([p[:, q * c : (q + 1) * c] for p in parts], axis=1)
+                for q in range(2)
+            ]
             r = lax.dot_general(
-                jnp.concatenate(lines[first : first + 4], axis=0),
-                pattern,
+                jnp.concatenate(sides, axis=0),
+                pattern[...],
                 (((0,), (0,)), ((), ())),
                 preferred_element_type=F32,
             )
-            r = r[:c, : 4 * nz] + r[c:, 4 * nz :]
-            for i in range(4):
-                stage[x, pl.ds(first + i, c, stride=ny), :] = r[
-                    :, i * nz : (i + 1) * nz
+            for i in range(ny):
+                stage[x, pl.ds(i, c, stride=ny), :] = r[
+                    i // 4 * c : (i // 4 + 1) * c, i % 4 * nz : (i % 4 + 1) * nz
                 ]
-        out[:, x] = stage[x].reshape(c, ny, nz).astype(BF16)
+            out[:, x] = stage[x].reshape(c, ny, nz).astype(BF16)
+
+    by_side(True, body)
 
 
 def shift(x, axis, up):
     count = lax.axis_size(axis)
     pairs = [(i, (i + 1) % count) if up else ((i + 1) % count, i) for i in range(count)]
+    return lax.ppermute(x, axis, pairs)
+
+
+def swap(x, axis, first):
+    count = lax.axis_size(axis)
+    assert count % 2 == 0
+    up = 1 if first else -1
+    pairs = [(i, (i + (up if i % 2 == 0 else -up)) % count) for i in range(count)]
     return lax.ppermute(x, axis, pairs)
 
 
@@ -262,6 +333,8 @@
         rows_kernel,
         [((nx, ny, rows, line), BF16), ((nx, ny, 4, line), BF16), xface, xface],
         [pltpu.VMEM((nx, c * ny, nz), F32)],
+        flops=8 * 10**9,
+        nbytes=10**6,
     )(field)
     if lax.axis_size("gz") == 2:
         edges = shift(edges, "gz", True)
@@ -272,31 +345,42 @@
         )
     xm = shift(xu, "gx", True)
     xp = shift(xd, "gx", False)
-    own, yu, yd, eu, ed = call(
+    parameters = (
+        kernel_one, kernel_two, kernel_three,
+        bias_one[None], bias_two[None], bias_three[None],
+    )
+    own, ya, yb, eu, ed = call(
         faces_kernel,
         [
             ((nx, ny * rows, line), BF16), yface, yface,
             ((h, ny, 4, line), BF16), ((h, ny, 4, line), BF16),
         ],
         [pltpu.VMEM((nx, ny, 8, line), F32)],
+        flops=8 * 10**9,
+        nbytes=10**6,
     )(pairs, edges)
     em = shift(eu, "gx", True)
     ep = shift(ed, "gx", False)
-    ym = shift(yu, "gy", True)
-    yp = shift(yd, "gy", False)
-    cmm = shift(ym[nx - h :], "gx", True)
-    cpm = shift(ym[:h], "gx", False)
-    cmp = shift(yp[nx - h :], "gx", True)
-    cpp = shift(yp[:h], "gx", False)
-    w1, w2, w3, bias = call(
+    ya = swap(ya, "gy", True)
+    yb = swap(yb, "gy", False)
+    tail = jnp.where(is_even("gx"), nx - h, 0)
+
+    def planes(side, start):
+        return lax.dynamic_slice_in_dim(side, start, h, axis=0)
+
+    caa = swap(planes(ya, tail), "gx", True)
+    cab = swap(planes(ya, nx - h - tail), "gx", False)
+    cba = swap(planes(yb, tail), "gx", True)
+    cbb = swap(planes(yb, nx - h - tail), "gx", False)
+    w1, w2, w3, bias, pattern = call(
         weights_kernel,
-        [((18 * c, 4 * c), BF16)] * 3 + [((3, line), F32)],
+        [((18 * c, 4 * c), BF16)] * 3
+        + [((3, line), F32), ((4 * nz, 4 * nz), BF16)],
+        [pltpu.VMEM((3, 1, c), F32), pltpu.SemaphoreType.DMA((3,))],
+        far=3,
         flops=2 * 10**9,
         nbytes=10**6,
-    )(
-        kernel_one, kernel_two, kernel_three,
-        bias_one[None], bias_two[None], bias_three[None],
-    )
+    )(*parameters)
     (l1own,) = call(
         lambda o, w, b, l: middle_own(o, w, b, rows, l),
         [((nx - 2, (ny - 2) * rows, line), BF16)],
@@ -327,16 +411,16 @@
     )(l1, w2, w3, bias)
     deep = around(3 * rows, 16) + 2 * rows
     strips = [pltpu.VMEM((nx + k, deep, line), BF16) for k in (6, 4, 2)]
-    (low,) = call(
-        lower_kernel, [((nx, 3, half, line), BF16)], strips,
+    (strip,) = call(
+        first_kernel, [((nx, 3, half, line), BF16)], strips,
         flops=4 * 10**9, nbytes=10**6,
-    )(near, ym, cmm, cpm, l1, l2, w1, w2, w3, bias)
+    )(near, ya, caa, cab, l1, l2, w1, w2, w3, bias)
     (out,) = call(
-        upper_kernel,
+        second_kernel,
         [((c, nx, ny, nz), BF16)],
         strips + [pltpu.VMEM((nx, c * ny, nz), F32)],
         flops=4 * 10**9, nbytes=10**6,
-    )(near, yp, cmp, cpp, l1, l2, low, l3, w1, w2, w3, bias)
+    )(near, yb, cba, cbb, l1, l2, strip, l3, w1, w2, w3, bias, pattern)
     return out[None]
 
 

time: 36.1 us -> 35.2 us (0.975)
  waiting for transfers between devices: 6.02 us -> 2.25 us
  local copies, waits for them, and re-layouts: 2.81 us -> 4.65 us
  starting transfers between devices: 12.8 us -> 13.5 us
    ppermute x0 -> x6, starting transfers between devices: none -> 6.93 us  [swap(): return lax.ppermute(x, axis, pairs)]
    ppermute x11 -> x5, starting transfers between devices: 12.8 us -> 6.59 us  [shift(): return lax.ppermute(x, axis, pairs)]
    ppermute x11 -> x5, waiting for transfers between devices: 6.02 us -> 0.16 us  [shift(): return lax.ppermute(x, axis, pairs)]
    ppermute x0 -> x6, waiting for transfers between devices: none -> 2.09 us  [swap(): return lax.ppermute(x, axis, pairs)]
    unnamed x14 -> x24, local copies, waits for them, and re-layouts: 2.73 us -> 4.55 us
  transfers between devices with their start and end apart: 11 -> 11, of which waited for: 4 -> 4; matrix products, arithmetic and copies ran while one was open for 0% -> 0% of each run, Pallas kernels for 25% -> 27%
where the time goes in v5:
time: 35.2 us; the launch traced here: 35 us
  Pallas kernels  14.5 us (41%)
  starting transfers between devices  13.5 us (38%)
  local copies, waits for them, and re-layouts  4.65 us (13%)
  waiting for transfers between devices  2.25 us (6%)
    pallas_call x8, Pallas kernels, run(): pl.pallas_call(kernel, out_shape=outs, in_specs=[VMEM] * (len(args) - far...  14.5 us
    ppermute x6, starting transfers between devices, swap(): return lax.ppermute(x, axis, pairs)  6.93 us
    ppermute x5, starting transfers between devices, shift(): return lax.ppermute(x, axis, pairs)  6.59 us
    unnamed x24, local copies, waits for them, and re-layouts  4.55 us
    ppermute x6, waiting for transfers between devices, swap(): return lax.ppermute(x, axis, pairs)  2.09 us
  transfers between devices with their start and end apart: 11, of which 4 were waited for; matrix products, arithmetic and copies ran while one was open for 0% of the time, Pallas kernels for 27%

profile of v5, /device:TPU:0, one launch (start us, length us, event | category | flops | bytes accessed | tf_op | source)
XLA Modules:
  0.0 35.0 jit_solution(11495006680801016361)
XLA Ops:
  0.0 0.0 copy-start
  0.0 1.0 %copy-done = bf16[1,64,4,8,128]{4,3,2,1,0:T(8,128)(2,1)S(1)} copy-done((bf16[1,64,4,8,128]{4,3,2,1,0:T(8,128)(2,1)S(1)}, bf16[1,64,4,8,128]{4,3,2,1,0:T(8,128)(2,1)}, u32[]{:S(2)}) %copy-start) | copy-done | bytes 524312
  1.0 0.8 %shard_map.73 = (bf16[4,8,72,128]{3,2,1,0:T(8,128)(2,1)S(1)}, bf16[4,8,4,128]{3,2,1,0:T(4,128)(2,1)S(1)}, bf16[3,8,72,128]{3,2,1,0:T(8,128)(2,1)S(1)}, bf16[3,8,72,128]{3,2,1,0:T(8,128)(2,1)S(1)}) custom-call(bf16[64,4,8,128]{3,2,1,0:T(8,128)(2,1)S(1)} %bitcast.5), custom_call_target="tpu_custom_call" | custom-call | flops 8000000000 | bytes 1000000 | tf_op jit(solution)/shard_map/pallas_call | solution.py:27
  1.8 3.1 %collective-permute-start = (bf16[4,8,4,128]{3,2,1,0:T(4,128)(2,1)S(1)}, bf16[4,8,4,128]{3,2,1,0:T(4,128)(2,1)S(1)}, u32[]{:S(2)}, u32[]{:S(2)}) collective-permute-start(bf16[4,8,4,128]{3,2,1,0:T(4,128)(2,1)S(1)} %get-tuple-element.24), channel_id=1, source_target_pairs={{0,1},{1,0},{2,3},{3,2},{4,5},{5,4},{6,7},{7,6},{8,9},{9,8},{10,11... | collective-permute-start | bytes 98312 | tf_op jit(solution)/shard_map/ppermute | solution.py:311
  4.9 0.0 collective-permute-start.1
  4.9 1.7 %collective-permute-start.2 = (bf16[3,8,72,128]{3,2,1,0:T(8,128)(2,1)S(1)}, bf16[3,8,72,128]{3,2,1,0:T(8,128)(2,1)S(1)}, u32[]{:S(2)}, u32[]{:S(2)}) collective-permute-start(bf16[3,8,72,128]{3,2,1,0:T(8,128)(2,1)S(1)} %get-tuple-element.27), channel_id=1, source_target_pairs={{8,0},{16,8},{24,16},{0,24},{9,1},{17,9},{25,17},{1,25},{10,2},{18... | collective-permute-start | bytes 1327112 | tf_op jit(solution)/shard_map/ppermute | solution.py:311
  6.6 0.1 collective-permute-done.edges
  6.8 0.0 copy-start.1
  6.8 0.0 copy-start.2
  6.8 0.0 copy-start.3
  6.8 0.2 shard_map.74
  7.0 0.0 copy-start.4
  7.0 2.1 %collective-permute-start.8 = (bf16[4,3,72,128]{3,2,1,0:T(8,128)(2,1)S(1)}, bf16[4,3,72,128]{3,2,1,0:T(8,128)(2,1)S(1)}, u32[]{:S(2)}, u32[]{:S(2)}) collective-permute-start(bf16[4,3,72,128]{3,2,1,0:T(8,128)(2,1)S(1)} %get-tuple-element.38), channel_id=1, source_target_pairs={{0,2},{2,0},{4,6},{6,4},{1,3},{3,1},{5,7},{7,5},{8,10},{10,8},{12,... | collective-permute-start | bytes 663560 | tf_op jit(solution)/shard_map/ppermute | solution.py:319
  9.2 2.5 %collective-permute-start.5 = (bf16[4,3,72,128]{3,2,1,0:T(8,128)(2,1)S(1)}, bf16[4,3,72,128]{3,2,1,0:T(8,128)(2,1)S(1)}, u32[]{:S(2)}, u32[]{:S(2)}) collective-permute-start(bf16[4,3,72,128]{3,2,1,0:T(8,128)(2,1)S(1)} %get-tuple-element.33), channel_id=1, source_target_pairs={{0,6},{2,4},{4,2},{6,0},{1,7},{3,5},{5,3},{7,1},{8,14},{10,12},{12... | collective-permute-start | bytes 663560 | tf_op jit(solution)/shard_map/ppermute | solution.py:319
  11.7 0.0 copy-done.1
  11.7 0.0 copy-done.2
  11.7 0.0 copy-done.3
  11.7 1.4 %shard_map.75 = (bf16[1152,256]{1,0:T(8,128)(2,1)S(1)}, bf16[1152,256]{1,0:T(8,128)(2,1)S(1)}, bf16[1152,256]{1,0:T(8,128)(2,1)S(1)}, f32[3,128]{1,0:T(4,128)S(1)}, bf16[512,512]{1,0:T(8,128)(2,1)S(1)}) custom-call(bf16[3,3,3,64,64]{4,3,2,1,0:T(8,128)(2,1)S(1)} %copy-done.1, bf16[3,3,3,64,64]{4,3,2,1,0:T(8,128)(2,1)S(1)} %copy-done.2, ...), custom_call_target="tpu_custom_call" | custom-call | flops 2000000000 | bytes 1000000 | tf_op jit(solution)/shard_map/pallas_call | solution.py:27
  13.0 0.0 copy-done.4
  13.1 0.0 copy-start.6
  13.1 0.8 %copy-done.6 = bf16[1152,256]{1,0:T(8,128)(2,1)} copy-done((bf16[1152,256]{1,0:T(8,128)(2,1)}, bf16[1152,256]{1,0:T(8,128)(2,1)S(1)}, u32[]{:S(2)}) %copy-start.6) | copy-done | bytes 589848
  13.9 0.8 %copy-done.8 = bf16[1152,256]{1,0:T(8,128)(2,1)} copy-done((bf16[1152,256]{1,0:T(8,128)(2,1)}, bf16[1152,256]{1,0:T(8,128)(2,1)S(1)}, u32[]{:S(2)}) %copy-start.8) | copy-done | bytes 589848
  14.7 0.8 %copy-done.10 = bf16[512,512]{1,0:T(8,128)(2,1)} copy-done((bf16[512,512]{1,0:T(8,128)(2,1)}, bf16[512,512]{1,0:T(8,128)(2,1)S(1)}, u32[]{:S(2)}) %copy-start.10) | copy-done | bytes 524312
  15.5 0.0 collective-permute-start.3
  15.5 1.1 %copy-done.5 = bf16[4,576,128]{2,1,0:T(8,128)(2,1)S(1)} copy-done((bf16[4,576,128]{2,1,0:T(8,128)(2,1)S(1)}, bf16[4,576,128]{2,1,0:T(8,128)(2,1)}, u32[]{:S(2)}) %copy-start.5) | copy-done | bytes 589848
  16.6 0.8 %shard_map.76.l1own = bf16[2,432,128]{2,1,0:T(8,128)(2,1)S(1)} custom-call(bf16[4,576,128]{2,1,0:T(8,128)(2,1)S(1)} %copy-done.5, bf16[1152,256]{1,0:T(8,128)(2,1)S(1)} %get-tuple-element.30.w.w1, f32[3,128]{1,0:T(4,128)S(1)} %get-tuple-element.31.b.bias), custom_call_target="tpu_custom_call" | custom-call | flops 1000000000 | bytes 1000000 | tf_op jit(solution)/shard_map/pallas_call | solution.py:27
  17.3 0.0 collective-permute-done.8.side
  17.3 1.8 %collective-permute-start.4 = (bf16[3,8,4,128]{3,2,1,0:T(4,128)(2,1)S(1)}, bf16[3,8,4,128]{3,2,1,0:T(4,128)(2,1)S(1)}, u32[]{:S(2)}, u32[]{:S(2)}) collective-permute-start(bf16[3,8,4,128]{3,2,1,0:T(4,128)(2,1)S(1)} %get-tuple-element.29), channel_id=1, source_target_pairs={{8,0},{16,8},{24,16},{0,24},{9,1},{17,9},{25,17},{1,25},{10,2},{18... | collective-permute-start | bytes 73736 | tf_op jit(solution)/shard_map/ppermute | solution.py:311
  19.2 1.9 %collective-permute-done.5.side = bf16[4,3,72,128]{3,2,1,0:T(8,128)(2,1)S(1)} collective-permute-done((bf16[4,3,72,128]{3,2,1,0:T(8,128)(2,1)S(1)}, bf16[4,3,72,128]{3,2,1,0:T(8,128)(2,1)S(1)}, u32[]{:S(2)}, u32[]{:S(2)}) %collective-permute-start.5) | collective-permute-done | bytes 221216 | tf_op jit(solution)/shard_map/ppermute | solution.py:319
  21.0 0.0 collective-permute-start.10
  21.1 0.0 collective-permute-done.3.em
  21.1 1.1 %collective-permute-start.9 = (bf16[3,3,72,128]{3,2,1,0:T(8,128)(2,1)S(1)}, bf16[3,3,72,128]{3,2,1,0:T(8,128)(2,1)S(1)}, u32[]{:S(2)}, u32[]{:S(2)}) collective-permute-start(bf16[3,3,72,128]{3,2,1,0:T(8,128)(2,1)S(1)} %get-tuple-element.42), channel_id=1, source_target_pairs={{0,8},{8,0},{16,24},{24,16},{1,9},{9,1},{17,25},{25,17},{2,10},{10... | collective-permute-start | bytes 497672 | tf_op jit(solution)/shard_map/ppermute | solution.py:319
  22.2 0.0 collective-permute-done.4.ep
  22.2 0.1 collective-permute-start.6
  22.3 0.0 collective-permute-done.1.xm
  22.3 1.1 %collective-permute-start.7 = (bf16[3,3,72,128]{3,2,1,0:T(8,128)(2,1)S(1)}, bf16[3,3,72,128]{3,2,1,0:T(8,128)(2,1)S(1)}, u32[]{:S(2)}, u32[]{:S(2)}) collective-permute-start(bf16[3,3,72,128]{3,2,1,0:T(8,128)(2,1)S(1)} %get-tuple-element.43), channel_id=1, source_target_pairs={{0,24},{8,16},{16,8},{24,0},{1,25},{9,17},{17,9},{25,1},{2,26},{10... | collective-permute-start | bytes 497672 | tf_op jit(solution)/shard_map/ppermute | solution.py:319
  23.4 0.0 collective-permute-done.2.xp
  23.4 2.2 %shard_map.77 = (bf16[8,432,128]{2,1,0:T(8,128)(2,1)S(1)}, bf16[10,288,128]{2,1,0:T(8,128)(2,1)S(1)}) custom-call(bf16[4,576,128]{2,1,0:T(8,128)(2,1)S(1)} %copy-done.5, bf16[3,8,72,128]{3,2,1,0:T(8,128)(2,1)S(1)} %collective-permute-done.1.xm, bf16[3,8,72,128]{3,2,1,0:T(8,128)(2,1)S(1)} %collective-permute-done.2.xp, ...), custom_call_target="tpu_custom_call" | custom-call | flops 2000000000 | bytes 1000000 | tf_op jit(solution)/shard_map/pallas_call | solution.py:27
  25.6 0.0 copy-done.7
  25.6 0.0 copy-done.9
  25.6 1.8 %shard_map.78 = (bf16[6,288,128]{2,1,0:T(8,128)(2,1)S(1)}, bf16[4,2,64,128]{3,2,1,0:T(8,128)(2,1)S(1)}) custom-call(bf16[8,432,128]{2,1,0:T(8,128)(2,1)S(1)} %get-tuple-element.34.a.l1, bf16[1152,256]{1,0:T(8,128)(2,1)S(1)} %copy-done.7, bf16[1152,256]{1,0:T(8,128)(2,1)S(1)} %copy-done.9, f32[3,128]{1,0:T(4,128)S(1)} %get-tuple-element.31.b.bias), custom_call_target="tpu_custom_call" | custom-call | flops 2000000000 | bytes 1000000 | tf_op jit(solution)/shard_map/pallas_call | solution.py:27
  27.4 0.2 collective-permute-done.10.cb
  27.6 0.0 collective-permute-done.9.ca
  27.6 3.0 %shard_map.79.other = bf16[4,3,64,128]{3,2,1,0:T(8,128)(2,1)S(1)} custom-call(bf16[10,288,128]{2,1,0:T(8,128)(2,1)S(1)} %get-tuple-element.32.near, bf16[4,3,72,128]{3,2,1,0:T(8,128)(2,1)S(1)} %collective-permute-done.8.side, bf16[3,3,72,128]{3,2,1,0:T(8,128)(2,1)S(1)} %collective-permute-done.9.ca, bf16[3,3,72,128]{3,2,1,0:T(8,128)(2,1)S(1)} %collective-permute-done.10.cb, ...), custom_call_target="tpu_custom_call" | custom-call | flops 4000000000 | bytes 1000000 | tf_op jit(solution)/shard_map/pallas_call | solution.py:27
  30.6 0.0 collective-permute-done.6.ca
  30.6 0.1 collective-permute-done.7.cb
  30.6 0.0 copy-done.11
  30.6 4.4 %shard_map.80 = bf16[64,4,8,128]{3,2,1,0:T(8,128)(2,1)} custom-call(bf16[10,288,128]{2,1,0:T(8,128)(2,1)S(1)} %get-tuple-element.32.near, bf16[4,3,72,128]{3,2,1,0:T(8,128)(2,1)S(1)} %collective-permute-done.5.side, bf16[3,3,72,128]{3,2,1,0:T(8,128)(2,1)S(1)} %collective-permute-done.6.ca, bf16[3,3,72,128]{3,2,1,0:T(8,128)(2,1)S(1)} %collective-permute-done.7.cb, ...), custom_call_target="tpu_custom_call" | custom-call | flops 4000000000 | bytes 1000000 | tf_op jit(solution)/shard_map/pallas_call | solution.py:27
  (8 shorter events, 0.1 us)
Async XLA Ops:
  0.0 1.0 %copy-start = (bf16[1,64,4,8,128]{4,3,2,1,0:T(8,128)(2,1)S(1)}, bf16[1,64,4,8,128]{4,3,2,1,0:T(8,128)(2,1)}, u32[]{:S(2)}) copy-start(bf16[1,64,4,8,128]{4,3,2,1,0:T(8,128)(2,1)} %param.7) | copy-start | bytes 1572868
  1.8 4.9 %collective-permute-start = (bf16[4,8,4,128]{3,2,1,0:T(4,128)(2,1)S(1)}, bf16[4,8,4,128]{3,2,1,0:T(4,128)(2,1)S(1)}, u32[]{:S(2)}, u32[]{:S(2)}) collective-permute-start(bf16[4,8,4,128]{3,2,1,0:T(4,128)(2,1)S(1)} %get-tuple-element.24), channel_id=1, source_target_pairs={{0,1},{1,0},{2,3},{3,2},{4,5},{5,4},{6,7},{7,6},{8,9},{9,8},{10,11... | collective-permute-start | bytes 98312 | tf_op jit(solution)/shard_map/ppermute | solution.py:311
  4.9 17.4 %collective-permute-start.1 = (bf16[3,8,72,128]{3,2,1,0:T(8,128)(2,1)S(1)}, bf16[3,8,72,128]{3,2,1,0:T(8,128)(2,1)S(1)}, u32[]{:S(2)}, u32[]{:S(2)}) collective-permute-start(bf16[3,8,72,128]{3,2,1,0:T(8,128)(2,1)S(1)} %get-tuple-element.26), channel_id=1, source_target_pairs={{0,8},{8,16},{16,24},{24,0},{1,9},{9,17},{17,25},{25,1},{2,10},{10... | collective-permute-start | bytes 1327112 | tf_op jit(solution)/shard_map/ppermute | solution.py:311
  4.9 18.5 %collective-permute-start.2 = (bf16[3,8,72,128]{3,2,1,0:T(8,128)(2,1)S(1)}, bf16[3,8,72,128]{3,2,1,0:T(8,128)(2,1)S(1)}, u32[]{:S(2)}, u32[]{:S(2)}) collective-permute-start(bf16[3,8,72,128]{3,2,1,0:T(8,128)(2,1)S(1)} %get-tuple-element.27), channel_id=1, source_target_pairs={{8,0},{16,8},{24,16},{0,24},{9,1},{17,9},{25,17},{1,25},{10,2},{18... | collective-permute-start | bytes 1327112 | tf_op jit(solution)/shard_map/ppermute | solution.py:311
  6.8 4.9 %copy-start.1 = (bf16[3,3,3,64,64]{4,3,2,1,0:T(8,128)(2,1)S(1)}, bf16[3,3,3,64,64]{4,3,2,1,0:T(8,128)(2,1)}, u32[]{:S(2)}) copy-start(bf16[3,3,3,64,64]{4,3,2,1,0:T(8,128)(2,1)} %k1.1) | copy-start | bytes 663556
  6.8 4.9 %copy-start.2 = (bf16[3,3,3,64,64]{4,3,2,1,0:T(8,128)(2,1)S(1)}, bf16[3,3,3,64,64]{4,3,2,1,0:T(8,128)(2,1)}, u32[]{:S(2)}) copy-start(bf16[3,3,3,64,64]{4,3,2,1,0:T(8,128)(2,1)} %k2.1) | copy-start | bytes 663556
  6.8 4.9 %copy-start.3 = (bf16[3,3,3,64,64]{4,3,2,1,0:T(8,128)(2,1)S(1)}, bf16[3,3,3,64,64]{4,3,2,1,0:T(8,128)(2,1)}, u32[]{:S(2)}) copy-start(bf16[3,3,3,64,64]{4,3,2,1,0:T(8,128)(2,1)} %k3.1) | copy-start | bytes 663556
  7.0 6.0 %copy-start.4 = (bf16[4,576,128]{2,1,0:T(8,128)(2,1)}, bf16[4,576,128]{2,1,0:T(8,128)(2,1)S(1)}, u32[]{:S(2)}) copy-start(bf16[4,576,128]{2,1,0:T(8,128)(2,1)S(1)} %get-tuple-element.25.o.own) | copy-start | bytes 1769476
  7.0 10.3 %collective-permute-start.8 = (bf16[4,3,72,128]{3,2,1,0:T(8,128)(2,1)S(1)}, bf16[4,3,72,128]{3,2,1,0:T(8,128)(2,1)S(1)}, u32[]{:S(2)}, u32[]{:S(2)}) collective-permute-start(bf16[4,3,72,128]{3,2,1,0:T(8,128)(2,1)S(1)} %get-tuple-element.38), channel_id=1, source_target_pairs={{0,2},{2,0},{4,6},{6,4},{1,3},{3,1},{5,7},{7,5},{8,10},{10,8},{12,... | collective-permute-start | bytes 663560 | tf_op jit(solution)/shard_map/ppermute | solution.py:319
  9.2 11.9 %collective-permute-start.5 = (bf16[4,3,72,128]{3,2,1,0:T(8,128)(2,1)S(1)}, bf16[4,3,72,128]{3,2,1,0:T(8,128)(2,1)S(1)}, u32[]{:S(2)}, u32[]{:S(2)}) collective-permute-start(bf16[4,3,72,128]{3,2,1,0:T(8,128)(2,1)S(1)} %get-tuple-element.33), channel_id=1, source_target_pairs={{0,6},{2,4},{4,2},{6,0},{1,7},{3,5},{5,3},{7,1},{8,14},{10,12},{12... | collective-permute-start | bytes 663560 | tf_op jit(solution)/shard_map/ppermute | solution.py:319
  13.1 0.8 %copy-start.6 = (bf16[1152,256]{1,0:T(8,128)(2,1)}, bf16[1152,256]{1,0:T(8,128)(2,1)S(1)}, u32[]{:S(2)}) copy-start(bf16[1152,256]{1,0:T(8,128)(2,1)S(1)} %get-tuple-element.35.v.w2) | copy-start | bytes 1769476
  13.9 0.8 %copy-start.8 = (bf16[1152,256]{1,0:T(8,128)(2,1)}, bf16[1152,256]{1,0:T(8,128)(2,1)S(1)}, u32[]{:S(2)}) copy-start(bf16[1152,256]{1,0:T(8,128)(2,1)S(1)} %get-tuple-element.36.w.w3) | copy-start | bytes 1769476
  14.7 0.8 %copy-start.10 = (bf16[512,512]{1,0:T(8,128)(2,1)}, bf16[512,512]{1,0:T(8,128)(2,1)S(1)}, u32[]{:S(2)}) copy-start(bf16[512,512]{1,0:T(8,128)(2,1)S(1)} %get-tuple-element.40.pattern) | copy-start | bytes 1572868
  15.5 5.6 %collective-permute-start.3 = (bf16[3,8,4,128]{3,2,1,0:T(4,128)(2,1)S(1)}, bf16[3,8,4,128]{3,2,1,0:T(4,128)(2,1)S(1)}, u32[]{:S(2)}, u32[]{:S(2)}) collective-permute-start(bf16[3,8,4,128]{3,2,1,0:T(4,128)(2,1)S(1)} %get-tuple-element.28), channel_id=1, source_target_pairs={{0,8},{8,16},{16,24},{24,0},{1,9},{9,17},{17,25},{25,1},{2,10},{10... | collective-permute-start | bytes 73736 | tf_op jit(solution)/shard_map/ppermute | solution.py:311
  15.5 1.1 %copy-start.5 = (bf16[4,576,128]{2,1,0:T(8,128)(2,1)S(1)}, bf16[4,576,128]{2,1,0:T(8,128)(2,1)}, u32[]{:S(2)}) copy-start(bf16[4,576,128]{2,1,0:T(8,128)(2,1)} %copy-done.4) | copy-start | bytes 1769476
  17.3 4.9 %collective-permute-start.4 = (bf16[3,8,4,128]{3,2,1,0:T(4,128)(2,1)S(1)}, bf16[3,8,4,128]{3,2,1,0:T(4,128)(2,1)S(1)}, u32[]{:S(2)}, u32[]{:S(2)}) collective-permute-start(bf16[3,8,4,128]{3,2,1,0:T(4,128)(2,1)S(1)} %get-tuple-element.29), channel_id=1, source_target_pairs={{8,0},{16,8},{24,16},{0,24},{9,1},{17,9},{25,17},{1,25},{10,2},{18... | collective-permute-start | bytes 73736 | tf_op jit(solution)/shard_map/ppermute | solution.py:311
  21.0 6.5 %collective-permute-start.10 = (bf16[3,3,72,128]{3,2,1,0:T(8,128)(2,1)S(1)}, bf16[3,3,72,128]{3,2,1,0:T(8,128)(2,1)S(1)}, u32[]{:S(2)}, u32[]{:S(2)}) collective-permute-start(bf16[3,3,72,128]{3,2,1,0:T(8,128)(2,1)S(1)} %get-tuple-element.41), channel_id=1, source_target_pairs={{0,24},{8,16},{16,8},{24,0},{1,25},{9,17},{17,9},{25,1},{2,26},{10... | collective-permute-start | bytes 497672 | tf_op jit(solution)/shard_map/ppermute | solution.py:319
  21.1 6.5 %collective-permute-start.9 = (bf16[3,3,72,128]{3,2,1,0:T(8,128)(2,1)S(1)}, bf16[3,3,72,128]{3,2,1,0:T(8,128)(2,1)S(1)}, u32[]{:S(2)}, u32[]{:S(2)}) collective-permute-start(bf16[3,3,72,128]{3,2,1,0:T(8,128)(2,1)S(1)} %get-tuple-element.42), channel_id=1, source_target_pairs={{0,8},{8,0},{16,24},{24,16},{1,9},{9,1},{17,25},{25,17},{2,10},{10... | collective-permute-start | bytes 497672 | tf_op jit(solution)/shard_map/ppermute | solution.py:319
  22.2 8.4 %collective-permute-start.6 = (bf16[3,3,72,128]{3,2,1,0:T(8,128)(2,1)S(1)}, bf16[3,3,72,128]{3,2,1,0:T(8,128)(2,1)S(1)}, u32[]{:S(2)}, u32[]{:S(2)}) collective-permute-start(bf16[3,3,72,128]{3,2,1,0:T(8,128)(2,1)S(1)} %get-tuple-element.44), channel_id=1, source_target_pairs={{0,8},{8,0},{16,24},{24,16},{1,9},{9,1},{17,25},{25,17},{2,10},{10... | collective-permute-start | bytes 497672 | tf_op jit(solution)/shard_map/ppermute | solution.py:319
  22.3 3.3 %copy-start.7 = (bf16[1152,256]{1,0:T(8,128)(2,1)S(1)}, bf16[1152,256]{1,0:T(8,128)(2,1)}, u32[]{:S(2)}) copy-start(bf16[1152,256]{1,0:T(8,128)(2,1)} %copy-done.6) | copy-start | bytes 1769476
  22.3 3.3 %copy-start.9 = (bf16[1152,256]{1,0:T(8,128)(2,1)S(1)}, bf16[1152,256]{1,0:T(8,128)(2,1)}, u32[]{:S(2)}) copy-start(bf16[1152,256]{1,0:T(8,128)(2,1)} %copy-done.8) | copy-start | bytes 1769476
  22.3 8.3 %collective-permute-start.7 = (bf16[3,3,72,128]{3,2,1,0:T(8,128)(2,1)S(1)}, bf16[3,3,72,128]{3,2,1,0:T(8,128)(2,1)S(1)}, u32[]{:S(2)}, u32[]{:S(2)}) collective-permute-start(bf16[3,3,72,128]{3,2,1,0:T(8,128)(2,1)S(1)} %get-tuple-element.43), channel_id=1, source_target_pairs={{0,24},{8,16},{16,8},{24,0},{1,25},{9,17},{17,9},{25,1},{2,26},{10... | collective-permute-start | bytes 497672 | tf_op jit(solution)/shard_map/ppermute | solution.py:319
  27.6 3.0 %copy-start.11 = (bf16[512,512]{1,0:T(8,128)(2,1)S(1)}, bf16[512,512]{1,0:T(8,128)(2,1)}, u32[]{:S(2)}) copy-start(bf16[512,512]{1,0:T(8,128)(2,1)} %copy-done.10) | copy-start | bytes 1572868

commit v6 on v5

--- a/solution.py
+++ b/solution.py
@@ -56,36 +56,35 @@
     c, nx, ny, nz = field.shape
     rows = pairs.shape[2]
     h = HALO
-    m = iota((rows + 8, 2 * nz), 0)
-    j = iota((rows + 8, 2 * nz), 1)
+    tall = rows + 8
+    m = iota((2 * tall, nz), 0)
+    second = (m >= tall).astype(jnp.int32)
+    m = m - tall * second
     half = nz // 2
     first = jnp.where(m < rows + 2, m - rows + half, m - rows - 1)
     m = jnp.where(m < rows, m, jnp.where(m < rows + 4, first, -8))
-    second = (j >= nz).astype(jnp.int32)
-    pick = (j - nz * second == 2 * m - 3 + second).astype(F32).astype(BF16)
-    blank = jnp.zeros((c, nz), BF16)
+    pick = (iota((2 * tall, nz), 1) == 2 * m - 3 + second).astype(F32).astype(BF16)
     for x in range(nx):
         planes[x] = field[:, x].astype(F32).reshape(c * ny, nz)
-        for y in range(0, ny, 2):
-            blocks = []
-            for k in range(2):
-                b = planes[x, pl.ds(y + k, c, stride=ny), :].astype(BF16)
-                blocks.append(jnp.concatenate([b, blank], axis=1))
-                blocks.append(jnp.concatenate([blank, b], axis=1))
+        for y in range(0, ny, 4):
+            lines = [
+                planes[x, pl.ds(y + k, c, stride=ny), :].astype(BF16) for k in range(4)
+            ]
             r = lax.dot_general(
                 pick,
-                jnp.concatenate(blocks, axis=0),
+                jnp.concatenate(lines, axis=0),
                 (((1,), (1,)), ((), ())),
                 preferred_element_type=F32,
             ).astype(BF16)
-            for k in range(2):
-                lanes = slice(2 * c * k, 2 * c * (k + 1))
-                pairs[x, y + k] = r[:rows, lanes]
-                edges[x, y + k] = r[rows : rows + 4, lanes]
+            for k in range(4):
+                lanes = slice(c * k, c * (k + 1))
+                line = jnp.concatenate([r[:tall, lanes], r[tall:, lanes]], axis=1)
+                pairs[x, y + k] = line[:rows]
+                edges[x, y + k] = line[rows : rows + 4]
                 if x >= nx - h:
-                    xu[x - nx + h, y + k] = r[:rows, lanes]
+                    xu[x - nx + h, y + k] = line[:rows]
                 if x < h:
-                    xd[x, y + k] = r[:rows, lanes]
+                    xd[x, y + k] = line[:rows]
 
 
 def end_rows(lines, edges, wide):

time: 35.2 us -> 35 us (level)
  no operation moved by 1% of the time
where the time goes in v6:
time: 35 us; the launch traced here: 34.8 us
  Pallas kernels  14.2 us (41%)
  starting transfers between devices  13.5 us (39%)
  local copies, waits for them, and re-layouts  4.65 us (13%)
  waiting for transfers between devices  2.24 us (6%)
    pallas_call x8, Pallas kernels, run(): pl.pallas_call(kernel, out_shape=outs, in_specs=[VMEM] * (len(args) - far...  14.2 us
    ppermute x6, starting transfers between devices, swap(): return lax.ppermute(x, axis, pairs)  6.93 us
    ppermute x5, starting transfers between devices, shift(): return lax.ppermute(x, axis, pairs)  6.6 us
    unnamed x24, local copies, waits for them, and re-layouts  4.55 us
    ppermute x6, waiting for transfers between devices, swap(): return lax.ppermute(x, axis, pairs)  2.09 us
  transfers between devices with their start and end apart: 11, of which 4 were waited for; matrix products, arithmetic and copies ran while one was open for 0% of the time, Pallas kernels for 27%

profile of v6, /device:TPU:0, one launch (start us, length us, event | category | flops | bytes accessed | tf_op | source)
XLA Modules:
  0.0 34.8 jit_solution(3999506925453224742)
XLA Ops:
  0.0 0.0 copy-start
  0.0 1.0 %copy-done = bf16[1,64,4,8,128]{4,3,2,1,0:T(8,128)(2,1)S(1)} copy-done((bf16[1,64,4,8,128]{4,3,2,1,0:T(8,128)(2,1)S(1)}, bf16[1,64,4,8,128]{4,3,2,1,0:T(8,128)(2,1)}, u32[]{:S(2)}) %copy-start) | copy-done | bytes 524312
  1.0 0.5 %shard_map.73 = (bf16[4,8,72,128]{3,2,1,0:T(8,128)(2,1)S(1)}, bf16[4,8,4,128]{3,2,1,0:T(4,128)(2,1)S(1)}, bf16[3,8,72,128]{3,2,1,0:T(8,128)(2,1)S(1)}, bf16[3,8,72,128]{3,2,1,0:T(8,128)(2,1)S(1)}) custom-call(bf16[64,4,8,128]{3,2,1,0:T(8,128)(2,1)S(1)} %bitcast.5), custom_call_target="tpu_custom_call" | custom-call | flops 8000000000 | bytes 1000000 | tf_op jit(solution)/shard_map/pallas_call | solution.py:27
  1.6 3.1 %collective-permute-start = (bf16[4,8,4,128]{3,2,1,0:T(4,128)(2,1)S(1)}, bf16[4,8,4,128]{3,2,1,0:T(4,128)(2,1)S(1)}, u32[]{:S(2)}, u32[]{:S(2)}) collective-permute-start(bf16[4,8,4,128]{3,2,1,0:T(4,128)(2,1)S(1)} %get-tuple-element.24), channel_id=1, source_target_pairs={{0,1},{1,0},{2,3},{3,2},{4,5},{5,4},{6,7},{7,6},{8,9},{9,8},{10,11... | collective-permute-start | bytes 98312 | tf_op jit(solution)/shard_map/ppermute | solution.py:310
  4.6 0.0 collective-permute-start.1
  4.6 1.7 %collective-permute-start.2 = (bf16[3,8,72,128]{3,2,1,0:T(8,128)(2,1)S(1)}, bf16[3,8,72,128]{3,2,1,0:T(8,128)(2,1)S(1)}, u32[]{:S(2)}, u32[]{:S(2)}) collective-permute-start(bf16[3,8,72,128]{3,2,1,0:T(8,128)(2,1)S(1)} %get-tuple-element.27), channel_id=1, source_target_pairs={{8,0},{16,8},{24,16},{0,24},{9,1},{17,9},{25,17},{1,25},{10,2},{18... | collective-permute-start | bytes 1327112 | tf_op jit(solution)/shard_map/ppermute | solution.py:310
  6.4 0.1 collective-permute-done.edges
  6.5 0.0 copy-start.1
  6.5 0.0 copy-start.2
  6.5 0.0 copy-start.3
  6.5 0.2 shard_map.74
  6.8 0.0 copy-start.4
  6.8 2.1 %collective-permute-start.8 = (bf16[4,3,72,128]{3,2,1,0:T(8,128)(2,1)S(1)}, bf16[4,3,72,128]{3,2,1,0:T(8,128)(2,1)S(1)}, u32[]{:S(2)}, u32[]{:S(2)}) collective-permute-start(bf16[4,3,72,128]{3,2,1,0:T(8,128)(2,1)S(1)} %get-tuple-element.38), channel_id=1, source_target_pairs={{0,2},{2,0},{4,6},{6,4},{1,3},{3,1},{5,7},{7,5},{8,10},{10,8},{12,... | collective-permute-start | bytes 663560 | tf_op jit(solution)/shard_map/ppermute | solution.py:318
  8.9 2.5 %collective-permute-start.5 = (bf16[4,3,72,128]{3,2,1,0:T(8,128)(2,1)S(1)}, bf16[4,3,72,128]{3,2,1,0:T(8,128)(2,1)S(1)}, u32[]{:S(2)}, u32[]{:S(2)}) collective-permute-start(bf16[4,3,72,128]{3,2,1,0:T(8,128)(2,1)S(1)} %get-tuple-element.33), channel_id=1, source_target_pairs={{0,6},{2,4},{4,2},{6,0},{1,7},{3,5},{5,3},{7,1},{8,14},{10,12},{12... | collective-permute-start | bytes 663560 | tf_op jit(solution)/shard_map/ppermute | solution.py:318
  11.4 0.0 copy-done.1
  11.4 0.0 copy-done.2
  11.4 0.0 copy-done.3
  11.4 1.4 %shard_map.75 = (bf16[1152,256]{1,0:T(8,128)(2,1)S(1)}, bf16[1152,256]{1,0:T(8,128)(2,1)S(1)}, bf16[1152,256]{1,0:T(8,128)(2,1)S(1)}, f32[3,128]{1,0:T(4,128)S(1)}, bf16[512,512]{1,0:T(8,128)(2,1)S(1)}) custom-call(bf16[3,3,3,64,64]{4,3,2,1,0:T(8,128)(2,1)S(1)} %copy-done.1, bf16[3,3,3,64,64]{4,3,2,1,0:T(8,128)(2,1)S(1)} %copy-done.2, ...), custom_call_target="tpu_custom_call" | custom-call | flops 2000000000 | bytes 1000000 | tf_op jit(solution)/shard_map/pallas_call | solution.py:27
  12.8 0.0 copy-done.4
  12.8 0.0 copy-start.6
  12.8 0.8 %copy-done.6 = bf16[1152,256]{1,0:T(8,128)(2,1)} copy-done((bf16[1152,256]{1,0:T(8,128)(2,1)}, bf16[1152,256]{1,0:T(8,128)(2,1)S(1)}, u32[]{:S(2)}) %copy-start.6) | copy-done | bytes 589848
  13.6 0.8 %copy-done.8 = bf16[1152,256]{1,0:T(8,128)(2,1)} copy-done((bf16[1152,256]{1,0:T(8,128)(2,1)}, bf16[1152,256]{1,0:T(8,128)(2,1)S(1)}, u32[]{:S(2)}) %copy-start.8) | copy-done | bytes 589848
  14.4 0.8 %copy-done.10 = bf16[512,512]{1,0:T(8,128)(2,1)} copy-done((bf16[512,512]{1,0:T(8,128)(2,1)}, bf16[512,512]{1,0:T(8,128)(2,1)S(1)}, u32[]{:S(2)}) %copy-start.10) | copy-done | bytes 524312
  15.2 0.0 collective-permute-start.3
  15.2 1.1 %copy-done.5 = bf16[4,576,128]{2,1,0:T(8,128)(2,1)S(1)} copy-done((bf16[4,576,128]{2,1,0:T(8,128)(2,1)S(1)}, bf16[4,576,128]{2,1,0:T(8,128)(2,1)}, u32[]{:S(2)}) %copy-start.5) | copy-done | bytes 589848
  16.3 0.8 %shard_map.76.l1own = bf16[2,432,128]{2,1,0:T(8,128)(2,1)S(1)} custom-call(bf16[4,576,128]{2,1,0:T(8,128)(2,1)S(1)} %copy-done.5, bf16[1152,256]{1,0:T(8,128)(2,1)S(1)} %get-tuple-element.30.w.w1, f32[3,128]{1,0:T(4,128)S(1)} %get-tuple-element.31.b.bias), custom_call_target="tpu_custom_call" | custom-call | flops 1000000000 | bytes 1000000 | tf_op jit(solution)/shard_map/pallas_call | solution.py:27
  17.1 0.0 collective-permute-done.8.side
  17.1 1.8 %collective-permute-start.4 = (bf16[3,8,4,128]{3,2,1,0:T(4,128)(2,1)S(1)}, bf16[3,8,4,128]{3,2,1,0:T(4,128)(2,1)S(1)}, u32[]{:S(2)}, u32[]{:S(2)}) collective-permute-start(bf16[3,8,4,128]{3,2,1,0:T(4,128)(2,1)S(1)} %get-tuple-element.29), channel_id=1, source_target_pairs={{8,0},{16,8},{24,16},{0,24},{9,1},{17,9},{25,17},{1,25},{10,2},{18... | collective-permute-start | bytes 73736 | tf_op jit(solution)/shard_map/ppermute | solution.py:310
  18.9 1.9 %collective-permute-done.5.side = bf16[4,3,72,128]{3,2,1,0:T(8,128)(2,1)S(1)} collective-permute-done((bf16[4,3,72,128]{3,2,1,0:T(8,128)(2,1)S(1)}, bf16[4,3,72,128]{3,2,1,0:T(8,128)(2,1)S(1)}, u32[]{:S(2)}, u32[]{:S(2)}) %collective-permute-start.5) | collective-permute-done | bytes 221216 | tf_op jit(solution)/shard_map/ppermute | solution.py:318
  20.8 0.0 collective-permute-start.10
  20.8 0.0 collective-permute-done.3.em
  20.8 1.1 %collective-permute-start.9 = (bf16[3,3,72,128]{3,2,1,0:T(8,128)(2,1)S(1)}, bf16[3,3,72,128]{3,2,1,0:T(8,128)(2,1)S(1)}, u32[]{:S(2)}, u32[]{:S(2)}) collective-permute-start(bf16[3,3,72,128]{3,2,1,0:T(8,128)(2,1)S(1)} %get-tuple-element.42), channel_id=1, source_target_pairs={{0,8},{8,0},{16,24},{24,16},{1,9},{9,1},{17,25},{25,17},{2,10},{10... | collective-permute-start | bytes 497672 | tf_op jit(solution)/shard_map/ppermute | solution.py:318
  21.9 0.0 collective-permute-done.4.ep
  21.9 0.1 collective-permute-start.6
  22.0 0.0 collective-permute-done.1.xm
  22.0 1.1 %collective-permute-start.7 = (bf16[3,3,72,128]{3,2,1,0:T(8,128)(2,1)S(1)}, bf16[3,3,72,128]{3,2,1,0:T(8,128)(2,1)S(1)}, u32[]{:S(2)}, u32[]{:S(2)}) collective-permute-start(bf16[3,3,72,128]{3,2,1,0:T(8,128)(2,1)S(1)} %get-tuple-element.43), channel_id=1, source_target_pairs={{0,24},{8,16},{16,8},{24,0},{1,25},{9,17},{17,9},{25,1},{2,26},{10... | collective-permute-start | bytes 497672 | tf_op jit(solution)/shard_map/ppermute | solution.py:318
  23.1 0.0 collective-permute-done.2.xp
  23.2 2.2 %shard_map.77 = (bf16[8,432,128]{2,1,0:T(8,128)(2,1)S(1)}, bf16[10,288,128]{2,1,0:T(8,128)(2,1)S(1)}) custom-call(bf16[4,576,128]{2,1,0:T(8,128)(2,1)S(1)} %copy-done.5, bf16[3,8,72,128]{3,2,1,0:T(8,128)(2,1)S(1)} %collective-permute-done.1.xm, bf16[3,8,72,128]{3,2,1,0:T(8,128)(2,1)S(1)} %collective-permute-done.2.xp, ...), custom_call_target="tpu_custom_call" | custom-call | flops 2000000000 | bytes 1000000 | tf_op jit(solution)/shard_map/pallas_call | solution.py:27
  25.3 0.0 copy-done.7
  25.3 0.0 copy-done.9
  25.3 1.8 %shard_map.78 = (bf16[6,288,128]{2,1,0:T(8,128)(2,1)S(1)}, bf16[4,2,64,128]{3,2,1,0:T(8,128)(2,1)S(1)}) custom-call(bf16[8,432,128]{2,1,0:T(8,128)(2,1)S(1)} %get-tuple-element.34.a.l1, bf16[1152,256]{1,0:T(8,128)(2,1)S(1)} %copy-done.7, bf16[1152,256]{1,0:T(8,128)(2,1)S(1)} %copy-done.9, f32[3,128]{1,0:T(4,128)S(1)} %get-tuple-element.31.b.bias), custom_call_target="tpu_custom_call" | custom-call | flops 2000000000 | bytes 1000000 | tf_op jit(solution)/shard_map/pallas_call | solution.py:27
  27.2 0.2 collective-permute-done.10.cb
  27.3 0.0 collective-permute-done.9.ca
  27.3 3.0 %shard_map.79.other = bf16[4,3,64,128]{3,2,1,0:T(8,128)(2,1)S(1)} custom-call(bf16[10,288,128]{2,1,0:T(8,128)(2,1)S(1)} %get-tuple-element.32.near, bf16[4,3,72,128]{3,2,1,0:T(8,128)(2,1)S(1)} %collective-permute-done.8.side, bf16[3,3,72,128]{3,2,1,0:T(8,128)(2,1)S(1)} %collective-permute-done.9.ca, bf16[3,3,72,128]{3,2,1,0:T(8,128)(2,1)S(1)} %collective-permute-done.10.cb, ...), custom_call_target="tpu_custom_call" | custom-call | flops 4000000000 | bytes 1000000 | tf_op jit(solution)/shard_map/pallas_call | solution.py:27
  30.3 0.0 collective-permute-done.6.ca
  30.3 0.1 collective-permute-done.7.cb
  30.4 0.0 copy-done.11
  30.4 4.4 %shard_map.80 = bf16[64,4,8,128]{3,2,1,0:T(8,128)(2,1)} custom-call(bf16[10,288,128]{2,1,0:T(8,128)(2,1)S(1)} %get-tuple-element.32.near, bf16[4,3,72,128]{3,2,1,0:T(8,128)(2,1)S(1)} %collective-permute-done.5.side, bf16[3,3,72,128]{3,2,1,0:T(8,128)(2,1)S(1)} %collective-permute-done.6.ca, bf16[3,3,72,128]{3,2,1,0:T(8,128)(2,1)S(1)} %collective-permute-done.7.cb, ...), custom_call_target="tpu_custom_call" | custom-call | flops 4000000000 | bytes 1000000 | tf_op jit(solution)/shard_map/pallas_call | solution.py:27
  (8 shorter events, 0.1 us)
Async XLA Ops:
  0.0 1.0 %copy-start = (bf16[1,64,4,8,128]{4,3,2,1,0:T(8,128)(2,1)S(1)}, bf16[1,64,4,8,128]{4,3,2,1,0:T(8,128)(2,1)}, u32[]{:S(2)}) copy-start(bf16[1,64,4,8,128]{4,3,2,1,0:T(8,128)(2,1)} %param.7) | copy-start | bytes 1572868
  1.6 5.0 %collective-permute-start = (bf16[4,8,4,128]{3,2,1,0:T(4,128)(2,1)S(1)}, bf16[4,8,4,128]{3,2,1,0:T(4,128)(2,1)S(1)}, u32[]{:S(2)}, u32[]{:S(2)}) collective-permute-start(bf16[4,8,4,128]{3,2,1,0:T(4,128)(2,1)S(1)} %get-tuple-element.24), channel_id=1, source_target_pairs={{0,1},{1,0},{2,3},{3,2},{4,5},{5,4},{6,7},{7,6},{8,9},{9,8},{10,11... | collective-permute-start | bytes 98312 | tf_op jit(solution)/shard_map/ppermute | solution.py:310
  4.6 17.4 %collective-permute-start.1 = (bf16[3,8,72,128]{3,2,1,0:T(8,128)(2,1)S(1)}, bf16[3,8,72,128]{3,2,1,0:T(8,128)(2,1)S(1)}, u32[]{:S(2)}, u32[]{:S(2)}) collective-permute-start(bf16[3,8,72,128]{3,2,1,0:T(8,128)(2,1)S(1)} %get-tuple-element.26), channel_id=1, source_target_pairs={{0,8},{8,16},{16,24},{24,0},{1,9},{9,17},{17,25},{25,1},{2,10},{10... | collective-permute-start | bytes 1327112 | tf_op jit(solution)/shard_map/ppermute | solution.py:310
  4.6 18.5 %collective-permute-start.2 = (bf16[3,8,72,128]{3,2,1,0:T(8,128)(2,1)S(1)}, bf16[3,8,72,128]{3,2,1,0:T(8,128)(2,1)S(1)}, u32[]{:S(2)}, u32[]{:S(2)}) collective-permute-start(bf16[3,8,72,128]{3,2,1,0:T(8,128)(2,1)S(1)} %get-tuple-element.27), channel_id=1, source_target_pairs={{8,0},{16,8},{24,16},{0,24},{9,1},{17,9},{25,17},{1,25},{10,2},{18... | collective-permute-start | bytes 1327112 | tf_op jit(solution)/shard_map/ppermute | solution.py:310
  6.5 4.9 %copy-start.1 = (bf16[3,3,3,64,64]{4,3,2,1,0:T(8,128)(2,1)S(1)}, bf16[3,3,3,64,64]{4,3,2,1,0:T(8,128)(2,1)}, u32[]{:S(2)}) copy-start(bf16[3,3,3,64,64]{4,3,2,1,0:T(8,128)(2,1)} %k1.1) | copy-start | bytes 663556
  6.5 4.9 %copy-start.2 = (bf16[3,3,3,64,64]{4,3,2,1,0:T(8,128)(2,1)S(1)}, bf16[3,3,3,64,64]{4,3,2,1,0:T(8,128)(2,1)}, u32[]{:S(2)}) copy-start(bf16[3,3,3,64,64]{4,3,2,1,0:T(8,128)(2,1)} %k2.1) | copy-start | bytes 663556
  6.5 4.9 %copy-start.3 = (bf16[3,3,3,64,64]{4,3,2,1,0:T(8,128)(2,1)S(1)}, bf16[3,3,3,64,64]{4,3,2,1,0:T(8,128)(2,1)}, u32[]{:S(2)}) copy-start(bf16[3,3,3,64,64]{4,3,2,1,0:T(8,128)(2,1)} %k3.1) | copy-start | bytes 663556
  6.8 6.0 %copy-start.4 = (bf16[4,576,128]{2,1,0:T(8,128)(2,1)}, bf16[4,576,128]{2,1,0:T(8,128)(2,1)S(1)}, u32[]{:S(2)}) copy-start(bf16[4,576,128]{2,1,0:T(8,128)(2,1)S(1)} %get-tuple-element.25.o.own) | copy-start | bytes 1769476
  6.8 10.3 %collective-permute-start.8 = (bf16[4,3,72,128]{3,2,1,0:T(8,128)(2,1)S(1)}, bf16[4,3,72,128]{3,2,1,0:T(8,128)(2,1)S(1)}, u32[]{:S(2)}, u32[]{:S(2)}) collective-permute-start(bf16[4,3,72,128]{3,2,1,0:T(8,128)(2,1)S(1)} %get-tuple-element.38), channel_id=1, source_target_pairs={{0,2},{2,0},{4,6},{6,4},{1,3},{3,1},{5,7},{7,5},{8,10},{10,8},{12,... | collective-permute-start | bytes 663560 | tf_op jit(solution)/shard_map/ppermute | solution.py:318
  8.9 11.9 %collective-permute-start.5 = (bf16[4,3,72,128]{3,2,1,0:T(8,128)(2,1)S(1)}, bf16[4,3,72,128]{3,2,1,0:T(8,128)(2,1)S(1)}, u32[]{:S(2)}, u32[]{:S(2)}) collective-permute-start(bf16[4,3,72,128]{3,2,1,0:T(8,128)(2,1)S(1)} %get-tuple-element.33), channel_id=1, source_target_pairs={{0,6},{2,4},{4,2},{6,0},{1,7},{3,5},{5,3},{7,1},{8,14},{10,12},{12... | collective-permute-start | bytes 663560 | tf_op jit(solution)/shard_map/ppermute | solution.py:318
  12.8 0.8 %copy-start.6 = (bf16[1152,256]{1,0:T(8,128)(2,1)}, bf16[1152,256]{1,0:T(8,128)(2,1)S(1)}, u32[]{:S(2)}) copy-start(bf16[1152,256]{1,0:T(8,128)(2,1)S(1)} %get-tuple-element.35.v.w2) | copy-start | bytes 1769476
  13.6 0.8 %copy-start.8 = (bf16[1152,256]{1,0:T(8,128)(2,1)}, bf16[1152,256]{1,0:T(8,128)(2,1)S(1)}, u32[]{:S(2)}) copy-start(bf16[1152,256]{1,0:T(8,128)(2,1)S(1)} %get-tuple-element.36.w.w3) | copy-start | bytes 1769476
  14.4 0.8 %copy-start.10 = (bf16[512,512]{1,0:T(8,128)(2,1)}, bf16[512,512]{1,0:T(8,128)(2,1)S(1)}, u32[]{:S(2)}) copy-start(bf16[512,512]{1,0:T(8,128)(2,1)S(1)} %get-tuple-element.40.pattern) | copy-start | bytes 1572868
  15.2 5.6 %collective-permute-start.3 = (bf16[3,8,4,128]{3,2,1,0:T(4,128)(2,1)S(1)}, bf16[3,8,4,128]{3,2,1,0:T(4,128)(2,1)S(1)}, u32[]{:S(2)}, u32[]{:S(2)}) collective-permute-start(bf16[3,8,4,128]{3,2,1,0:T(4,128)(2,1)S(1)} %get-tuple-element.28), channel_id=1, source_target_pairs={{0,8},{8,16},{16,24},{24,0},{1,9},{9,17},{17,25},{25,1},{2,10},{10... | collective-permute-start | bytes 73736 | tf_op jit(solution)/shard_map/ppermute | solution.py:310
  15.2 1.1 %copy-start.5 = (bf16[4,576,128]{2,1,0:T(8,128)(2,1)S(1)}, bf16[4,576,128]{2,1,0:T(8,128)(2,1)}, u32[]{:S(2)}) copy-start(bf16[4,576,128]{2,1,0:T(8,128)(2,1)} %copy-done.4) | copy-start | bytes 1769476
  17.1 4.9 %collective-permute-start.4 = (bf16[3,8,4,128]{3,2,1,0:T(4,128)(2,1)S(1)}, bf16[3,8,4,128]{3,2,1,0:T(4,128)(2,1)S(1)}, u32[]{:S(2)}, u32[]{:S(2)}) collective-permute-start(bf16[3,8,4,128]{3,2,1,0:T(4,128)(2,1)S(1)} %get-tuple-element.29), channel_id=1, source_target_pairs={{8,0},{16,8},{24,16},{0,24},{9,1},{17,9},{25,17},{1,25},{10,2},{18... | collective-permute-start | bytes 73736 | tf_op jit(solution)/shard_map/ppermute | solution.py:310
  20.8 6.5 %collective-permute-start.10 = (bf16[3,3,72,128]{3,2,1,0:T(8,128)(2,1)S(1)}, bf16[3,3,72,128]{3,2,1,0:T(8,128)(2,1)S(1)}, u32[]{:S(2)}, u32[]{:S(2)}) collective-permute-start(bf16[3,3,72,128]{3,2,1,0:T(8,128)(2,1)S(1)} %get-tuple-element.41), channel_id=1, source_target_pairs={{0,24},{8,16},{16,8},{24,0},{1,25},{9,17},{17,9},{25,1},{2,26},{10... | collective-permute-start | bytes 497672 | tf_op jit(solution)/shard_map/ppermute | solution.py:318
  20.8 6.5 %collective-permute-start.9 = (bf16[3,3,72,128]{3,2,1,0:T(8,128)(2,1)S(1)}, bf16[3,3,72,128]{3,2,1,0:T(8,128)(2,1)S(1)}, u32[]{:S(2)}, u32[]{:S(2)}) collective-permute-start(bf16[3,3,72,128]{3,2,1,0:T(8,128)(2,1)S(1)} %get-tuple-element.42), channel_id=1, source_target_pairs={{0,8},{8,0},{16,24},{24,16},{1,9},{9,1},{17,25},{25,17},{2,10},{10... | collective-permute-start | bytes 497672 | tf_op jit(solution)/shard_map/ppermute | solution.py:318
  21.9 8.4 %collective-permute-start.6 = (bf16[3,3,72,128]{3,2,1,0:T(8,128)(2,1)S(1)}, bf16[3,3,72,128]{3,2,1,0:T(8,128)(2,1)S(1)}, u32[]{:S(2)}, u32[]{:S(2)}) collective-permute-start(bf16[3,3,72,128]{3,2,1,0:T(8,128)(2,1)S(1)} %get-tuple-element.44), channel_id=1, source_target_pairs={{0,8},{8,0},{16,24},{24,16},{1,9},{9,1},{17,25},{25,17},{2,10},{10... | collective-permute-start | bytes 497672 | tf_op jit(solution)/shard_map/ppermute | solution.py:318
  22.0 3.3 %copy-start.7 = (bf16[1152,256]{1,0:T(8,128)(2,1)S(1)}, bf16[1152,256]{1,0:T(8,128)(2,1)}, u32[]{:S(2)}) copy-start(bf16[1152,256]{1,0:T(8,128)(2,1)} %copy-done.6) | copy-start | bytes 1769476
  22.0 3.3 %copy-start.9 = (bf16[1152,256]{1,0:T(8,128)(2,1)S(1)}, bf16[1152,256]{1,0:T(8,128)(2,1)}, u32[]{:S(2)}) copy-start(bf16[1152,256]{1,0:T(8,128)(2,1)} %copy-done.8) | copy-start | bytes 1769476
  22.0 8.3 %collective-permute-start.7 = (bf16[3,3,72,128]{3,2,1,0:T(8,128)(2,1)S(1)}, bf16[3,3,72,128]{3,2,1,0:T(8,128)(2,1)S(1)}, u32[]{:S(2)}, u32[]{:S(2)}) collective-permute-start(bf16[3,3,72,128]{3,2,1,0:T(8,128)(2,1)S(1)} %get-tuple-element.43), channel_id=1, source_target_pairs={{0,24},{8,16},{16,8},{24,0},{1,25},{9,17},{17,9},{25,1},{2,26},{10... | collective-permute-start | bytes 497672 | tf_op jit(solution)/shard_map/ppermute | solution.py:318
  27.3 3.0 %copy-start.11 = (bf16[512,512]{1,0:T(8,128)(2,1)S(1)}, bf16[512,512]{1,0:T(8,128)(2,1)}, u32[]{:S(2)}) copy-start(bf16[512,512]{1,0:T(8,128)(2,1)} %copy-done.10) | copy-start | bytes 1572868

commit v7 on v6

--- a/solution.py
+++ b/solution.py
@@ -109,19 +109,8 @@
     )
     own[...] = e.reshape(nx, ny * rows, line).astype(BF16)
     e = e.astype(BF16)
-    even = is_even("gy")
-    head, tail = e[:, :h], e[:, ny - h :]
-
-    @pl.when(even)
-    def _():
-        ya[...] = tail
-        yb[...] = head
-
-    @pl.when(jnp.logical_not(even))
-    def _():
-        ya[...] = head
-        yb[...] = tail
-
+    ya[...] = e[:, ny - h :]
+    yb[...] = e[:, :h]
     eu[...] = edges[nx - h :]
     ed[...] = edges[:h]
 
@@ -239,18 +228,6 @@
     return [conv(s2, x, rows, 3, ws[2][...], bias[2:3]) for x in range(nx)]
 
 
-def by_side(even_below, body):
-    even = is_even("gy")
-
-    @pl.when(even)
-    def _():
-        body(even_below)
-
-    @pl.when(jnp.logical_not(even))
-    def _():
-        body(not even_below)
-
-
 def first_kernel(near, side, ca, cb, l1, l2, w1, w2, w3, bias, out, s0, s1, s2):
     rows = side.shape[2]
     half = out.shape[2]
@@ -262,7 +239,7 @@
             for i in range(3):
                 out[x, i] = lines[i * rows : i * rows + half]
 
-    by_side(False, body)
+    body(True)
 
 
 def second_kernel(
@@ -301,7 +278,7 @@
                 ]
             out[:, x] = stage[x].reshape(c, ny, nz).astype(BF16)
 
-    by_side(True, body)
+    body(False)
 
 
 def shift(x, axis, up):
@@ -360,8 +337,8 @@
     )(pairs, edges)
     em = shift(eu, "gx", True)
     ep = shift(ed, "gx", False)
-    ya = swap(ya, "gy", True)
-    yb = swap(yb, "gy", False)
+    ya = shift(ya, "gy", True)
+    yb = shift(yb, "gy", False)
     tail = jnp.where(is_even("gx"), nx - h, 0)
 
     def planes(side, start):

time: 35 us -> 34.1 us (0.974)
  starting transfers between devices: 13.5 us -> 12.5 us
    ppermute x6 -> x4, starting transfers between devices: 6.93 us -> 2.31 us  [swap(): return lax.ppermute(x, axis, pairs)]
    ppermute x5 -> x7, starting transfers between devices: 6.6 us -> 10.2 us  [shift(): return lax.ppermute(x, axis, pairs)]
    ppermute x5 -> x7, waiting for transfers between devices: 0.16 us -> 2.17 us  [shift(): return lax.ppermute(x, axis, pairs)]
    ppermute x6 -> x4, waiting for transfers between devices: 2.09 us -> 0.34 us  [swap(): return lax.ppermute(x, axis, pairs)]
  transfers between devices with their start and end apart: 11 -> 11, of which waited for: 4 -> 5; matrix products, arithmetic and copies ran while one was open for 0% -> 0% of each run, Pallas kernels for 27% -> 27%
where the time goes in v7:
time: 34.1 us; the launch traced here: 33.9 us
  Pallas kernels  14.1 us (41%)
  starting transfers between devices  12.5 us (37%)
  local copies, waits for them, and re-layouts  4.65 us (14%)
  waiting for transfers between devices  2.51 us (7%)
    pallas_call x8, Pallas kernels, run(): pl.pallas_call(kernel, out_shape=outs, in_specs=[VMEM] * (len(args) - far...  14.1 us
    ppermute x7, starting transfers between devices, shift(): return lax.ppermute(x, axis, pairs)  10.2 us
    unnamed x24, local copies, waits for them, and re-layouts  4.55 us
    ppermute x4, starting transfers between devices, swap(): return lax.ppermute(x, axis, pairs)  2.31 us
    ppermute x7, waiting for transfers between devices, shift(): return lax.ppermute(x, axis, pairs)  2.17 us
  transfers between devices with their start and end apart: 11, of which 5 were waited for; matrix products, arithmetic and copies ran while one was open for 0% of the time, Pallas kernels for 27%

profile of v7, /device:TPU:0, one launch (start us, length us, event | category | flops | bytes accessed | tf_op | source)
XLA Modules:
  0.0 33.9 jit_solution(7300807982682218957)
XLA Ops:
  0.0 0.0 copy-start
  0.0 1.0 %copy-done = bf16[1,64,4,8,128]{4,3,2,1,0:T(8,128)(2,1)S(1)} copy-done((bf16[1,64,4,8,128]{4,3,2,1,0:T(8,128)(2,1)S(1)}, bf16[1,64,4,8,128]{4,3,2,1,0:T(8,128)(2,1)}, u32[]{:S(2)}) %copy-start) | copy-done | bytes 524312
  1.0 0.5 %shard_map.73 = (bf16[4,8,72,128]{3,2,1,0:T(8,128)(2,1)S(1)}, bf16[4,8,4,128]{3,2,1,0:T(4,128)(2,1)S(1)}, bf16[3,8,72,128]{3,2,1,0:T(8,128)(2,1)S(1)}, bf16[3,8,72,128]{3,2,1,0:T(8,128)(2,1)S(1)}) custom-call(bf16[64,4,8,128]{3,2,1,0:T(8,128)(2,1)S(1)} %bitcast.5), custom_call_target="tpu_custom_call" | custom-call | flops 8000000000 | bytes 1000000 | tf_op jit(solution)/shard_map/pallas_call | solution.py:27
  1.6 3.1 %collective-permute-start = (bf16[4,8,4,128]{3,2,1,0:T(4,128)(2,1)S(1)}, bf16[4,8,4,128]{3,2,1,0:T(4,128)(2,1)S(1)}, u32[]{:S(2)}, u32[]{:S(2)}) collective-permute-start(bf16[4,8,4,128]{3,2,1,0:T(4,128)(2,1)S(1)} %get-tuple-element.24), channel_id=1, source_target_pairs={{0,1},{1,0},{2,3},{3,2},{4,5},{5,4},{6,7},{7,6},{8,9},{9,8},{10,11... | collective-permute-start | bytes 98312 | tf_op jit(solution)/shard_map/ppermute | solution.py:287
  4.6 0.0 collective-permute-start.1
  4.6 1.7 %collective-permute-start.2 = (bf16[3,8,72,128]{3,2,1,0:T(8,128)(2,1)S(1)}, bf16[3,8,72,128]{3,2,1,0:T(8,128)(2,1)S(1)}, u32[]{:S(2)}, u32[]{:S(2)}) collective-permute-start(bf16[3,8,72,128]{3,2,1,0:T(8,128)(2,1)S(1)} %get-tuple-element.27), channel_id=1, source_target_pairs={{8,0},{16,8},{24,16},{0,24},{9,1},{17,9},{25,17},{1,25},{10,2},{18... | collective-permute-start | bytes 1327112 | tf_op jit(solution)/shard_map/ppermute | solution.py:287
  6.4 0.1 collective-permute-done.edges
  6.5 0.0 copy-start.1
  6.5 0.0 copy-start.2
  6.5 0.0 copy-start.3
  6.5 0.2 shard_map.74
  6.7 0.0 copy-start.4
  6.7 2.1 %collective-permute-start.8 = (bf16[4,3,72,128]{3,2,1,0:T(8,128)(2,1)S(1)}, bf16[4,3,72,128]{3,2,1,0:T(8,128)(2,1)S(1)}, u32[]{:S(2)}, u32[]{:S(2)}) collective-permute-start(bf16[4,3,72,128]{3,2,1,0:T(8,128)(2,1)S(1)} %get-tuple-element.38), channel_id=1, source_target_pairs={{0,2},{2,4},{4,6},{6,0},{1,3},{3,5},{5,7},{7,1},{8,10},{10,12},{12... | collective-permute-start | bytes 663560 | tf_op jit(solution)/shard_map/ppermute | solution.py:287
  8.8 2.1 %collective-permute-start.5 = (bf16[4,3,72,128]{3,2,1,0:T(8,128)(2,1)S(1)}, bf16[4,3,72,128]{3,2,1,0:T(8,128)(2,1)S(1)}, u32[]{:S(2)}, u32[]{:S(2)}) collective-permute-start(bf16[4,3,72,128]{3,2,1,0:T(8,128)(2,1)S(1)} %get-tuple-element.33), channel_id=1, source_target_pairs={{2,0},{4,2},{6,4},{0,6},{3,1},{5,3},{7,5},{1,7},{10,8},{12,10},{14... | collective-permute-start | bytes 663560 | tf_op jit(solution)/shard_map/ppermute | solution.py:287
  10.9 0.0 copy-done.1
  10.9 0.0 copy-done.2
  11.0 0.0 copy-done.3
  11.0 1.4 %shard_map.75 = (bf16[1152,256]{1,0:T(8,128)(2,1)S(1)}, bf16[1152,256]{1,0:T(8,128)(2,1)S(1)}, bf16[1152,256]{1,0:T(8,128)(2,1)S(1)}, f32[3,128]{1,0:T(4,128)S(1)}, bf16[512,512]{1,0:T(8,128)(2,1)S(1)}) custom-call(bf16[3,3,3,64,64]{4,3,2,1,0:T(8,128)(2,1)S(1)} %copy-done.1, bf16[3,3,3,64,64]{4,3,2,1,0:T(8,128)(2,1)S(1)} %copy-done.2, ...), custom_call_target="tpu_custom_call" | custom-call | flops 2000000000 | bytes 1000000 | tf_op jit(solution)/shard_map/pallas_call | solution.py:27
  12.3 0.0 copy-done.4
  12.3 0.0 copy-start.6
  12.4 0.8 %copy-done.6 = bf16[1152,256]{1,0:T(8,128)(2,1)} copy-done((bf16[1152,256]{1,0:T(8,128)(2,1)}, bf16[1152,256]{1,0:T(8,128)(2,1)S(1)}, u32[]{:S(2)}) %copy-start.6) | copy-done | bytes 589848
  13.2 0.8 %copy-done.8 = bf16[1152,256]{1,0:T(8,128)(2,1)} copy-done((bf16[1152,256]{1,0:T(8,128)(2,1)}, bf16[1152,256]{1,0:T(8,128)(2,1)S(1)}, u32[]{:S(2)}) %copy-start.8) | copy-done | bytes 589848
  14.0 0.8 %copy-done.10 = bf16[512,512]{1,0:T(8,128)(2,1)} copy-done((bf16[512,512]{1,0:T(8,128)(2,1)}, bf16[512,512]{1,0:T(8,128)(2,1)S(1)}, u32[]{:S(2)}) %copy-start.10) | copy-done | bytes 524312
  14.8 0.0 collective-permute-start.3
  14.8 1.1 %copy-done.5 = bf16[4,576,128]{2,1,0:T(8,128)(2,1)S(1)} copy-done((bf16[4,576,128]{2,1,0:T(8,128)(2,1)S(1)}, bf16[4,576,128]{2,1,0:T(8,128)(2,1)}, u32[]{:S(2)}) %copy-start.5) | copy-done | bytes 589848
  15.8 0.8 %shard_map.76.l1own = bf16[2,432,128]{2,1,0:T(8,128)(2,1)S(1)} custom-call(bf16[4,576,128]{2,1,0:T(8,128)(2,1)S(1)} %copy-done.5, bf16[1152,256]{1,0:T(8,128)(2,1)S(1)} %get-tuple-element.30.w.w1, f32[3,128]{1,0:T(4,128)S(1)} %get-tuple-element.31.b.bias), custom_call_target="tpu_custom_call" | custom-call | flops 1000000000 | bytes 1000000 | tf_op jit(solution)/shard_map/pallas_call | solution.py:27
  16.6 0.6 %collective-permute-done.8.side = bf16[4,3,72,128]{3,2,1,0:T(8,128)(2,1)S(1)} collective-permute-done((bf16[4,3,72,128]{3,2,1,0:T(8,128)(2,1)S(1)}, bf16[4,3,72,128]{3,2,1,0:T(8,128)(2,1)S(1)}, u32[]{:S(2)}, u32[]{:S(2)}) %collective-permute-start.8) | collective-permute-done | bytes 221216 | tf_op jit(solution)/shard_map/ppermute | solution.py:287
  17.2 1.2 %collective-permute-start.4 = (bf16[3,8,4,128]{3,2,1,0:T(4,128)(2,1)S(1)}, bf16[3,8,4,128]{3,2,1,0:T(4,128)(2,1)S(1)}, u32[]{:S(2)}, u32[]{:S(2)}) collective-permute-start(bf16[3,8,4,128]{3,2,1,0:T(4,128)(2,1)S(1)} %get-tuple-element.29), channel_id=1, source_target_pairs={{8,0},{16,8},{24,16},{0,24},{9,1},{17,9},{25,17},{1,25},{10,2},{18... | collective-permute-start | bytes 73736 | tf_op jit(solution)/shard_map/ppermute | solution.py:287
  18.5 1.4 %collective-permute-done.5.side = bf16[4,3,72,128]{3,2,1,0:T(8,128)(2,1)S(1)} collective-permute-done((bf16[4,3,72,128]{3,2,1,0:T(8,128)(2,1)S(1)}, bf16[4,3,72,128]{3,2,1,0:T(8,128)(2,1)S(1)}, u32[]{:S(2)}, u32[]{:S(2)}) %collective-permute-start.5) | collective-permute-done | bytes 221216 | tf_op jit(solution)/shard_map/ppermute | solution.py:287
  19.9 0.0 collective-permute-start.10
  19.9 0.0 collective-permute-done.3.em
  20.0 1.1 %collective-permute-start.9 = (bf16[3,3,72,128]{3,2,1,0:T(8,128)(2,1)S(1)}, bf16[3,3,72,128]{3,2,1,0:T(8,128)(2,1)S(1)}, u32[]{:S(2)}, u32[]{:S(2)}) collective-permute-start(bf16[3,3,72,128]{3,2,1,0:T(8,128)(2,1)S(1)} %get-tuple-element.42), channel_id=1, source_target_pairs={{0,8},{8,0},{16,24},{24,16},{1,9},{9,1},{17,25},{25,17},{2,10},{10... | collective-permute-start | bytes 497672 | tf_op jit(solution)/shard_map/ppermute | solution.py:295
  21.0 0.0 collective-permute-done.4.ep
  21.0 0.6 %collective-permute-start.6 = (bf16[3,3,72,128]{3,2,1,0:T(8,128)(2,1)S(1)}, bf16[3,3,72,128]{3,2,1,0:T(8,128)(2,1)S(1)}, u32[]{:S(2)}, u32[]{:S(2)}) collective-permute-start(bf16[3,3,72,128]{3,2,1,0:T(8,128)(2,1)S(1)} %get-tuple-element.44), channel_id=1, source_target_pairs={{0,8},{8,0},{16,24},{24,16},{1,9},{9,1},{17,25},{25,17},{2,10},{10... | collective-permute-start | bytes 497672 | tf_op jit(solution)/shard_map/ppermute | solution.py:295
  21.7 0.0 collective-permute-done.1.xm
  21.7 0.6 %collective-permute-start.7 = (bf16[3,3,72,128]{3,2,1,0:T(8,128)(2,1)S(1)}, bf16[3,3,72,128]{3,2,1,0:T(8,128)(2,1)S(1)}, u32[]{:S(2)}, u32[]{:S(2)}) collective-permute-start(bf16[3,3,72,128]{3,2,1,0:T(8,128)(2,1)S(1)} %get-tuple-element.43), channel_id=1, source_target_pairs={{0,24},{8,16},{16,8},{24,0},{1,25},{9,17},{17,9},{25,1},{2,26},{10... | collective-permute-start | bytes 497672 | tf_op jit(solution)/shard_map/ppermute | solution.py:295
  22.3 0.0 collective-permute-done.2.xp
  22.3 2.2 %shard_map.77 = (bf16[8,432,128]{2,1,0:T(8,128)(2,1)S(1)}, bf16[10,288,128]{2,1,0:T(8,128)(2,1)S(1)}) custom-call(bf16[4,576,128]{2,1,0:T(8,128)(2,1)S(1)} %copy-done.5, bf16[3,8,72,128]{3,2,1,0:T(8,128)(2,1)S(1)} %collective-permute-done.1.xm, bf16[3,8,72,128]{3,2,1,0:T(8,128)(2,1)S(1)} %collective-permute-done.2.xp, ...), custom_call_target="tpu_custom_call" | custom-call | flops 2000000000 | bytes 1000000 | tf_op jit(solution)/shard_map/pallas_call | solution.py:27
  24.4 0.0 copy-done.7
  24.5 0.0 copy-done.9
  24.5 1.8 %shard_map.78 = (bf16[6,288,128]{2,1,0:T(8,128)(2,1)S(1)}, bf16[4,2,64,128]{3,2,1,0:T(8,128)(2,1)S(1)}) custom-call(bf16[8,432,128]{2,1,0:T(8,128)(2,1)S(1)} %get-tuple-element.34.a.l1, bf16[1152,256]{1,0:T(8,128)(2,1)S(1)} %copy-done.7, bf16[1152,256]{1,0:T(8,128)(2,1)S(1)} %copy-done.9, f32[3,128]{1,0:T(4,128)S(1)} %get-tuple-element.31.b.bias), custom_call_target="tpu_custom_call" | custom-call | flops 2000000000 | bytes 1000000 | tf_op jit(solution)/shard_map/pallas_call | solution.py:27
  26.3 0.2 collective-permute-done.10.cb
  26.4 0.0 collective-permute-done.9.ca
  26.4 3.0 %shard_map.79.other = bf16[4,3,64,128]{3,2,1,0:T(8,128)(2,1)S(1)} custom-call(bf16[10,288,128]{2,1,0:T(8,128)(2,1)S(1)} %get-tuple-element.32.near, bf16[4,3,72,128]{3,2,1,0:T(8,128)(2,1)S(1)} %collective-permute-done.8.side, bf16[3,3,72,128]{3,2,1,0:T(8,128)(2,1)S(1)} %collective-permute-done.9.ca, bf16[3,3,72,128]{3,2,1,0:T(8,128)(2,1)S(1)} %collective-permute-done.10.cb, ...), custom_call_target="tpu_custom_call" | custom-call | flops 4000000000 | bytes 1000000 | tf_op jit(solution)/shard_map/pallas_call | solution.py:27
  29.4 0.0 collective-permute-done.6.ca
  29.4 0.2 collective-permute-done.7.cb
  29.6 0.0 copy-done.11
  29.6 4.3 %shard_map.80 = bf16[64,4,8,128]{3,2,1,0:T(8,128)(2,1)} custom-call(bf16[10,288,128]{2,1,0:T(8,128)(2,1)S(1)} %get-tuple-element.32.near, bf16[4,3,72,128]{3,2,1,0:T(8,128)(2,1)S(1)} %collective-permute-done.5.side, bf16[3,3,72,128]{3,2,1,0:T(8,128)(2,1)S(1)} %collective-permute-done.6.ca, bf16[3,3,72,128]{3,2,1,0:T(8,128)(2,1)S(1)} %collective-permute-done.7.cb, ...), custom_call_target="tpu_custom_call" | custom-call | flops 4000000000 | bytes 1000000 | tf_op jit(solution)/shard_map/pallas_call | solution.py:27
  (8 shorter events, 0.1 us)
Async XLA Ops:
  0.0 1.0 %copy-start = (bf16[1,64,4,8,128]{4,3,2,1,0:T(8,128)(2,1)S(1)}, bf16[1,64,4,8,128]{4,3,2,1,0:T(8,128)(2,1)}, u32[]{:S(2)}) copy-start(bf16[1,64,4,8,128]{4,3,2,1,0:T(8,128)(2,1)} %param.7) | copy-start | bytes 1572868
  1.6 5.0 %collective-permute-start = (bf16[4,8,4,128]{3,2,1,0:T(4,128)(2,1)S(1)}, bf16[4,8,4,128]{3,2,1,0:T(4,128)(2,1)S(1)}, u32[]{:S(2)}, u32[]{:S(2)}) collective-permute-start(bf16[4,8,4,128]{3,2,1,0:T(4,128)(2,1)S(1)} %get-tuple-element.24), channel_id=1, source_target_pairs={{0,1},{1,0},{2,3},{3,2},{4,5},{5,4},{6,7},{7,6},{8,9},{9,8},{10,11... | collective-permute-start | bytes 98312 | tf_op jit(solution)/shard_map/ppermute | solution.py:287
  4.6 17.1 %collective-permute-start.1 = (bf16[3,8,72,128]{3,2,1,0:T(8,128)(2,1)S(1)}, bf16[3,8,72,128]{3,2,1,0:T(8,128)(2,1)S(1)}, u32[]{:S(2)}, u32[]{:S(2)}) collective-permute-start(bf16[3,8,72,128]{3,2,1,0:T(8,128)(2,1)S(1)} %get-tuple-element.26), channel_id=1, source_target_pairs={{0,8},{8,16},{16,24},{24,0},{1,9},{9,17},{17,25},{25,1},{2,10},{10... | collective-permute-start | bytes 1327112 | tf_op jit(solution)/shard_map/ppermute | solution.py:287
  4.6 17.6 %collective-permute-start.2 = (bf16[3,8,72,128]{3,2,1,0:T(8,128)(2,1)S(1)}, bf16[3,8,72,128]{3,2,1,0:T(8,128)(2,1)S(1)}, u32[]{:S(2)}, u32[]{:S(2)}) collective-permute-start(bf16[3,8,72,128]{3,2,1,0:T(8,128)(2,1)S(1)} %get-tuple-element.27), channel_id=1, source_target_pairs={{8,0},{16,8},{24,16},{0,24},{9,1},{17,9},{25,17},{1,25},{10,2},{18... | collective-permute-start | bytes 1327112 | tf_op jit(solution)/shard_map/ppermute | solution.py:287
  6.5 4.4 %copy-start.1 = (bf16[3,3,3,64,64]{4,3,2,1,0:T(8,128)(2,1)S(1)}, bf16[3,3,3,64,64]{4,3,2,1,0:T(8,128)(2,1)}, u32[]{:S(2)}) copy-start(bf16[3,3,3,64,64]{4,3,2,1,0:T(8,128)(2,1)} %k1.1) | copy-start | bytes 663556
  6.5 4.4 %copy-start.2 = (bf16[3,3,3,64,64]{4,3,2,1,0:T(8,128)(2,1)S(1)}, bf16[3,3,3,64,64]{4,3,2,1,0:T(8,128)(2,1)}, u32[]{:S(2)}) copy-start(bf16[3,3,3,64,64]{4,3,2,1,0:T(8,128)(2,1)} %k2.1) | copy-start | bytes 663556
  6.5 4.4 %copy-start.3 = (bf16[3,3,3,64,64]{4,3,2,1,0:T(8,128)(2,1)S(1)}, bf16[3,3,3,64,64]{4,3,2,1,0:T(8,128)(2,1)}, u32[]{:S(2)}) copy-start(bf16[3,3,3,64,64]{4,3,2,1,0:T(8,128)(2,1)} %k3.1) | copy-start | bytes 663556
  6.7 5.6 %copy-start.4 = (bf16[4,576,128]{2,1,0:T(8,128)(2,1)}, bf16[4,576,128]{2,1,0:T(8,128)(2,1)S(1)}, u32[]{:S(2)}) copy-start(bf16[4,576,128]{2,1,0:T(8,128)(2,1)S(1)} %get-tuple-element.25.o.own) | copy-start | bytes 1769476
  6.7 10.5 %collective-permute-start.8 = (bf16[4,3,72,128]{3,2,1,0:T(8,128)(2,1)S(1)}, bf16[4,3,72,128]{3,2,1,0:T(8,128)(2,1)S(1)}, u32[]{:S(2)}, u32[]{:S(2)}) collective-permute-start(bf16[4,3,72,128]{3,2,1,0:T(8,128)(2,1)S(1)} %get-tuple-element.38), channel_id=1, source_target_pairs={{0,2},{2,4},{4,6},{6,0},{1,3},{3,5},{5,7},{7,1},{8,10},{10,12},{12... | collective-permute-start | bytes 663560 | tf_op jit(solution)/shard_map/ppermute | solution.py:287
  8.8 11.0 %collective-permute-start.5 = (bf16[4,3,72,128]{3,2,1,0:T(8,128)(2,1)S(1)}, bf16[4,3,72,128]{3,2,1,0:T(8,128)(2,1)S(1)}, u32[]{:S(2)}, u32[]{:S(2)}) collective-permute-start(bf16[4,3,72,128]{3,2,1,0:T(8,128)(2,1)S(1)} %get-tuple-element.33), channel_id=1, source_target_pairs={{2,0},{4,2},{6,4},{0,6},{3,1},{5,3},{7,5},{1,7},{10,8},{12,10},{14... | collective-permute-start | bytes 663560 | tf_op jit(solution)/shard_map/ppermute | solution.py:287
  12.3 0.8 %copy-start.6 = (bf16[1152,256]{1,0:T(8,128)(2,1)}, bf16[1152,256]{1,0:T(8,128)(2,1)S(1)}, u32[]{:S(2)}) copy-start(bf16[1152,256]{1,0:T(8,128)(2,1)S(1)} %get-tuple-element.35.v.w2) | copy-start | bytes 1769476
  13.2 0.8 %copy-start.8 = (bf16[1152,256]{1,0:T(8,128)(2,1)}, bf16[1152,256]{1,0:T(8,128)(2,1)S(1)}, u32[]{:S(2)}) copy-start(bf16[1152,256]{1,0:T(8,128)(2,1)S(1)} %get-tuple-element.36.w.w3) | copy-start | bytes 1769476
  14.0 0.8 %copy-start.10 = (bf16[512,512]{1,0:T(8,128)(2,1)}, bf16[512,512]{1,0:T(8,128)(2,1)S(1)}, u32[]{:S(2)}) copy-start(bf16[512,512]{1,0:T(8,128)(2,1)S(1)} %get-tuple-element.40.pattern) | copy-start | bytes 1572868
  14.8 5.2 %collective-permute-start.3 = (bf16[3,8,4,128]{3,2,1,0:T(4,128)(2,1)S(1)}, bf16[3,8,4,128]{3,2,1,0:T(4,128)(2,1)S(1)}, u32[]{:S(2)}, u32[]{:S(2)}) collective-permute-start(bf16[3,8,4,128]{3,2,1,0:T(4,128)(2,1)S(1)} %get-tuple-element.28), channel_id=1, source_target_pairs={{0,8},{8,16},{16,24},{24,0},{1,9},{9,17},{17,25},{25,1},{2,10},{10... | collective-permute-start | bytes 73736 | tf_op jit(solution)/shard_map/ppermute | solution.py:287
  14.8 1.1 %copy-start.5 = (bf16[4,576,128]{2,1,0:T(8,128)(2,1)S(1)}, bf16[4,576,128]{2,1,0:T(8,128)(2,1)}, u32[]{:S(2)}) copy-start(bf16[4,576,128]{2,1,0:T(8,128)(2,1)} %copy-done.4) | copy-start | bytes 1769476
  17.2 3.8 %collective-permute-start.4 = (bf16[3,8,4,128]{3,2,1,0:T(4,128)(2,1)S(1)}, bf16[3,8,4,128]{3,2,1,0:T(4,128)(2,1)S(1)}, u32[]{:S(2)}, u32[]{:S(2)}) collective-permute-start(bf16[3,8,4,128]{3,2,1,0:T(4,128)(2,1)S(1)} %get-tuple-element.29), channel_id=1, source_target_pairs={{8,0},{16,8},{24,16},{0,24},{9,1},{17,9},{25,17},{1,25},{10,2},{18... | collective-permute-start | bytes 73736 | tf_op jit(solution)/shard_map/ppermute | solution.py:287
  19.9 6.5 %collective-permute-start.10 = (bf16[3,3,72,128]{3,2,1,0:T(8,128)(2,1)S(1)}, bf16[3,3,72,128]{3,2,1,0:T(8,128)(2,1)S(1)}, u32[]{:S(2)}, u32[]{:S(2)}) collective-permute-start(bf16[3,3,72,128]{3,2,1,0:T(8,128)(2,1)S(1)} %get-tuple-element.41), channel_id=1, source_target_pairs={{0,24},{8,16},{16,8},{24,0},{1,25},{9,17},{17,9},{25,1},{2,26},{10... | collective-permute-start | bytes 497672 | tf_op jit(solution)/shard_map/ppermute | solution.py:295
  20.0 6.5 %collective-permute-start.9 = (bf16[3,3,72,128]{3,2,1,0:T(8,128)(2,1)S(1)}, bf16[3,3,72,128]{3,2,1,0:T(8,128)(2,1)S(1)}, u32[]{:S(2)}, u32[]{:S(2)}) collective-permute-start(bf16[3,3,72,128]{3,2,1,0:T(8,128)(2,1)S(1)} %get-tuple-element.42), channel_id=1, source_target_pairs={{0,8},{8,0},{16,24},{24,16},{1,9},{9,1},{17,25},{25,17},{2,10},{10... | collective-permute-start | bytes 497672 | tf_op jit(solution)/shard_map/ppermute | solution.py:295
  21.0 8.4 %collective-permute-start.6 = (bf16[3,3,72,128]{3,2,1,0:T(8,128)(2,1)S(1)}, bf16[3,3,72,128]{3,2,1,0:T(8,128)(2,1)S(1)}, u32[]{:S(2)}, u32[]{:S(2)}) collective-permute-start(bf16[3,3,72,128]{3,2,1,0:T(8,128)(2,1)S(1)} %get-tuple-element.44), channel_id=1, source_target_pairs={{0,8},{8,0},{16,24},{24,16},{1,9},{9,1},{17,25},{25,17},{2,10},{10... | collective-permute-start | bytes 497672 | tf_op jit(solution)/shard_map/ppermute | solution.py:295
  21.7 2.7 %copy-start.7 = (bf16[1152,256]{1,0:T(8,128)(2,1)S(1)}, bf16[1152,256]{1,0:T(8,128)(2,1)}, u32[]{:S(2)}) copy-start(bf16[1152,256]{1,0:T(8,128)(2,1)} %copy-done.6) | copy-start | bytes 1769476
  21.7 2.8 %copy-start.9 = (bf16[1152,256]{1,0:T(8,128)(2,1)S(1)}, bf16[1152,256]{1,0:T(8,128)(2,1)}, u32[]{:S(2)}) copy-start(bf16[1152,256]{1,0:T(8,128)(2,1)} %copy-done.8) | copy-start | bytes 1769476
  21.7 7.9 %collective-permute-start.7 = (bf16[3,3,72,128]{3,2,1,0:T(8,128)(2,1)S(1)}, bf16[3,3,72,128]{3,2,1,0:T(8,128)(2,1)S(1)}, u32[]{:S(2)}, u32[]{:S(2)}) collective-permute-start(bf16[3,3,72,128]{3,2,1,0:T(8,128)(2,1)S(1)} %get-tuple-element.43), channel_id=1, source_target_pairs={{0,24},{8,16},{16,8},{24,0},{1,25},{9,17},{17,9},{25,1},{2,26},{10... | collective-permute-start | bytes 497672 | tf_op jit(solution)/shard_map/ppermute | solution.py:295
  26.4 3.2 %copy-start.11 = (bf16[512,512]{1,0:T(8,128)(2,1)S(1)}, bf16[512,512]{1,0:T(8,128)(2,1)}, u32[]{:S(2)}) copy-start(bf16[512,512]{1,0:T(8,128)(2,1)} %copy-done.10) | copy-start | bytes 1572868
